TPU v7x, 32 devices: a whole 2x2x4 slice. The times are simulated.
32 devices in a mesh: grp: 2 (over y), mem: 16 (over z, x, core).
Axes of the slice: x: 2, y: 2, z: 4, core: 2. Of those that a mesh axis runs over, the one named last changes fastest.
Arguments:
- pooled: bfloat16 [4096, 2560], P(('grp', 'mem')), may hold values from -6 to 6
- grad_hidden: bfloat16 [4096, 512], P(('grp', 'mem')), may hold values from -0.059814453 to 0.059814453
- w_first: bfloat16 [2560, 512], replicated, may hold values from -0.125 to 0.125
- bias_first: float32 [512], replicated, may hold values from -4 to 4
- table_owner: int32 [2, 16], P('grp'), may hold values from 0 to 15, each once within a row
- shard_owner: int32 [2, 16], P('grp'), may hold values from 0 to 15, each once within a row
- lookups_whole: int32 [2, 16, 2048, 8], P('grp', 'mem'), may hold values from 0 to 1023
- lookups_split: int32 [2, 4, 2048, 8], P('grp'), may hold values from 0 to 1023
- table_whole: float32 [2, 16, 128, 1024], P('grp', 'mem'), may hold values from -3 to 3
- accum_whole: float32 [2, 16, 1024], P('grp', 'mem'), may hold values from 2e-05 to 0.0002
- table_split: float32 [2, 16, 32, 1024], P('grp', 'mem'), may hold values from -3 to 3
- accum_split: float32 [2, 4, 1024], P('grp'), may hold values from 2e-05 to 0.0002
Outputs:
- grad_first: float32 [2560, 512], P('mem')
- grad_bias: float32 [512], replicated
- new_whole: float32 [2, 16, 128, 1024], P('grp', 'mem')
- new_split: float32 [2, 16, 32, 1024], P('grp', 'mem')
Inputs may be any that keep to these rules, and one draw needn't show every extreme that they name: `table_owner`: each row is a permutation of the owner slots. `shard_owner`: each row is a permutation of the owner slots.
All inputs are finite; a program needn't handle non-finite values.
Results may differ from a plain program's by a relative error of at most 0.0055.
Values may be sent and summed in bfloat16 or wider, within the bound.
No kernel may reach another device: no remote copies, remote signals or barrier semaphores. Data moves between devices by JAX's collectives and lax.ppermute only.
A program may use at most 128 MiB of HBM per device.

v0:
```python
import jax
import jax.numpy as jnp
from jax import lax
from jax.sharding import PartitionSpec as P

E = 128
CS = 4
COLS = 32


LEARN_RATE = 0.5
EPSILON = 1e-08


def tower_block(inputs, upstream, weights, bias_row):
    pre_act = jnp.dot(inputs, weights, preferred_element_type=jnp.float32) + bias_row
    sigmoid_pre = jax.nn.sigmoid(pre_act)
    gradient_slope = sigmoid_pre * (1.0 + pre_act * (1.0 - sigmoid_pre))
    delta_rows = (upstream.astype(jnp.float32) * gradient_slope).astype(jnp.bfloat16)
    back_rows = lax.dot_general(
        delta_rows, weights, (((1,), (1,)), ((), ())), preferred_element_type=jnp.float32
    ).astype(jnp.bfloat16)
    return (delta_rows, back_rows)


def arrange(back_rows, whole_order, split_order, owners):
    sample_rows = back_rows.shape[0]
    whole_part = back_rows[:, : owners * E].reshape(sample_rows, owners, E)
    split_part = back_rows[:, owners * E :].reshape(sample_rows, owners, COLS)
    return (jnp.take(whole_part, whole_order, axis=1), jnp.take(split_part, split_order, axis=1))


def row_gradient(values, key_rows, row_count):
    total_rows = values.shape[0]
    block_rows = min(512, total_rows)
    column_count = values.shape[1]
    value_blocks = values.reshape(total_rows // block_rows, block_rows, column_count)
    key_blocks = key_rows.reshape(total_rows // block_rows, block_rows, key_rows.shape[1])
    positions = lax.broadcasted_iota(jnp.int32, (1, 1, row_count), 2)

    def accumulate(running, inputs_pair):
        piece_rows, pick_keys = inputs_pair
        hit_counts = jnp.sum((pick_keys[:, :, None] == positions).astype(jnp.bfloat16), axis=1)
        added = lax.dot_general(
            piece_rows, hit_counts, (((0,), (0,)), ((), ())), preferred_element_type=jnp.float32
        )
        return (running + added, None)

    initial = jnp.zeros((column_count, row_count), jnp.float32)
    result, _ = lax.scan(accumulate, initial, (value_blocks, key_blocks))
    return result


def adagrad(weights_in, accum_rows, row_grad, squares):
    state_rows = accum_rows + squares / E
    return weights_in - LEARN_RATE * row_grad / (jnp.sqrt(state_rows) + EPSILON)


def per_device(
    pooled,
    grad_hidden,
    w_first,
    bias_first,
    table_owner,
    shard_owner,
    lookups_whole,
    lookups_split,
    table_whole,
    accum_whole,
    table_split,
    accum_split,
):
    owners = lax.axis_size("mem")
    groups = lax.axis_size("grp")
    position = lax.axis_index("mem")
    whole_order = jnp.argsort(table_owner[0])
    split_order = jnp.argsort(shard_owner[0])
    split_table = split_order[position] // CS
    keys_whole = lookups_whole[0, 0]
    keys_split = lax.dynamic_index_in_dim(lookups_split[0], split_table, 0, keepdims=False)
    rows_whole = table_whole.shape[-1]
    rows_split = table_split.shape[-1]
    samples = pooled.shape[0]
    feature_count = pooled.shape[1]
    delta_rows, back_rows = tower_block(pooled, grad_hidden, w_first, bias_first)
    send_whole, send_split = arrange(back_rows, whole_order, split_order, owners)
    got_whole, got_split = (
        lax.all_to_all(send_whole, "mem", split_axis=1, concat_axis=0, tiled=True),
        lax.all_to_all(send_split, "mem", split_axis=1, concat_axis=0, tiled=True),
    )
    grad_whole = row_gradient(got_whole.reshape(owners * samples, E), keys_whole, rows_whole)
    grad_split = row_gradient(got_split.reshape(owners * samples, COLS), keys_split, rows_split)
    share_rows = feature_count // (owners * groups)
    reordered = (
        pooled.reshape(samples, owners, groups, share_rows)
        .transpose(0, 2, 1, 3)
        .reshape(samples, feature_count)
    )
    own_rows = lax.psum_scatter(
        lax.dot_general(
            reordered, delta_rows, (((0,), (0,)), ((), ())), preferred_element_type=jnp.float32
        ),
        ("grp", "mem"),
        scatter_dimension=0,
        tiled=True,
    )
    grad_first = lax.all_gather(own_rows, "grp", axis=0, tiled=True)
    grad_bias = lax.psum(jnp.sum(delta_rows.astype(jnp.float32), axis=0), ("grp", "mem"))
    new_whole = adagrad(
        table_whole[0, 0], accum_whole[0, 0], grad_whole, jnp.sum(grad_whole * grad_whole, axis=0)
    )
    shard_squares = jnp.sum(grad_split * grad_split, axis=0)
    table_count = accum_split.shape[1]
    table_pick = (lax.iota(jnp.int32, table_count) == split_table).astype(jnp.float32)
    spread = table_pick[:, None] * shard_squares[None, :]
    totals = lax.psum(spread.astype(jnp.bfloat16), "mem").astype(jnp.float32)
    total_squares = lax.dynamic_index_in_dim(totals, split_table, 0, keepdims=False)
    accum_here = lax.dynamic_index_in_dim(accum_split[0], split_table, 0, keepdims=False)
    new_split = adagrad(table_split[0, 0], accum_here, grad_split, total_squares)
    return (grad_first, grad_bias, new_whole[None, None], new_split[None, None])


def solution(mesh):
    return jax.shard_map(
        per_device,
        mesh=mesh,
        in_specs=(
            P(("grp", "mem"), None),
            P(("grp", "mem"), None),
            P(),
            P(),
            P("grp", None),
            P("grp", None),
            P("grp", "mem", None, None),
            P("grp", None, None, None),
            P("grp", "mem", None, None),
            P("grp", "mem", None),
            P("grp", "mem", None, None),
            P("grp", None, None),
        ),
        out_specs=(P("mem", None), P(), P("grp", "mem", None, None), P("grp", "mem", None, None)),
        check_vma=False,
    )
```

profile of v0, /device:TPU:0, one launch (start us, length us, event | category | flops | bytes accessed | tf_op | source)
XLA Modules:
  0.0 218.9 jit_solution(365951078167600067)
XLA Ops:
  7.2 2.3 %copy.46 = bf16[128,2560]{0,1:T(8,128)(2,1)} copy(bf16[128,2560]{1,0:T(8,128)(2,1)} %param.16) | data formatting | bytes 1310720 | tf_op args[0]
  9.5 1.1 copy.47
  10.7 1.7 convert_reduce_fusion
  12.4 3.2 %convolution_bitcast_fusion = f32[2560,512]{0,1:T(8,128)} fusion(bf16[128,512]{1,0:T(8,128)(2,1)S(1)} %get-tuple-element.215, bf16[128,2560]{0,1:T(8,128)(2,1)S(1)} %bitcast.81), kind=kOutput, calls=%fused_computation.20 | convolution fusion | flops 335544320 | bytes 6029312 | tf_op jit(solution)/shard_map/dot_general | solution.py:100
  15.6 5.9 %copy.54 = f32[2560,512]{1,0:T(8,128)} copy(f32[2560,512]{0,1:T(8,128)} %convolution_bitcast_fusion) | data formatting | bytes 10485760
  21.6 1.0 convolution_convert_fusion
  22.6 0.8 copy-done.1
  23.4 0.1 copy.50
  23.6 1.2 sort.32
  24.8 1.2 sort.31
  26.1 0.6 gather_fusion.1
  26.7 0.7 select_bitcast_fusion.1
  27.4 7.4 %all-to-all-start.1 = ((bf16[128,16,32]{0,2,1:T(8,128)(2,1)}), bf16[128,16,32]{0,2,1:T(8,128)(2,1)S(1)}, u32[]{:S(2)}, u32[]{:S(2)}) async-start(bf16[128,16,32]{0,2,1:T(8,128)(2,1)} %select_bitcast_fusion.1), calls=%async_computation.1 | async-start | bytes 262144 | tf_op jit(solution)/shard_map/all_to_all | solution.py:89
  34.9 0.6 dynamic_slice.41
  38.1 2.0 copy_bitcast_fusion
  40.0 2.5 %gather_fusion = bf16[16,128,128]{2,1,0:T(8,128)(2,1)} fusion(bf16[128,16,128]{2,0,1:T(8,128)(2,1)} %copy_bitcast_fusion, s32[1024]{0:T(1024)S(1)} %pad_clamp_fusion.1), kind=kCustom, calls=%fused_computation | custom fusion | bytes 1048640 | tf_op jit(solution)/shard_map/jit(_take)/gather | solution.py:30
  42.5 41.9 %psum.14 = f32[512]{0:T(512)} all-reduce(f32[512]{0:T(512)S(1)} %get-tuple-element.214), channel_id=1, replica_groups=mesh['grp'=2,'mem'=16] {'grp','mem'}, use_global_device_ids=true, to_apply=%region_2.3 | all-reduce | flops 512 | bytes 4096 | tf_op jit(solution)/shard_map/psum | solution.py:108
  84.4 0.5 compare_convert_fusion
  85.0 1.5 constant_dynamic-slice_fusion
  86.4 1.9 select_bitcast_fusion
  88.4 4.6 %all-to-all-start = ((bf16[128,16,128]{2,0,1:T(8,128)(2,1)}), bf16[128,16,128]{2,0,1:T(8,128)(2,1)}, u32[]{:S(2)}, u32[]{:S(2)}) async-start(bf16[128,16,128]{2,0,1:T(8,128)(2,1)} %select_bitcast_fusion), calls=%async_computation | async-start | bytes 1048576 | tf_op jit(solution)/shard_map/all_to_all | solution.py:88
  93.0 1.0 copy.53
  94.1 35.7 %while.27 = (s32[]{:T(128)}, f32[32,1024]{1,0:T(8,128)S(1)}, bf16[4,512,32]{2,1,0:T(8,128)(2,1)}, s32[4,512,8]{1,2,0:T(8,128)}, s32[]{:T(128)}, /*index=5*/s32[]{:T(128)}) while((s32[]{:T(128)}, f32[32,1024]{1,0:T(8,128)S(1)}, bf16[4,512,32]{2,1,0:T(8,128)(2,1)}, s32[4,512,8]{1,2,0:T(8,128)}, s32[]{:T(128)}, ...), condition=%wide.region_11.12_spmd.clone, body=%wide.region_9.11_spmd.clone.sunk | while | flops 45678592 | bytes 2572383 | solution.py:50
  94.1 0.7 dynamic-slice_bitcast_fusion.5
  94.8 0.1 copy.62
  94.9 6.4 %fusion.37 = bf16[512,1024]{1,0:T(8,128)(2,1)} fusion(s32[512,8]{1,0:T(8,128)S(1)} %copy.62), kind=kLoop, calls=%fused_computation.14.clone.1 | loop fusion | flops 12058624 | bytes 1064960 | tf_op jit(solution)/shard_map/while/body/eval_jaxpr/reduce_sum | solution.py:43
  101.3 1.6 convolution_add_fusion.6
  103.0 0.7 dynamic-slice_bitcast_fusion.5
  103.7 0.1 copy.62
  103.8 6.4 %fusion.37 = bf16[512,1024]{1,0:T(8,128)(2,1)} fusion(s32[512,8]{1,0:T(8,128)S(1)} %copy.62), kind=kLoop, calls=%fused_computation.14.clone.1 | loop fusion | flops 12058624 | bytes 1064960 | tf_op jit(solution)/shard_map/while/body/eval_jaxpr/reduce_sum | solution.py:43
  110.2 1.6 convolution_add_fusion.6
  111.9 0.7 dynamic-slice_bitcast_fusion.5
  112.6 0.1 copy.62
  112.8 6.4 %fusion.37 = bf16[512,1024]{1,0:T(8,128)(2,1)} fusion(s32[512,8]{1,0:T(8,128)S(1)} %copy.62), kind=kLoop, calls=%fused_computation.14.clone.1 | loop fusion | flops 12058624 | bytes 1064960 | tf_op jit(solution)/shard_map/while/body/eval_jaxpr/reduce_sum | solution.py:43
  119.2 1.6 convolution_add_fusion.6
  120.8 0.7 dynamic-slice_bitcast_fusion.5
  121.6 0.1 copy.62
  121.7 6.4 %fusion.37 = bf16[512,1024]{1,0:T(8,128)(2,1)} fusion(s32[512,8]{1,0:T(8,128)S(1)} %copy.62), kind=kLoop, calls=%fused_computation.14.clone.1 | loop fusion | flops 12058624 | bytes 1064960 | tf_op jit(solution)/shard_map/while/body/eval_jaxpr/reduce_sum | solution.py:43
  128.1 1.6 convolution_add_fusion.6
  129.8 0.7 multiply_convert_fusion.1
  130.5 34.5 %psum.15 = bf16[4,1024]{1,0:T(4,128)(2,1)S(1)} all-reduce(bf16[4,1024]{1,0:T(4,128)(2,1)S(1)} %multiply_convert_fusion.1), channel_id=1, replica_groups=mesh['grp'=2,'mem'=16] {'mem'}, use_global_device_ids=true, to_apply=%region_13.14 | all-reduce | flops 4096 | bytes 16384 | tf_op jit(solution)/shard_map/psum | solution.py:116
  165.0 0.7 sqrt_add_fusion
  165.7 1.6 fusion.15
  167.3 35.8 %while.26 = (s32[]{:T(128)}, f32[128,1024]{1,0:T(8,128)S(1)}, bf16[4,512,128]{2,1,0:T(8,128)(2,1)}, s32[4,512,8]{1,2,0:T(8,128)}, s32[]{:T(128)}, /*index=5*/s32[]{:T(128)}) while((s32[]{:T(128)}, f32[128,1024]{1,0:T(8,128)S(1)}, bf16[4,512,128]{2,1,0:T(8,128)(2,1)}, s32[4,512,8]{1,2,0:T(8,128)}, s32[]{:T(128)}, ...), condition=%wide.region_6.7_spmd.clone, body=%wide.region_4.6_spmd.clone.sunk | while | flops 146538496 | bytes 3358815 | solution.py:50
  167.3 0.7 dynamic-slice_bitcast_fusion.4
  168.0 0.1 copy.61
  168.2 6.4 %fusion.34 = bf16[512,1024]{1,0:T(8,128)(2,1)} fusion(s32[512,8]{1,0:T(8,128)S(1)} %copy.61), kind=kLoop, calls=%fused_computation.6.clone.1 | loop fusion | flops 12058624 | bytes 1064960 | tf_op jit(solution)/shard_map/while/body/eval_jaxpr/reduce_sum | solution.py:43
  174.6 1.7 convolution_add_fusion.5
  176.3 0.7 dynamic-slice_bitcast_fusion.4
  177.0 0.1 copy.61
  177.1 6.4 %fusion.34 = bf16[512,1024]{1,0:T(8,128)(2,1)} fusion(s32[512,8]{1,0:T(8,128)S(1)} %copy.61), kind=kLoop, calls=%fused_computation.6.clone.1 | loop fusion | flops 12058624 | bytes 1064960 | tf_op jit(solution)/shard_map/while/body/eval_jaxpr/reduce_sum | solution.py:43
  183.5 1.7 convolution_add_fusion.5
  185.2 0.7 dynamic-slice_bitcast_fusion.4
  185.9 0.1 copy.61
  186.1 6.4 %fusion.34 = bf16[512,1024]{1,0:T(8,128)(2,1)} fusion(s32[512,8]{1,0:T(8,128)S(1)} %copy.61), kind=kLoop, calls=%fused_computation.6.clone.1 | loop fusion | flops 12058624 | bytes 1064960 | tf_op jit(solution)/shard_map/while/body/eval_jaxpr/reduce_sum | solution.py:43
  192.5 1.7 convolution_add_fusion.5
  194.2 0.7 dynamic-slice_bitcast_fusion.4
  194.9 0.1 copy.61
  195.0 6.4 %fusion.34 = bf16[512,1024]{1,0:T(8,128)(2,1)} fusion(s32[512,8]{1,0:T(8,128)S(1)} %copy.61), kind=kLoop, calls=%fused_computation.6.clone.1 | loop fusion | flops 12058624 | bytes 1064960 | tf_op jit(solution)/shard_map/while/body/eval_jaxpr/reduce_sum | solution.py:43
  201.4 1.7 convolution_add_fusion.5
  203.1 0.1 multiply_reduce_fusion
  203.2 1.9 fusion.14
  205.1 6.2 %all_gather.3 = f32[160,512]{1,0:T(8,128)S(1)} all-gather(f32[80,512]{1,0:T(8,128)} %reduce-scatter.4.cloned.1.call-done), channel_id=1, replica_groups=mesh['grp'=2,'mem'=16] {'grp'}, dimensions={0}, use_global_device_ids=true | all-gather | bytes 491520 | tf_op jit(solution)/shard_map/all_gather | solution.py:107
  211.4 0.7 copy.76
  (25 shorter events, 0.2 us)
Async XLA Ops:
  7.2 3.5 %copy-start = (bf16[2560,512]{1,0:T(8,128)(2,1)S(1)}, bf16[2560,512]{1,0:T(8,128)(2,1)}, u32[]{:S(2)}) copy-start(bf16[2560,512]{1,0:T(8,128)(2,1)} %param.18) | copy-start | bytes 7864324
  7.2 198.0 %reduce-scatter.4.cloned.1.call-start = ((), (), s32[]{:S(2)}) async-start(), calls=%async_computation.3 | async-start | bytes 5406720 | tf_op jit(solution)/shard_map/reduce_scatter | solution.py:99
  21.6 2.0 copy-start.3
  21.6 3.3 %copy-start.4 = (s32[1,16]{1,0:T(1,128)S(1)}, s32[1,16]{1,0:T(1,128)}, u32[]{:S(2)}) copy-start(s32[1,16]{1,0:T(1,128)} %param.20) | copy-start | bytes 196
  22.6 0.9 copy-start.1
  27.4 60.9 %all-to-all-start.1 = ((bf16[128,16,32]{0,2,1:T(8,128)(2,1)}), bf16[128,16,32]{0,2,1:T(8,128)(2,1)S(1)}, u32[]{:S(2)}, u32[]{:S(2)}) async-start(bf16[128,16,32]{0,2,1:T(8,128)(2,1)} %select_bitcast_fusion.1), calls=%async_computation.1 | async-start | bytes 262144 | tf_op jit(solution)/shard_map/all_to_all | solution.py:89
  88.4 78.9 %all-to-all-start = ((bf16[128,16,128]{2,0,1:T(8,128)(2,1)}), bf16[128,16,128]{2,0,1:T(8,128)(2,1)}, u32[]{:S(2)}, u32[]{:S(2)}) async-start(bf16[128,16,128]{2,0,1:T(8,128)(2,1)} %select_bitcast_fusion), calls=%async_computation | async-start | bytes 1048576 | tf_op jit(solution)/shard_map/all_to_all | solution.py:88
  167.3 35.9 %copy-start.2 = (f32[1,1,1024]{2,1,0:T(1,128)S(1)}, f32[1,1,1024]{2,1,0:T(1,128)}, u32[]{:S(2)}) copy-start(f32[1,1,1024]{2,1,0:T(1,128)} %param.25) | copy-start | bytes 12292
Sparse Core Ops, SparseCore 0:
  21.7 149.0 reduce-scatter.3
where the time goes:
time: 220 us; the launch traced here: 219 us
  blocking collectives  82.6 us (38%)
  other arithmetic  62.1 us (28%)
  local copies, waits for them, and re-layouts  26 us (12%)
  matrix products  19.2 us (9%)
  between operations  16.8 us (8%)
  starting transfers between devices  12.1 us (6%)
    reduce_sum x8, other arithmetic, accumulate(): jnp.sum((pick_keys[:, :, None] == positions).astype(jnp.bfloat16), axis=1)  51.3 us
    psum x1, blocking collectives, per_device(): lax.psum(jnp.sum(delta_rows.astype(jnp.float32), axis=0), ('grp', 'mem'))  41.9 us
    psum x1, blocking collectives, per_device(): totals = lax.psum(spread.astype(jnp.bfloat16), 'mem').astype(jnp.float32)  34.5 us
    dot_general x8, matrix products, accumulate(): lax.dot_general(piece_rows, hit_counts, (((0,), (0,)), ((), ())), preferr...  13.2 us
    unnamed x14, local copies, waits for them, and re-layouts  10.9 us
    all_to_all x1, starting transfers between devices, per_device(): lax.all_to_all(send_split, 'mem', split_axis=1, concat_axis=0, tiled=True)  7.39 us
    eq x16, local copies, waits for them, and re-layouts, accumulate(): pick_keys[:, :, None] == positions  6.77 us
    all_gather x1, blocking collectives, per_device(): grad_first = lax.all_gather(own_rows, 'grp', axis=0, tiled=True)  6.23 us
  transfers between devices with their start and end apart: 3, of which 0 were waited for; matrix products, arithmetic and copies ran while one was open for 42% of the time, Pallas kernels for 0%

commit v1 on v0

v1 whole, which is shorter than its diff:
```python
import functools

import jax
import jax.numpy as jnp
from jax import lax
from jax.experimental import pallas as pl
from jax.experimental.pallas import tpu as pltpu
from jax.sharding import PartitionSpec as P

E = 128
CS = 4
LEARN_RATE = 0.5
EPSILON = 1e-08
BF16 = jnp.bfloat16
F32 = jnp.float32

NT_DIMS = (((1,), (1,)), ((), ()))
NN_DIMS = (((1,), (0,)), ((), ()))


def dot_nt(lhs, rhs):
    return lax.dot_general(lhs, rhs, NT_DIMS, preferred_element_type=F32)


def dot_nn(lhs, rhs):
    return lax.dot_general(lhs, rhs, NN_DIMS, preferred_element_type=F32)


def pack_kernel(spans, half_rows, idx_ref, pooled_ref, *rest):
    outs, turned = rest[:-1], rest[-1]
    features = pooled_ref.shape[1]
    for start in range(0, features, E):
        turned[start : start + E, :] = pooled_ref[:, start : start + E].T
    low = idx_ref[0] % 4
    side = idx_ref[1] % 2
    for chip, out in enumerate(outs):
        turn_side, turn_low = chip // 2, (chip % 2) * 2
        for core in range(2):
            there = jnp.bitwise_xor(low, turn_low + core)
            there_side = jnp.bitwise_xor(side, turn_side)
            for span in range(spans):
                row = pl.multiple_of(((span * 4 + there) * 2 + there_side) * half_rows, 16)
                out[core, span * half_rows : (span + 1) * half_rows, :] = turned[
                    pl.ds(row, half_rows), :
                ]


def pack(idx, pooled, spans, half_rows):
    samples, features = pooled.shape
    piece = jax.ShapeDtypeStruct((2, spans * half_rows, samples), BF16)
    return pl.pallas_call(
        functools.partial(pack_kernel, spans, half_rows),
        out_shape=[piece] * 4,
        in_specs=[
            pl.BlockSpec(memory_space=pltpu.SMEM),
            pl.BlockSpec(memory_space=pltpu.VMEM),
        ],
        out_specs=[pl.BlockSpec(memory_space=pltpu.VMEM)] * 4,
        scratch_shapes=[pltpu.VMEM((features, samples), BF16)],
        name="pack",
    )(idx, pooled)


def count_kernel(bits, idx_ref, whole_ref, split_ref, whole_out, split_out):
    for keys_ref, out in ((whole_ref, whole_out), (split_ref, split_out)):
        rows, lanes = out.shape
        pool = keys_ref.shape[0]
        fields = 32 // bits
        low_rows = rows // fields
        spots = lax.broadcasted_iota(jnp.int32, (low_rows, lanes), 0)
        words = jnp.zeros((low_rows, lanes), jnp.int32)
        for place in range(pool):
            key = keys_ref[place : place + 1, :]
            low = lax.rem(key, low_rows)
            unit = lax.shift_left(jnp.ones_like(key), lax.div(key, low_rows) * bits)
            words = words + jnp.where(spots == low, unit, 0)
        for field in range(fields):
            hits = lax.shift_right_logical(words, jnp.full_like(words, field * bits))
            hits = jnp.bitwise_and(hits, (1 << bits) - 1)
            out[field * low_rows : (field + 1) * low_rows, :] = hits.astype(F32).astype(BF16)


def hit_counts(idx, keys_whole, keys_split, rows_whole, rows_split):
    pool, total = keys_whole.shape
    bits = pool.bit_length()
    block = 128
    return pl.pallas_call(
        functools.partial(count_kernel, bits),
        out_shape=[
            jax.ShapeDtypeStruct((rows_whole, total), BF16),
            jax.ShapeDtypeStruct((rows_split, total), BF16),
        ],
        grid_spec=pltpu.PrefetchScalarGridSpec(
            num_scalar_prefetch=1,
            grid=(total // block,),
            in_specs=[
                pl.BlockSpec((pool, block), lambda i, idx: (0, i)),
                pl.BlockSpec((None, pool, block), lambda i, idx: (idx[3], 0, i)),
            ],
            out_specs=[
                pl.BlockSpec((rows_whole, block), lambda i, idx: (0, i)),
                pl.BlockSpec((rows_split, block), lambda i, idx: (0, i)),
            ],
        ),
        name="hit_counts",
    )(idx, keys_whole, keys_split)


def table_kernel(chunks, idx_ref, *refs):
    deltas = refs[:chunks]
    (w_whole, w_split, hits_whole, hits_split, table_whole, accum_whole, table_split,
     accum_split, new_whole, new_split, back, grads) = refs[chunks:]
    samples = deltas[0].shape[0]

    @pl.when(pl.program_id(0) == 0)
    def _():
        for turn in range(chunks):
            lane = pl.multiple_of(jnp.bitwise_xor(idx_ref[0], turn) * samples, samples)
            rows = deltas[turn][...]
            back[:E, pl.ds(lane, samples)] = dot_nt(w_whole[...], rows).astype(BF16)
            back[E:, pl.ds(lane, samples)] = dot_nt(w_split[...], rows).astype(BF16)

    grad = dot_nt(back[:E, :], hits_whole[...])
    squares = jnp.sum(grad * grad, axis=0, keepdims=True)
    scale = LEARN_RATE / (jnp.sqrt(accum_whole[...] + squares / E) + EPSILON)
    new_whole[...] = table_whole[...] - grad * scale
    grads[...] = dot_nt(back[E:, :], hits_split[...])
    squares = jnp.sum(grads[...] * grads[...], axis=0, keepdims=True)
    scale = LEARN_RATE / (jnp.sqrt(accum_split[...] + squares / E) + EPSILON)
    columns = table_split.shape[0]
    first = pl.multiple_of(idx_ref[4] * columns, columns)
    new_split[...] = table_split[...] - grads[pl.ds(first, columns), :] * scale


def table_update(idx, deltas, w_first, hits_whole, hits_split, table_whole, accum_whole,
                 table_split, accum_split, whole_tables):
    chunks = len(deltas)
    samples, hidden = deltas[0].shape
    rows = table_whole.shape[1]
    total = chunks * samples
    columns = table_split.shape[0]
    block = 256
    return pl.pallas_call(
        functools.partial(table_kernel, chunks),
        out_shape=[
            jax.ShapeDtypeStruct(table_whole.shape, F32),
            jax.ShapeDtypeStruct(table_split.shape, F32),
        ],
        grid_spec=pltpu.PrefetchScalarGridSpec(
            num_scalar_prefetch=1,
            grid=(rows // block,),
            in_specs=[pl.BlockSpec((samples, hidden), lambda i, idx: (0, 0))] * chunks
            + [
                pl.BlockSpec((E, hidden), lambda i, idx: (idx[2], 0)),
                pl.BlockSpec((E, hidden), lambda i, idx: (whole_tables + idx[3], 0)),
                pl.BlockSpec((block, total), lambda i, idx: (i, 0)),
                pl.BlockSpec((block, total), lambda i, idx: (i, 0)),
                pl.BlockSpec((E, block), lambda i, idx: (0, i)),
                pl.BlockSpec((1, block), lambda i, idx: (0, i)),
                pl.BlockSpec((columns, block), lambda i, idx: (0, i)),
                pl.BlockSpec((None, 1, block), lambda i, idx: (idx[3], 0, i)),
            ],
            out_specs=[
                pl.BlockSpec((E, block), lambda i, idx: (0, i)),
                pl.BlockSpec((columns, block), lambda i, idx: (0, i)),
            ],
            scratch_shapes=[
                pltpu.VMEM((2 * E, total), BF16),
                pltpu.VMEM((E, block), F32),
            ],
        ),
        name="table_update",
    )(idx, *deltas, w_first, w_first, hits_whole, hits_split, table_whole, accum_whole,
      table_split, accum_split)


def partial_kernel(spans, half_rows, idx_ref, *refs):
    count = 8
    pooled, deltas = refs[:count], refs[count : 2 * count]
    own, sends, acc = refs[2 * count], refs[2 * count + 1 : -1], refs[-1]
    acc[...] = dot_nn(pooled[0][...], deltas[0][...])
    for piece, rows in zip(pooled[1:], deltas[1:]):
        acc[...] += dot_nn(piece[...], rows[...])
    sums = [jnp.sum(rows[...].astype(F32), axis=0, keepdims=True) for rows in deltas]
    while len(sums) > 1:
        sums = [a + b for a, b in zip(sums[0::2], sums[1::2])]
    high = sums[0].astype(BF16)
    low = (sums[0] - high.astype(F32)).astype(BF16)
    hidden = high.shape[1]
    place = lax.broadcasted_iota(jnp.int32, (16, hidden), 0)
    extra = jnp.where(place == 0, high.astype(F32), jnp.where(place == 1, low.astype(F32), 0.0))
    extra = extra.astype(BF16)
    here = idx_ref[0] // 4
    for turn in range(spans):
        row = pl.multiple_of(jnp.bitwise_xor(here, turn) * half_rows, 16)
        block = acc[pl.ds(row, half_rows), :]
        if turn == 0:
            own[:half_rows, :] = block
            own[half_rows:, :] = extra.astype(F32)
        else:
            sends[turn - 1][:half_rows, :] = block.astype(BF16)
            sends[turn - 1][half_rows:, :] = extra


def partial_gradient(idx, pooled, deltas, spans, half_rows):
    hidden = deltas[0].shape[1]
    shape = (half_rows + 16, hidden)
    vmem = pl.BlockSpec(memory_space=pltpu.VMEM)
    return pl.pallas_call(
        functools.partial(partial_kernel, spans, half_rows),
        out_shape=[jax.ShapeDtypeStruct(shape, F32)]
        + [jax.ShapeDtypeStruct(shape, BF16)] * (spans - 1),
        in_specs=[pl.BlockSpec(memory_space=pltpu.SMEM)] + [vmem] * 16,
        out_specs=[vmem] * spans,
        scratch_shapes=[pltpu.VMEM((spans * half_rows, hidden), F32)],
        name="partial_gradient",
    )(idx, *pooled, *deltas)


def per_device(
    groups,
    owners,
    pooled,
    grad_hidden,
    w_first,
    bias_first,
    table_owner,
    shard_owner,
    lookups_whole,
    lookups_split,
    table_whole,
    accum_whole,
    table_split,
    accum_split,
):
    position = lax.axis_index("mem")
    side = lax.axis_index("grp")
    order = lax.iota(jnp.int32, owners)
    whole_id = jnp.sum(jnp.where(table_owner[0] == position, order, 0))
    shard_id = jnp.sum(jnp.where(shard_owner[0] == position, order, 0))
    idx = jnp.stack([position, side, whole_id, shard_id // CS, shard_id % CS])
    samples, features = pooled.shape
    spans = owners // 4
    half_rows = features // owners // 2

    def send(values, turn, side_turn=0):
        pairs = [
            (g * owners + m, (g ^ side_turn) * owners + (m ^ turn))
            for g in range(groups)
            for m in range(owners)
        ]
        return lax.ppermute(values, ("grp", "mem"), pairs)

    pre_act = jnp.dot(pooled, w_first, preferred_element_type=F32) + bias_first
    sigmoid_pre = jax.nn.sigmoid(pre_act)
    slope = sigmoid_pre * (1.0 + pre_act * (1.0 - sigmoid_pre))
    delta = (grad_hidden.astype(F32) * slope).astype(BF16)

    packed = pack(idx, pooled, spans, half_rows)
    arrived = [packed[0]] + [send(packed[chip], (chip % 2) * 2, chip // 2) for chip in (1, 2, 3)]
    crossed = send(jnp.stack([piece[1] for piece in arrived]), 1)
    pooled_pieces = []
    for chip in range(4):
        pooled_pieces += [arrived[chip][0], crossed[chip]]

    chunk = {0: delta}
    near = {}
    tops = [1 << b for b in range(1, owners.bit_length() - 1)]
    for top in tops:
        chunk[top] = send(delta, top)
    near[0] = send(delta, 0, 1)
    near[2] = send(delta, 2, 1)
    for top in tops:
        for rest in range(2, top, 2):
            chunk[top + rest] = send(chunk[top], rest)
    for turn in range(0, owners, 2):
        chunk[turn + 1] = send(chunk[turn], 1)
    for turn in (0, 2):
        near[turn + 1] = send(near[turn], 1)

    group_deltas = [chunk[turn] for turn in range(4)] + [near[turn] for turn in range(4)]
    own, *leaving = partial_gradient(idx, pooled_pieces, group_deltas, spans, half_rows)
    parts = [own] + [send(leaving[turn - 1], 4 * turn).astype(F32) for turn in range(1, spans)]
    while len(parts) > 1:
        parts = [a + b for a, b in zip(parts[0::2], parts[1::2])]
    total = parts[0]
    turn = 2
    while turn < groups:
        total = total + send(total, 0, turn)
        turn *= 2
    grad_bias = total[half_rows] + total[half_rows + 1]
    mine = lax.reduce_precision(total[:half_rows], 8, 7)
    other = send(mine.astype(BF16), 0, 1).astype(F32)
    first = side % 2 == 0
    grad_first = jnp.concatenate([jnp.where(first, mine, other), jnp.where(first, other, mine)])

    rows_whole = table_whole.shape[-1]
    rows_split = table_split.shape[-1]
    hits_whole, hits_split = hit_counts(
        idx,
        lookups_whole[0, 0].T,
        jnp.transpose(lookups_split[0], (0, 2, 1)),
        rows_whole,
        rows_split,
    )
    new_whole, new_split = table_update(
        idx,
        [chunk[turn] for turn in range(owners)],
        w_first,
        hits_whole,
        hits_split,
        table_whole[0, 0],
        accum_whole[0],
        table_split[0, 0],
        accum_split[0][:, None, :],
        owners,
    )
    return (grad_first, grad_bias, new_whole[None, None], new_split[None, None])


def solution(mesh):
    return jax.shard_map(
        functools.partial(per_device, mesh.shape["grp"], mesh.shape["mem"]),
        mesh=mesh,
        in_specs=(
            P(("grp", "mem"), None),
            P(("grp", "mem"), None),
            P(),
            P(),
            P("grp", None),
            P("grp", None),
            P("grp", "mem", None, None),
            P("grp", None, None, None),
            P("grp", "mem", None, None),
            P("grp", "mem", None),
            P("grp", "mem", None, None),
            P("grp", None, None),
        ),
        out_specs=(P("mem", None), P(), P("grp", "mem", None, None), P("grp", "mem", None, None)),
        check_vma=False,
    )
```

time: 220 us -> 89.7 us (0.41)
  blocking collectives: 82.6 us -> 0 us
  other arithmetic: 62.1 us -> 2.1 us
  Pallas kernels: 0 us -> 26 us
  waiting for transfers between devices: 0.02 us -> 23.4 us
  local copies, waits for them, and re-layouts: 26 us -> 6.85 us
  matrix products: 19.2 us -> 2.49 us
  between operations: 16.8 us -> 3.6 us
  starting transfers between devices: 12.1 us -> 24.4 us
    psum x2 -> x0, blocking collectives: 76.4 us -> none  [the longest x1 41.9 us: per_device(): lax.psum(jnp.sum(delta_rows.astype(jnp.float32), axis=0), ('grp', 'mem'))]
    reduce_sum x10 -> x1, other arithmetic: 51.4 us -> 0.64 us  [per_device(): whole_id = jnp.sum(jnp.where(table_owner[0] == position, order, 0))]
    pallas_call x0 -> x4, Pallas kernels: none -> 26 us  [the longest x1 10.8 us: hit_counts(): pl.pallas_call(functools.partial(count_kernel, bits), out_shape=[jax.Shap...]
    ppermute x0 -> x27, starting transfers between devices: none -> 24.4 us  [send(): return lax.ppermute(values, ('grp', 'mem'), pairs)]
    ppermute x0 -> x27, waiting for transfers between devices: none -> 23.4 us  [send(): return lax.ppermute(values, ('grp', 'mem'), pairs)]
    dot_general x11 -> x1, matrix products: 19.2 us -> 2.49 us  [per_device(): pre_act = jnp.dot(pooled, w_first, preferred_element_type=F32) + bias_first]
    all_to_all x2 -> x0, starting transfers between devices: 12 us -> none  [the longest x1 7.39 us: per_device(): lax.all_to_all(send_split, 'mem', split_axis=1, concat_axis=0, tiled=True)]
    unnamed x14 -> x48, local copies, waits for them, and re-layouts: 10.9 us -> 0.67 us
  transfers between devices with their start and end apart: 3 -> 27, of which waited for: 0 -> 10; matrix products, arithmetic and copies ran while one was open for 42% -> 8% of each run, Pallas kernels for 0% -> 29%
where the time goes in v1:
time: 89.7 us; the launch traced here: 88.9 us
  Pallas kernels  26 us (29%)
  starting transfers between devices  24.4 us (27%)
  waiting for transfers between devices  23.4 us (26%)
  local copies, waits for them, and re-layouts  6.85 us (8%)
  between operations  3.6 us (4%)
  matrix products  2.49 us (3%)
  other arithmetic  2.1 us (2%)
    ppermute x27, starting transfers between devices, send(): return lax.ppermute(values, ('grp', 'mem'), pairs)  24.4 us
    ppermute x27, waiting for transfers between devices, send(): return lax.ppermute(values, ('grp', 'mem'), pairs)  23.4 us
    pallas_call x1, Pallas kernels, hit_counts(): pl.pallas_call(functools.partial(count_kernel, bits), out_shape=[jax.Shap...  10.8 us
    pallas_call x1, Pallas kernels, table_update(): pl.pallas_call(functools.partial(table_kernel, chunks), out_shape=[jax.Sh...  9.85 us
    pallas_call x1, Pallas kernels, partial_gradient(): pl.pallas_call(functools.partial(partial_kernel, spans, half_rows), out_s...  3.21 us
    squeeze x4, local copies, waits for them, and re-layouts, per_device(): pooled_pieces += [arrived[chip][0], crossed[chip]]  2.67 us
    dot_general x1, matrix products, per_device(): pre_act = jnp.dot(pooled, w_first, preferred_element_type=F32) + bias_first  2.49 us
    pallas_call x1, Pallas kernels, pack(): pl.pallas_call(functools.partial(pack_kernel, spans, half_rows), out_shap...  2.16 us
  transfers between devices with their start and end apart: 27, of which 10 were waited for; matrix products, arithmetic and copies ran while one was open for 8% of the time, Pallas kernels for 29%

profile of v1, /device:TPU:0, one launch (start us, length us, event | category | flops | bytes accessed | tf_op | source)
XLA Modules:
  0.0 88.9 jit_solution(4067522662620132179)
XLA Ops:
  0.7 2.5 %multiply_convert_fusion.refs_8_.refs_0_ = bf16[128,512]{1,0:T(8,128)(2,1)S(1)} fusion(bf16[128,2560]{1,0:T(8,128)(2,1)} %pooled_ref.1, bf16[2560,512]{1,0:T(8,128)(2,1)} %refs_17_.1, bf16[128,512]{1,0:T(8,128)(2,1)} %param.13, f32[512]{0:T(512)} %param.15), kind=kOutput, calls=%fused_computation.3 | convolution fusion | flops 336265216 | bytes 3540992 | tf_op jit(solution)/shard_map/dot_general | solution.py:254
  3.2 0.0 copy-start.21
  3.2 4.1 %collective-permute-start.19 = (bf16[128,512]{1,0:T(8,128)(2,1)S(1)}, bf16[128,512]{1,0:T(8,128)(2,1)S(1)}, u32[]{:S(2)}, u32[]{:S(2)}) collective-permute-start(bf16[128,512]{1,0:T(8,128)(2,1)S(1)} %multiply_convert_fusion.refs_8_.refs_0_), channel_id=1, source_target_pairs={{0,8},{1,9},{2,10},{3,11},{4,12},{5,13},{6,14},{7,15},{8,0},{9,1},... | collective-permute-start | bytes 393224 | tf_op jit(solution)/shard_map/ppermute | solution.py:252
  7.3 1.6 %collective-permute-start.15 = (bf16[128,512]{1,0:T(8,128)(2,1)S(1)}, bf16[128,512]{1,0:T(8,128)(2,1)S(1)}, u32[]{:S(2)}, u32[]{:S(2)}) collective-permute-start(bf16[128,512]{1,0:T(8,128)(2,1)S(1)} %multiply_convert_fusion.refs_8_.refs_0_), channel_id=1, source_target_pairs={{0,4},{1,5},{2,6},{3,7},{4,0},{5,1},{6,2},{7,3},{8,12},{9,13},{10,... | collective-permute-start | bytes 393224 | tf_op jit(solution)/shard_map/ppermute | solution.py:252
  8.9 1.5 %collective-permute-start.5 = (bf16[128,512]{1,0:T(8,128)(2,1)S(1)}, bf16[128,512]{1,0:T(8,128)(2,1)S(1)}, u32[]{:S(2)}, u32[]{:S(2)}) collective-permute-start(bf16[128,512]{1,0:T(8,128)(2,1)S(1)} %multiply_convert_fusion.refs_8_.refs_0_), channel_id=1, source_target_pairs={{0,2},{1,3},{2,0},{3,1},{4,6},{5,7},{6,4},{7,5},{8,10},{9,11},{10,... | collective-permute-start | bytes 393224 | tf_op jit(solution)/shard_map/ppermute | solution.py:252
  10.4 0.0 collective-permute-start.4
  10.4 0.6 fusion.1
  13.6 1.3 %stack.26.idx_ref = s32[5]{0:T(128)} concatenate(s32[1]{0:T(128)} %bitcast, s32[1]{0:T(128)} %bitcast.1, s32[1]{0:T(128)} %bitcast.3, s32[1]{0:T(128)} %bitcast.5, s32[1]{0:T(128)} %bitcast.6), dimensions={0} | concatenate | bytes 40 | tf_op jit(solution)/shard_map/stack | solution.py:241
  15.0 2.2 %pack.1 = (bf16[2,320,128]{2,1,0:T(8,128)(2,1)}, bf16[2,320,128]{2,1,0:T(8,128)(2,1)}, bf16[2,320,128]{2,1,0:T(8,128)(2,1)}, bf16[2,320,128]{2,1,0:T(8,128)(2,1)}) custom-call(s32[5]{0:T(128)} %stack.26.idx_ref, bf16[128,2560]{1,0:T(8,128)(2,1)} %pooled_ref.1), custom_call_target="tpu_custom_call" | custom-call | tf_op jit(solution)/shard_map/pack/pallas_call | solution.py:51
  17.1 1.5 %collective-permute-start.2 = (bf16[2,320,128]{2,1,0:T(8,128)(2,1)}, bf16[2,320,128]{2,1,0:T(8,128)(2,1)S(1)}, u32[]{:S(2)}, u32[]{:S(2)}) collective-permute-start(bf16[2,320,128]{2,1,0:T(8,128)(2,1)} %get-tuple-element.19), channel_id=1, source_target_pairs={{0,18},{1,19},{2,16},{3,17},{4,22},{5,23},{6,20},{7,21},{8,26},{9,... | collective-permute-start | bytes 491528 | tf_op jit(solution)/shard_map/ppermute | solution.py:252
  18.6 1.6 %fusion.3 = (bf16[1,320,128]{2,1,0:T(8,128)(2,1)S(1)}, bf16[320,128]{1,0:T(8,128)(2,1)}) fusion(bf16[2,320,128]{2,1,0:T(8,128)(2,1)} %get-tuple-element.16), kind=kLoop, calls=%fused_computation.22 | loop fusion | bytes 327680 | tf_op jit(solution)/shard_map/slice | solution.py:261
  20.2 4.7 %collective-permute-done.2 = bf16[2,320,128]{2,1,0:T(8,128)(2,1)S(1)} collective-permute-done((bf16[2,320,128]{2,1,0:T(8,128)(2,1)}, bf16[2,320,128]{2,1,0:T(8,128)(2,1)S(1)}, u32[]{:S(2)}, u32[]{:S(2)}) %collective-permute-start.2) | collective-permute-done | bytes 163872 | tf_op jit(solution)/shard_map/ppermute | solution.py:252
  24.8 1.5 %collective-permute-start.1 = (bf16[2,320,128]{2,1,0:T(8,128)(2,1)}, bf16[2,320,128]{2,1,0:T(8,128)(2,1)S(1)}, u32[]{:S(2)}, u32[]{:S(2)}) collective-permute-start(bf16[2,320,128]{2,1,0:T(8,128)(2,1)} %get-tuple-element.18), channel_id=1, source_target_pairs={{0,16},{1,17},{2,18},{3,19},{4,20},{5,21},{6,22},{7,23},{8,24},{9,... | collective-permute-start | bytes 491528 | tf_op jit(solution)/shard_map/ppermute | solution.py:252
  26.4 0.6 slice_bitcast_fusion.1
  27.0 3.8 %collective-permute-done.1 = bf16[2,320,128]{2,1,0:T(8,128)(2,1)S(1)} collective-permute-done((bf16[2,320,128]{2,1,0:T(8,128)(2,1)}, bf16[2,320,128]{2,1,0:T(8,128)(2,1)S(1)}, u32[]{:S(2)}, u32[]{:S(2)}) %collective-permute-start.1) | collective-permute-done | bytes 163872 | tf_op jit(solution)/shard_map/ppermute | solution.py:252
  30.8 0.5 collective-permute-start
  31.3 0.6 slice_bitcast_fusion.3
  32.0 4.3 %collective-permute-done = bf16[2,320,128]{2,1,0:T(8,128)(2,1)S(1)} collective-permute-done((bf16[2,320,128]{2,1,0:T(8,128)(2,1)}, bf16[2,320,128]{2,1,0:T(8,128)(2,1)S(1)}, u32[]{:S(2)}, u32[]{:S(2)}) %collective-permute-start) | collective-permute-done | bytes 163872 | tf_op jit(solution)/shard_map/ppermute | solution.py:252
  36.3 1.5 %collective-permute-start.9 = (bf16[128,512]{1,0:T(8,128)(2,1)S(1)}, bf16[128,512]{1,0:T(8,128)(2,1)S(1)}, u32[]{:S(2)}, u32[]{:S(2)}) collective-permute-start(bf16[128,512]{1,0:T(8,128)(2,1)S(1)} %multiply_convert_fusion.refs_8_.refs_0_), channel_id=1, source_target_pairs={{0,18},{1,19},{2,16},{3,17},{4,22},{5,23},{6,20},{7,21},{8,26},{9,... | collective-permute-start | bytes 393224 | tf_op jit(solution)/shard_map/ppermute | solution.py:252
  37.8 0.6 slice_bitcast_fusion.5
  38.5 0.0 collective-permute-done.19.refs_8_
  38.5 0.5 collective-permute-start.7
  39.0 0.1 collective-permute-start.3
  39.1 0.0 collective-permute-done.5.refs_10_.refs_2_
  39.1 1.6 %collective-permute-start.21 = (bf16[128,512]{1,0:T(8,128)(2,1)S(1)}, bf16[128,512]{1,0:T(8,128)(2,1)S(1)}, u32[]{:S(2)}, u32[]{:S(2)}) collective-permute-start(bf16[128,512]{1,0:T(8,128)(2,1)S(1)} %collective-permute-done.19.refs_8_), channel_id=1, source_target_pairs={{0,2},{1,3},{2,0},{3,1},{4,6},{5,7},{6,4},{7,5},{8,10},{9,11},{10,... | collective-permute-start | bytes 393224 | tf_op jit(solution)/shard_map/ppermute | solution.py:252
  40.7 0.5 collective-permute-start.23
  41.2 1.1 %collective-permute-done.9.refs_14_ = bf16[128,512]{1,0:T(8,128)(2,1)S(1)} collective-permute-done((bf16[128,512]{1,0:T(8,128)(2,1)S(1)}, bf16[128,512]{1,0:T(8,128)(2,1)S(1)}, u32[]{:S(2)}, u32[]{:S(2)}) %collective-permute-start.9) | collective-permute-done | bytes 131104 | tf_op jit(solution)/shard_map/ppermute | solution.py:252
  42.2 0.5 collective-permute-start.25
  42.7 0.9 %collective-permute-done.7.refs_12_ = bf16[128,512]{1,0:T(8,128)(2,1)S(1)} collective-permute-done((bf16[128,512]{1,0:T(8,128)(2,1)S(1)}, bf16[128,512]{1,0:T(8,128)(2,1)S(1)}, u32[]{:S(2)}, u32[]{:S(2)}) %collective-permute-start.7) | collective-permute-done | bytes 131104 | tf_op jit(solution)/shard_map/ppermute | solution.py:252
  43.6 0.0 collective-permute-start.20
  43.6 1.5 %collective-permute-done.21.refs_10_ = bf16[128,512]{1,0:T(8,128)(2,1)S(1)} collective-permute-done((bf16[128,512]{1,0:T(8,128)(2,1)S(1)}, bf16[128,512]{1,0:T(8,128)(2,1)S(1)}, u32[]{:S(2)}, u32[]{:S(2)}) %collective-permute-start.21) | collective-permute-done | bytes 131104 | tf_op jit(solution)/shard_map/ppermute | solution.py:252
  45.1 1.5 %collective-permute-start.17 = (bf16[128,512]{1,0:T(8,128)(2,1)S(1)}, bf16[128,512]{1,0:T(8,128)(2,1)S(1)}, u32[]{:S(2)}, u32[]{:S(2)}) collective-permute-start(bf16[128,512]{1,0:T(8,128)(2,1)S(1)} %collective-permute-done.15.refs_4_), channel_id=1, source_target_pairs={{0,2},{1,3},{2,0},{3,1},{4,6},{5,7},{6,4},{7,5},{8,10},{9,11},{10,... | collective-permute-start | bytes 393224 | tf_op jit(solution)/shard_map/ppermute | solution.py:252
  46.5 0.6 collective-permute-done.23.refs_12_
  47.1 0.0 collective-permute-start.6
  47.1 2.0 %collective-permute-done.25.refs_14_ = bf16[128,512]{1,0:T(8,128)(2,1)S(1)} collective-permute-done((bf16[128,512]{1,0:T(8,128)(2,1)S(1)}, bf16[128,512]{1,0:T(8,128)(2,1)S(1)}, u32[]{:S(2)}, u32[]{:S(2)}) %collective-permute-start.25) | collective-permute-done | bytes 131104 | tf_op jit(solution)/shard_map/ppermute | solution.py:252
  49.1 0.0 collective-permute-done.20.refs_9_
  49.1 0.5 collective-permute-start.8
  49.6 2.2 %collective-permute-done.17.refs_6_ = bf16[128,512]{1,0:T(8,128)(2,1)S(1)} collective-permute-done((bf16[128,512]{1,0:T(8,128)(2,1)S(1)}, bf16[128,512]{1,0:T(8,128)(2,1)S(1)}, u32[]{:S(2)}, u32[]{:S(2)}) %collective-permute-start.17) | collective-permute-done | bytes 131104 | tf_op jit(solution)/shard_map/ppermute | solution.py:252
  51.8 0.0 collective-permute-start.16
  51.9 0.5 collective-permute-start.22
  52.4 0.1 collective-permute-start.24
  52.4 0.0 collective-permute-done.8.refs_13_
  52.5 0.4 collective-permute-start.26
  52.9 0.0 collective-permute-done.3
  52.9 0.1 collective-permute-start.18
  53.0 0.7 slice_bitcast_fusion
  53.8 3.2 %partial_gradient.1 = (f32[96,512]{1,0:T(8,128)}, bf16[96,512]{1,0:T(8,128)(2,1)}, bf16[96,512]{1,0:T(8,128)(2,1)}, bf16[96,512]{1,0:T(8,128)(2,1)}) custom-call(s32[5]{0:T(128)} %stack.26.idx_ref, bf16[320,128]{1,0:T(8,128)(2,1)} %get-tuple-element.41.refs_0_, bf16[320,128]{1,0:T(8,128)(2,1)} %get-tuple-element.31.refs_1_, ...), custom_call_target="tpu_custom_call" | custom-call | tf_op jit(solution)/shard_map/partial_gradient/pallas_call | solution.py:209
  57.0 0.5 collective-permute-start.11
  57.5 0.0 collective-permute-done.22.refs_11_
  57.5 0.2 collective-permute-start.12
  57.7 3.7 %collective-permute-start.13 = (bf16[96,512]{1,0:T(8,128)(2,1)}, bf16[96,512]{1,0:T(8,128)(2,1)S(1)}, u32[]{:S(2)}, u32[]{:S(2)}) collective-permute-start(bf16[96,512]{1,0:T(8,128)(2,1)} %get-tuple-element.23), channel_id=1, source_target_pairs={{0,12},{1,13},{2,14},{3,15},{4,8},{5,9},{6,10},{7,11},{8,4},{9,5},... | collective-permute-start | bytes 294920 | tf_op jit(solution)/shard_map/ppermute | solution.py:252
  61.5 0.6 broadcast_in_dim_squeeze.3.refs_23_
  62.1 10.8 %hit_counts.1 = (bf16[1024,2048]{1,0:T(8,128)(2,1)}, bf16[1024,2048]{1,0:T(8,128)(2,1)}) custom-call(s32[5]{0:T(128)} %stack.26.idx_ref, s32[8,2048]{1,0:T(8,128)} %bitcast.46, s32[4,8,2048]{2,1,0:T(8,128)} %bitcast.44), custom_call_target="tpu_custom_call" | custom-call | tf_op jit(solution)/shard_map/hit_counts/pallas_call | solution.py:87
  72.9 0.0 collective-permute-done.26.refs_15_
  72.9 0.0 collective-permute-done.18.refs_7_
  73.0 0.5 copy-done.15
  73.5 0.1 copy-done.16
  73.6 9.8 %table_update.1 = (f32[128,1024]{1,0:T(8,128)}, f32[32,1024]{1,0:T(8,128)}) custom-call(s32[5]{0:T(128)} %stack.26.idx_ref, bf16[128,512]{1,0:T(8,128)(2,1)} %copy-done, bf16[128,512]{1,0:T(8,128)(2,1)} %copy-done.2, bf16[128,512]{1,0:T(8,128)(2,1)} %copy-done.1, bf16[128,512]{1,0:T(8,128)(2,1)} %copy-done.3, bf16[128,512]{1,0:T(8,128)(2,1)} %copy-done.6, ...), custom_call_target="tpu_custom_call" | custom-call | tf_op jit(solution)/shard_map/table_update/pallas_call | solution.py:143
  83.4 0.0 collective-permute-done.11
  83.5 0.0 collective-permute-done.13
  83.6 1.6 %collective-permute-start.14 = (bf16[80,512]{1,0:T(8,128)(2,1)S(1)}, bf16[80,512]{1,0:T(8,128)(2,1)S(1)}, u32[]{:S(2)}, u32[]{:S(2)}) collective-permute-start(bf16[80,512]{1,0:T(8,128)(2,1)S(1)} %fusion), channel_id=1, source_target_pairs={{0,16},{1,17},{2,18},{3,19},{4,20},{5,21},{6,22},{7,23},{8,24},{9,... | collective-permute-start | bytes 245768 | tf_op jit(solution)/shard_map/ppermute | solution.py:252
  85.1 0.6 slice_add_fusion
  85.7 2.3 %collective-permute-done.14 = bf16[80,512]{1,0:T(8,128)(2,1)S(1)} collective-permute-done((bf16[80,512]{1,0:T(8,128)(2,1)S(1)}, bf16[80,512]{1,0:T(8,128)(2,1)S(1)}, u32[]{:S(2)}, u32[]{:S(2)}) %collective-permute-start.14) | collective-permute-done | bytes 81952 | tf_op jit(solution)/shard_map/ppermute | solution.py:252
  88.1 0.8 pad_maximum_fusion.1
  (57 shorter events, 0.2 us)
Async XLA Ops:
  0.6 9.7 %copy-start.22 = (s32[1,16]{1,0:T(1,128)S(1)}, s32[1,16]{1,0:T(1,128)}, u32[]{:S(2)}) copy-start(s32[1,16]{1,0:T(1,128)} %param.16) | copy-start | bytes 196
  0.6 9.7 %copy-start.23 = (s32[1,16]{1,0:T(1,128)S(1)}, s32[1,16]{1,0:T(1,128)}, u32[]{:S(2)}) copy-start(s32[1,16]{1,0:T(1,128)} %param.17) | copy-start | bytes 196
  3.1 50.6 %copy-start = (bf16[128,512]{1,0:T(8,128)(2,1)}, bf16[128,512]{1,0:T(8,128)(2,1)S(1)}, u32[]{:S(2)}) copy-start(bf16[128,512]{1,0:T(8,128)(2,1)S(1)} %multiply_convert_fusion.refs_8_.refs_0_) | copy-start | bytes 393220
  3.2 58.3 %copy-start.21 = (f32[1,4,1024]{2,1,0:T(4,128)S(1)}, f32[1,4,1024]{2,1,0:T(4,128)}, u32[]{:S(2)}) copy-start(f32[1,4,1024]{2,1,0:T(4,128)} %param.23) | copy-start | bytes 49156
  3.2 35.3 %collective-permute-start.19 = (bf16[128,512]{1,0:T(8,128)(2,1)S(1)}, bf16[128,512]{1,0:T(8,128)(2,1)S(1)}, u32[]{:S(2)}, u32[]{:S(2)}) collective-permute-start(bf16[128,512]{1,0:T(8,128)(2,1)S(1)} %multiply_convert_fusion.refs_8_.refs_0_), channel_id=1, source_target_pairs={{0,8},{1,9},{2,10},{3,11},{4,12},{5,13},{6,14},{7,15},{8,0},{9,1},... | collective-permute-start | bytes 393224 | tf_op jit(solution)/shard_map/ppermute | solution.py:252
  7.3 31.7 %collective-permute-start.15 = (bf16[128,512]{1,0:T(8,128)(2,1)S(1)}, bf16[128,512]{1,0:T(8,128)(2,1)S(1)}, u32[]{:S(2)}, u32[]{:S(2)}) collective-permute-start(bf16[128,512]{1,0:T(8,128)(2,1)S(1)} %multiply_convert_fusion.refs_8_.refs_0_), channel_id=1, source_target_pairs={{0,4},{1,5},{2,6},{3,7},{4,0},{5,1},{6,2},{7,3},{8,12},{9,13},{10,... | collective-permute-start | bytes 393224 | tf_op jit(solution)/shard_map/ppermute | solution.py:252
  8.9 30.2 %collective-permute-start.5 = (bf16[128,512]{1,0:T(8,128)(2,1)S(1)}, bf16[128,512]{1,0:T(8,128)(2,1)S(1)}, u32[]{:S(2)}, u32[]{:S(2)}) collective-permute-start(bf16[128,512]{1,0:T(8,128)(2,1)S(1)} %multiply_convert_fusion.refs_8_.refs_0_), channel_id=1, source_target_pairs={{0,2},{1,3},{2,0},{3,1},{4,6},{5,7},{6,4},{7,5},{8,10},{9,11},{10,... | collective-permute-start | bytes 393224 | tf_op jit(solution)/shard_map/ppermute | solution.py:252
  10.4 30.3 %collective-permute-start.4 = (bf16[128,512]{1,0:T(8,128)(2,1)S(1)}, bf16[128,512]{1,0:T(8,128)(2,1)S(1)}, u32[]{:S(2)}, u32[]{:S(2)}) collective-permute-start(bf16[128,512]{1,0:T(8,128)(2,1)S(1)} %multiply_convert_fusion.refs_8_.refs_0_), channel_id=1, source_target_pairs={{0,1},{1,0},{2,3},{3,2},{4,5},{5,4},{6,7},{7,6},{8,9},{9,8},{10,11... | collective-permute-start | bytes 393224 | tf_op jit(solution)/shard_map/ppermute | solution.py:252
  17.1 7.7 %collective-permute-start.2 = (bf16[2,320,128]{2,1,0:T(8,128)(2,1)}, bf16[2,320,128]{2,1,0:T(8,128)(2,1)S(1)}, u32[]{:S(2)}, u32[]{:S(2)}) collective-permute-start(bf16[2,320,128]{2,1,0:T(8,128)(2,1)} %get-tuple-element.19), channel_id=1, source_target_pairs={{0,18},{1,19},{2,16},{3,17},{4,22},{5,23},{6,20},{7,21},{8,26},{9,... | collective-permute-start | bytes 491528 | tf_op jit(solution)/shard_map/ppermute | solution.py:252
  24.8 6.0 %collective-permute-start.1 = (bf16[2,320,128]{2,1,0:T(8,128)(2,1)}, bf16[2,320,128]{2,1,0:T(8,128)(2,1)S(1)}, u32[]{:S(2)}, u32[]{:S(2)}) collective-permute-start(bf16[2,320,128]{2,1,0:T(8,128)(2,1)} %get-tuple-element.18), channel_id=1, source_target_pairs={{0,16},{1,17},{2,18},{3,19},{4,20},{5,21},{6,22},{7,23},{8,24},{9,... | collective-permute-start | bytes 491528 | tf_op jit(solution)/shard_map/ppermute | solution.py:252
  30.8 5.5 %collective-permute-start = (bf16[2,320,128]{2,1,0:T(8,128)(2,1)}, bf16[2,320,128]{2,1,0:T(8,128)(2,1)S(1)}, u32[]{:S(2)}, u32[]{:S(2)}) collective-permute-start(bf16[2,320,128]{2,1,0:T(8,128)(2,1)} %get-tuple-element.17), channel_id=1, source_target_pairs={{0,2},{1,3},{2,0},{3,1},{4,6},{5,7},{6,4},{7,5},{8,10},{9,11},{10,... | collective-permute-start | bytes 491528 | tf_op jit(solution)/shard_map/ppermute | solution.py:252
  36.3 5.9 %collective-permute-start.9 = (bf16[128,512]{1,0:T(8,128)(2,1)S(1)}, bf16[128,512]{1,0:T(8,128)(2,1)S(1)}, u32[]{:S(2)}, u32[]{:S(2)}) collective-permute-start(bf16[128,512]{1,0:T(8,128)(2,1)S(1)} %multiply_convert_fusion.refs_8_.refs_0_), channel_id=1, source_target_pairs={{0,18},{1,19},{2,16},{3,17},{4,22},{5,23},{6,20},{7,21},{8,26},{9,... | collective-permute-start | bytes 393224 | tf_op jit(solution)/shard_map/ppermute | solution.py:252
  38.5 34.5 %copy-start.5 = (bf16[128,512]{1,0:T(8,128)(2,1)}, bf16[128,512]{1,0:T(8,128)(2,1)S(1)}, u32[]{:S(2)}) copy-start(bf16[128,512]{1,0:T(8,128)(2,1)S(1)} %collective-permute-done.19.refs_8_) | copy-start | bytes 393220
  38.5 5.1 %collective-permute-start.7 = (bf16[128,512]{1,0:T(8,128)(2,1)S(1)}, bf16[128,512]{1,0:T(8,128)(2,1)S(1)}, u32[]{:S(2)}, u32[]{:S(2)}) collective-permute-start(bf16[128,512]{1,0:T(8,128)(2,1)S(1)} %multiply_convert_fusion.refs_8_.refs_0_), channel_id=1, source_target_pairs={{0,16},{1,17},{2,18},{3,19},{4,20},{5,21},{6,22},{7,23},{8,24},{9,... | collective-permute-start | bytes 393224 | tf_op jit(solution)/shard_map/ppermute | solution.py:252
  39.0 33.9 %copy-start.6 = (bf16[128,512]{1,0:T(8,128)(2,1)}, bf16[128,512]{1,0:T(8,128)(2,1)S(1)}, u32[]{:S(2)}) copy-start(bf16[128,512]{1,0:T(8,128)(2,1)S(1)} %collective-permute-done.15.refs_4_) | copy-start | bytes 393220
  39.0 13.8 %collective-permute-start.3 = (bf16[4,320,128]{2,1,0:T(8,128)(2,1)S(1)}, bf16[4,320,128]{2,1,0:T(8,128)(2,1)S(1)}, u32[]{:S(2)}, u32[]{:S(2)}) collective-permute-start(bf16[4,320,128]{2,1,0:T(8,128)(2,1)S(1)} %pad_maximum_fusion), channel_id=1, source_target_pairs={{0,1},{1,0},{2,3},{3,2},{4,5},{5,4},{6,7},{7,6},{8,9},{9,8},{10,11... | collective-permute-start | bytes 983048 | tf_op jit(solution)/shard_map/ppermute | solution.py:252
  39.1 14.6 %copy-start.1 = (bf16[128,512]{1,0:T(8,128)(2,1)}, bf16[128,512]{1,0:T(8,128)(2,1)S(1)}, u32[]{:S(2)}) copy-start(bf16[128,512]{1,0:T(8,128)(2,1)S(1)} %collective-permute-done.5.refs_10_.refs_2_) | copy-start | bytes 393220
  39.1 5.9 %collective-permute-start.21 = (bf16[128,512]{1,0:T(8,128)(2,1)S(1)}, bf16[128,512]{1,0:T(8,128)(2,1)S(1)}, u32[]{:S(2)}, u32[]{:S(2)}) collective-permute-start(bf16[128,512]{1,0:T(8,128)(2,1)S(1)} %collective-permute-done.19.refs_8_), channel_id=1, source_target_pairs={{0,2},{1,3},{2,0},{3,1},{4,6},{5,7},{6,4},{7,5},{8,10},{9,11},{10,... | collective-permute-start | bytes 393224 | tf_op jit(solution)/shard_map/ppermute | solution.py:252
  40.7 13.0 %copy-start.2 = (bf16[128,512]{1,0:T(8,128)(2,1)}, bf16[128,512]{1,0:T(8,128)(2,1)S(1)}, u32[]{:S(2)}) copy-start(bf16[128,512]{1,0:T(8,128)(2,1)S(1)} %collective-permute-done.4.refs_9_.refs_1_) | copy-start | bytes 393220
  40.7 6.4 %collective-permute-start.23 = (bf16[128,512]{1,0:T(8,128)(2,1)S(1)}, bf16[128,512]{1,0:T(8,128)(2,1)S(1)}, u32[]{:S(2)}, u32[]{:S(2)}) collective-permute-start(bf16[128,512]{1,0:T(8,128)(2,1)S(1)} %collective-permute-done.19.refs_8_), channel_id=1, source_target_pairs={{0,4},{1,5},{2,6},{3,7},{4,0},{5,1},{6,2},{7,3},{8,12},{9,13},{10,... | collective-permute-start | bytes 393224 | tf_op jit(solution)/shard_map/ppermute | solution.py:252
  42.2 11.5 %copy-start.17 = (bf16[128,512]{1,0:T(8,128)(2,1)}, bf16[128,512]{1,0:T(8,128)(2,1)S(1)}, u32[]{:S(2)}) copy-start(bf16[128,512]{1,0:T(8,128)(2,1)S(1)} %collective-permute-done.9.refs_14_) | copy-start | bytes 393220
  42.2 6.9 %collective-permute-start.25 = (bf16[128,512]{1,0:T(8,128)(2,1)S(1)}, bf16[128,512]{1,0:T(8,128)(2,1)S(1)}, u32[]{:S(2)}, u32[]{:S(2)}) collective-permute-start(bf16[128,512]{1,0:T(8,128)(2,1)S(1)} %collective-permute-done.19.refs_8_), channel_id=1, source_target_pairs={{0,6},{1,7},{2,4},{3,5},{4,2},{5,3},{6,0},{7,1},{8,14},{9,15},{10,... | collective-permute-start | bytes 393224 | tf_op jit(solution)/shard_map/ppermute | solution.py:252
  43.6 10.1 %copy-start.18 = (bf16[128,512]{1,0:T(8,128)(2,1)}, bf16[128,512]{1,0:T(8,128)(2,1)S(1)}, u32[]{:S(2)}) copy-start(bf16[128,512]{1,0:T(8,128)(2,1)S(1)} %collective-permute-done.7.refs_12_) | copy-start | bytes 393220
  43.6 5.5 %collective-permute-start.20 = (bf16[128,512]{1,0:T(8,128)(2,1)S(1)}, bf16[128,512]{1,0:T(8,128)(2,1)S(1)}, u32[]{:S(2)}, u32[]{:S(2)}) collective-permute-start(bf16[128,512]{1,0:T(8,128)(2,1)S(1)} %collective-permute-done.19.refs_8_), channel_id=1, source_target_pairs={{0,1},{1,0},{2,3},{3,2},{4,5},{5,4},{6,7},{7,6},{8,9},{9,8},{10,11... | collective-permute-start | bytes 393224 | tf_op jit(solution)/shard_map/ppermute | solution.py:252
  45.1 27.9 %copy-start.7 = (bf16[128,512]{1,0:T(8,128)(2,1)}, bf16[128,512]{1,0:T(8,128)(2,1)S(1)}, u32[]{:S(2)}) copy-start(bf16[128,512]{1,0:T(8,128)(2,1)S(1)} %collective-permute-done.21.refs_10_) | copy-start | bytes 393220
  45.1 6.8 %collective-permute-start.17 = (bf16[128,512]{1,0:T(8,128)(2,1)S(1)}, bf16[128,512]{1,0:T(8,128)(2,1)S(1)}, u32[]{:S(2)}, u32[]{:S(2)}) collective-permute-start(bf16[128,512]{1,0:T(8,128)(2,1)S(1)} %collective-permute-done.15.refs_4_), channel_id=1, source_target_pairs={{0,2},{1,3},{2,0},{3,1},{4,6},{5,7},{6,4},{7,5},{8,10},{9,11},{10,... | collective-permute-start | bytes 393224 | tf_op jit(solution)/shard_map/ppermute | solution.py:252
  47.1 25.9 %copy-start.8 = (bf16[128,512]{1,0:T(8,128)(2,1)}, bf16[128,512]{1,0:T(8,128)(2,1)S(1)}, u32[]{:S(2)}) copy-start(bf16[128,512]{1,0:T(8,128)(2,1)S(1)} %collective-permute-done.23.refs_12_) | copy-start | bytes 393220
  47.1 4.8 %collective-permute-start.6 = (bf16[128,512]{1,0:T(8,128)(2,1)S(1)}, bf16[128,512]{1,0:T(8,128)(2,1)S(1)}, u32[]{:S(2)}, u32[]{:S(2)}) collective-permute-start(bf16[128,512]{1,0:T(8,128)(2,1)S(1)} %collective-permute-done.5.refs_10_.refs_2_), channel_id=1, source_target_pairs={{0,1},{1,0},{2,3},{3,2},{4,5},{5,4},{6,7},{7,6},{8,9},{9,8},{10,11... | collective-permute-start | bytes 393224 | tf_op jit(solution)/shard_map/ppermute | solution.py:252
  49.1 23.8 %copy-start.9 = (bf16[128,512]{1,0:T(8,128)(2,1)}, bf16[128,512]{1,0:T(8,128)(2,1)S(1)}, u32[]{:S(2)}) copy-start(bf16[128,512]{1,0:T(8,128)(2,1)S(1)} %collective-permute-done.25.refs_14_) | copy-start | bytes 393220
  49.1 3.2 %collective-permute-start.10 = (bf16[128,512]{1,0:T(8,128)(2,1)S(1)}, bf16[128,512]{1,0:T(8,128)(2,1)S(1)}, u32[]{:S(2)}, u32[]{:S(2)}) collective-permute-start(bf16[128,512]{1,0:T(8,128)(2,1)S(1)} %collective-permute-done.9.refs_14_), channel_id=1, source_target_pairs={{0,1},{1,0},{2,3},{3,2},{4,5},{5,4},{6,7},{7,6},{8,9},{9,8},{10,11... | collective-permute-start | bytes 393224 | tf_op jit(solution)/shard_map/ppermute | solution.py:252
  49.1 23.8 %copy-start.10 = (bf16[128,512]{1,0:T(8,128)(2,1)}, bf16[128,512]{1,0:T(8,128)(2,1)S(1)}, u32[]{:S(2)}) copy-start(bf16[128,512]{1,0:T(8,128)(2,1)S(1)} %collective-permute-done.20.refs_9_) | copy-start | bytes 393220
  49.1 3.3 %collective-permute-start.8 = (bf16[128,512]{1,0:T(8,128)(2,1)S(1)}, bf16[128,512]{1,0:T(8,128)(2,1)S(1)}, u32[]{:S(2)}, u32[]{:S(2)}) collective-permute-start(bf16[128,512]{1,0:T(8,128)(2,1)S(1)} %collective-permute-done.7.refs_12_), channel_id=1, source_target_pairs={{0,1},{1,0},{2,3},{3,2},{4,5},{5,4},{6,7},{7,6},{8,9},{9,8},{10,11... | collective-permute-start | bytes 393224 | tf_op jit(solution)/shard_map/ppermute | solution.py:252
  51.8 21.1 %copy-start.11 = (bf16[128,512]{1,0:T(8,128)(2,1)}, bf16[128,512]{1,0:T(8,128)(2,1)S(1)}, u32[]{:S(2)}) copy-start(bf16[128,512]{1,0:T(8,128)(2,1)S(1)} %collective-permute-done.17.refs_6_) | copy-start | bytes 393220
  51.8 5.2 %collective-permute-start.16 = (bf16[128,512]{1,0:T(8,128)(2,1)S(1)}, bf16[128,512]{1,0:T(8,128)(2,1)S(1)}, u32[]{:S(2)}, u32[]{:S(2)}) collective-permute-start(bf16[128,512]{1,0:T(8,128)(2,1)S(1)} %collective-permute-done.15.refs_4_), channel_id=1, source_target_pairs={{0,1},{1,0},{2,3},{3,2},{4,5},{5,4},{6,7},{7,6},{8,9},{9,8},{10,11... | collective-permute-start | bytes 393224 | tf_op jit(solution)/shard_map/ppermute | solution.py:252
  51.9 1.9 %copy-start.3 = (bf16[128,512]{1,0:T(8,128)(2,1)}, bf16[128,512]{1,0:T(8,128)(2,1)S(1)}, u32[]{:S(2)}) copy-start(bf16[128,512]{1,0:T(8,128)(2,1)S(1)} %collective-permute-done.6.refs_11_.refs_3_) | copy-start | bytes 393220
  51.9 5.7 %collective-permute-start.22 = (bf16[128,512]{1,0:T(8,128)(2,1)S(1)}, bf16[128,512]{1,0:T(8,128)(2,1)S(1)}, u32[]{:S(2)}, u32[]{:S(2)}) collective-permute-start(bf16[128,512]{1,0:T(8,128)(2,1)S(1)} %collective-permute-done.21.refs_10_), channel_id=1, source_target_pairs={{0,1},{1,0},{2,3},{3,2},{4,5},{5,4},{6,7},{7,6},{8,9},{9,8},{10,11... | collective-permute-start | bytes 393224 | tf_op jit(solution)/shard_map/ppermute | solution.py:252
  52.4 1.4 %copy-start.19 = (bf16[128,512]{1,0:T(8,128)(2,1)}, bf16[128,512]{1,0:T(8,128)(2,1)S(1)}, u32[]{:S(2)}) copy-start(bf16[128,512]{1,0:T(8,128)(2,1)S(1)} %collective-permute-done.10.refs_15_) | copy-start | bytes 393220
  52.4 5.4 %collective-permute-start.24 = (bf16[128,512]{1,0:T(8,128)(2,1)S(1)}, bf16[128,512]{1,0:T(8,128)(2,1)S(1)}, u32[]{:S(2)}, u32[]{:S(2)}) collective-permute-start(bf16[128,512]{1,0:T(8,128)(2,1)S(1)} %collective-permute-done.23.refs_12_), channel_id=1, source_target_pairs={{0,1},{1,0},{2,3},{3,2},{4,5},{5,4},{6,7},{7,6},{8,9},{9,8},{10,11... | collective-permute-start | bytes 393224 | tf_op jit(solution)/shard_map/ppermute | solution.py:252
  52.5 1.3 %copy-start.20 = (bf16[128,512]{1,0:T(8,128)(2,1)}, bf16[128,512]{1,0:T(8,128)(2,1)S(1)}, u32[]{:S(2)}) copy-start(bf16[128,512]{1,0:T(8,128)(2,1)S(1)} %collective-permute-done.8.refs_13_) | copy-start | bytes 393220
  52.5 20.4 %collective-permute-start.26 = (bf16[128,512]{1,0:T(8,128)(2,1)S(1)}, bf16[128,512]{1,0:T(8,128)(2,1)S(1)}, u32[]{:S(2)}, u32[]{:S(2)}) collective-permute-start(bf16[128,512]{1,0:T(8,128)(2,1)S(1)} %collective-permute-done.25.refs_14_), channel_id=1, source_target_pairs={{0,1},{1,0},{2,3},{3,2},{4,5},{5,4},{6,7},{7,6},{8,9},{9,8},{10,11... | collective-permute-start | bytes 393224 | tf_op jit(solution)/shard_map/ppermute | solution.py:252
  52.9 20.0 %collective-permute-start.18 = (bf16[128,512]{1,0:T(8,128)(2,1)S(1)}, bf16[128,512]{1,0:T(8,128)(2,1)S(1)}, u32[]{:S(2)}, u32[]{:S(2)}) collective-permute-start(bf16[128,512]{1,0:T(8,128)(2,1)S(1)} %collective-permute-done.17.refs_6_), channel_id=1, source_target_pairs={{0,1},{1,0},{2,3},{3,2},{4,5},{5,4},{6,7},{7,6},{8,9},{9,8},{10,11... | collective-permute-start | bytes 393224 | tf_op jit(solution)/shard_map/ppermute | solution.py:252
  57.0 16.0 %copy-start.12 = (bf16[128,512]{1,0:T(8,128)(2,1)}, bf16[128,512]{1,0:T(8,128)(2,1)S(1)}, u32[]{:S(2)}) copy-start(bf16[128,512]{1,0:T(8,128)(2,1)S(1)} %collective-permute-done.16.refs_5_) | copy-start | bytes 393220
  57.0 26.4 %collective-permute-start.11 = (bf16[96,512]{1,0:T(8,128)(2,1)}, bf16[96,512]{1,0:T(8,128)(2,1)S(1)}, u32[]{:S(2)}, u32[]{:S(2)}) collective-permute-start(bf16[96,512]{1,0:T(8,128)(2,1)} %get-tuple-element.21), channel_id=1, source_target_pairs={{0,4},{1,5},{2,6},{3,7},{4,0},{5,1},{6,2},{7,3},{8,12},{9,13},{10,... | collective-permute-start | bytes 294920 | tf_op jit(solution)/shard_map/ppermute | solution.py:252
  57.5 15.5 %copy-start.13 = (bf16[128,512]{1,0:T(8,128)(2,1)}, bf16[128,512]{1,0:T(8,128)(2,1)S(1)}, u32[]{:S(2)}) copy-start(bf16[128,512]{1,0:T(8,128)(2,1)S(1)} %collective-permute-done.22.refs_11_) | copy-start | bytes 393220
  57.5 25.9 %collective-permute-start.12 = (bf16[96,512]{1,0:T(8,128)(2,1)}, bf16[96,512]{1,0:T(8,128)(2,1)S(1)}, u32[]{:S(2)}, u32[]{:S(2)}) collective-permute-start(bf16[96,512]{1,0:T(8,128)(2,1)} %get-tuple-element.22), channel_id=1, source_target_pairs={{0,8},{1,9},{2,10},{3,11},{4,12},{5,13},{6,14},{7,15},{8,0},{9,1},... | collective-permute-start | bytes 294920 | tf_op jit(solution)/shard_map/ppermute | solution.py:252
  57.7 15.3 %copy-start.14 = (bf16[128,512]{1,0:T(8,128)(2,1)}, bf16[128,512]{1,0:T(8,128)(2,1)S(1)}, u32[]{:S(2)}) copy-start(bf16[128,512]{1,0:T(8,128)(2,1)S(1)} %collective-permute-done.24.refs_13_) | copy-start | bytes 393220
  57.7 25.7 %collective-permute-start.13 = (bf16[96,512]{1,0:T(8,128)(2,1)}, bf16[96,512]{1,0:T(8,128)(2,1)S(1)}, u32[]{:S(2)}, u32[]{:S(2)}) collective-permute-start(bf16[96,512]{1,0:T(8,128)(2,1)} %get-tuple-element.23), channel_id=1, source_target_pairs={{0,12},{1,13},{2,14},{3,15},{4,8},{5,9},{6,10},{7,11},{8,4},{9,5},... | collective-permute-start | bytes 294920 | tf_op jit(solution)/shard_map/ppermute | solution.py:252
  72.9 0.6 copy-start.15
  72.9 0.7 copy-start.16
  73.6 9.9 %copy-start.4 = (f32[96,512]{1,0:T(8,128)S(1)}, f32[96,512]{1,0:T(8,128)}, u32[]{:S(2)}) copy-start(f32[96,512]{1,0:T(8,128)} %get-tuple-element.20) | copy-start | bytes 589828
  83.6 4.5 %collective-permute-start.14 = (bf16[80,512]{1,0:T(8,128)(2,1)S(1)}, bf16[80,512]{1,0:T(8,128)(2,1)S(1)}, u32[]{:S(2)}, u32[]{:S(2)}) collective-permute-start(bf16[80,512]{1,0:T(8,128)(2,1)S(1)} %fusion), channel_id=1, source_target_pairs={{0,16},{1,17},{2,18},{3,19},{4,20},{5,21},{6,22},{7,23},{8,24},{9,... | collective-permute-start | bytes 245768 | tf_op jit(solution)/shard_map/ppermute | solution.py:252

commit v2 on v0

v2 whole, which is shorter than its diff:
```python
import functools

import jax
import jax.numpy as jnp
from jax import lax
from jax.experimental import pallas as pl
from jax.experimental.pallas import tpu as pltpu
from jax.sharding import PartitionSpec as P

E = 128
CS = 4
LEARN_RATE = 0.5
EPSILON = 1e-08
BF16 = jnp.bfloat16
F32 = jnp.float32

NT_DIMS = (((1,), (1,)), ((), ()))
NN_DIMS = (((1,), (0,)), ((), ()))


def dot_nt(lhs, rhs):
    return lax.dot_general(lhs, rhs, NT_DIMS, preferred_element_type=F32)


def dot_nn(lhs, rhs):
    return lax.dot_general(lhs, rhs, NN_DIMS, preferred_element_type=F32)


def word_kernel(bits, turns, idx_ref, whole_ref, split_ref, *outs):
    samples = outs[0].shape[1] // len(turns[0])
    for keys_ref, table in ((whole_ref, 0), (split_ref, 1)):
        pool = keys_ref.shape[0]
        for stage, order in enumerate(turns):
            out = outs[2 * stage + table]
            low_rows = out.shape[0]
            shift = low_rows.bit_length() - 1
            spots = lax.broadcasted_iota(jnp.int32, (low_rows, samples), 0)
            for spot, turn in enumerate(order):
                lane = pl.multiple_of(jnp.bitwise_xor(idx_ref[0], turn) * samples, samples)
                keys = keys_ref[:, pl.ds(lane, samples)]
                low = jnp.bitwise_and(keys, low_rows - 1)
                field = lax.shift_right_logical(keys, jnp.full_like(keys, shift))
                unit = lax.shift_left(jnp.ones_like(keys), field * bits)
                words = jnp.zeros((low_rows, samples), jnp.int32)
                for place in range(pool):
                    row = slice(place, place + 1)
                    words = words + jnp.where(spots == low[row, :], unit[row, :], 0)
                out[:, spot * samples : (spot + 1) * samples] = words


def hit_words(idx, keys_whole, keys_split, rows_whole, rows_split, samples, turns):
    pool, total = keys_whole.shape
    bits = pool.bit_length()
    fields = 32 // bits
    whole = lambda i, idx: (0, 0)
    shapes = [
        jax.ShapeDtypeStruct((rows // fields, len(order) * samples), jnp.int32)
        for order in turns
        for rows in (rows_whole, rows_split)
    ]
    return pl.pallas_call(
        functools.partial(word_kernel, bits, turns),
        out_shape=shapes,
        grid_spec=pltpu.PrefetchScalarGridSpec(
            num_scalar_prefetch=1,
            grid=(1,),
            in_specs=[
                pl.BlockSpec((pool, total), whole),
                pl.BlockSpec((None, pool, total), lambda i, idx: (idx[3], 0, 0)),
            ],
            out_specs=[pl.BlockSpec(shape.shape, whole) for shape in shapes],
        ),
        cost_estimate=pl.CostEstimate(flops=4_000_000_000, bytes_accessed=2_000_000, transcendentals=0),
        name="hit_words",
    )(idx, keys_whole, keys_split)


def slot_gradients(bits, refs, w_whole, w_split, words_whole, words_split, back, hits, take):
    spot = 0
    for ref in refs:
        rows = ref.shape[0]
        lanes = slice(spot, spot + rows)
        back[:E, lanes] = dot_nt(w_whole[...], ref[...]).astype(BF16)
        back[E:, lanes] = dot_nt(w_split[...], ref[...]).astype(BF16)
        spot += rows
    fields = 32 // bits
    for table, words in enumerate((words_whole, words_split)):
        low = words.shape[0]
        for field in range(fields):
            packed = words[...]
            count = lax.shift_right_logical(packed, jnp.full_like(packed, field * bits))
            count = jnp.bitwise_and(count, (1 << bits) - 1)
            hits[field * low : (field + 1) * low, :] = count.astype(F32).astype(BF16)
        for first in range(0, fields * low, 2 * low):
            rows = slice(first, first + 2 * low)
            take(table, rows, dot_nt(back[table * E : (table + 1) * E, :], hits[rows, :]))


def early_kernel(bits, count, idx_ref, *refs):
    arrays, rest = refs[:count], refs[count:]
    w_whole, w_split, words_whole, words_split, out_whole, out_split, back, hits = rest
    outs = (out_whole, out_split)

    def take(table, rows, grad):
        outs[table][:, rows] = grad

    slot_gradients(bits, arrays, w_whole, w_split, words_whole, words_split, back, hits, take)


def late_kernel(bits, count, idx_ref, *refs):
    arrays, rest = refs[:count], refs[count:]
    (w_whole, w_split, words_whole, words_split, sum_whole, sum_split, table_whole, accum_whole,
     table_split, accum_split, new_whole, new_split, back, hits, grads) = rest
    columns = table_split.shape[0]
    first = pl.multiple_of(idx_ref[4] * columns, columns)

    def take(table, rows, grad):
        accum = (accum_whole, accum_split)[table]
        grad = grad + (sum_whole, sum_split)[table][:, rows]
        squares = jnp.sum(grad * grad, axis=0, keepdims=True)
        scale = LEARN_RATE / (jnp.sqrt(accum[:, rows] + squares / E) + EPSILON)
        if table == 0:
            new_whole[:, rows] = table_whole[:, rows] - grad * scale
        else:
            grads[...] = grad
            own = grads[pl.ds(first, columns), :]
            new_split[:, rows] = table_split[:, rows] - own * scale

    slot_gradients(bits, arrays, w_whole, w_split, words_whole, words_split, back, hits, take)


def slot_call(kernel, name, idx, arrays, w_first, words, whole_tables, bits, extra, out_shape, more):
    hidden = w_first.shape[1]
    fixed = lambda i, idx: (0, 0)
    specs = [pl.BlockSpec(array.shape, fixed) for array in arrays]
    specs += [
        pl.BlockSpec((E, hidden), lambda i, idx: (idx[2], 0)),
        pl.BlockSpec((E, hidden), lambda i, idx: (whole_tables + idx[3], 0)),
    ]
    specs += [pl.BlockSpec(word.shape, fixed) for word in words]
    for array in extra:
        if array.ndim == 2:
            specs.append(pl.BlockSpec(array.shape, fixed))
        else:
            specs.append(pl.BlockSpec((None,) + array.shape[1:], lambda i, idx: (idx[3], 0, 0)))
    low, total = words[0].shape
    rows = low * (32 // bits)
    return pl.pallas_call(
        functools.partial(kernel, bits, len(arrays)),
        out_shape=out_shape,
        grid_spec=pltpu.PrefetchScalarGridSpec(
            num_scalar_prefetch=1,
            grid=(1,),
            in_specs=specs,
            out_specs=[pl.BlockSpec(shape.shape, fixed) for shape in out_shape],
            scratch_shapes=[pltpu.VMEM((2 * E, total), BF16), pltpu.VMEM((rows, total), BF16)]
            + more(low),
        ),
        cost_estimate=pl.CostEstimate(flops=4_000_000_000, bytes_accessed=4_000_000, transcendentals=0),
        name=name,
    )(idx, *arrays, w_first, w_first, *words, *extra)


def block_kernel(places, count, idx_ref, *refs):
    arrays, pooled, out, acc = refs[:count], refs[count], refs[count + 1], refs[count + 2]
    samples = pooled.shape[2]
    sums = []
    for turn, (array, row) in enumerate(places):
        rows = arrays[array][row : row + samples, :]
        piece = dot_nn(pooled[jnp.bitwise_xor(idx_ref[0], turn)], rows)
        if turn == 0:
            acc[...] = piece
        else:
            acc[...] += piece
        sums.append(jnp.sum(rows.astype(F32), axis=0, keepdims=True))
    while len(sums) > 1:
        sums = [a + b for a, b in zip(sums[0::2], sums[1::2])]
    high = sums[0].astype(BF16)
    low = (sums[0] - high.astype(F32)).astype(BF16)
    block = acc.shape[0]
    out[:block, :] = acc[...].astype(BF16)
    place = lax.broadcasted_iota(jnp.int32, (16, acc.shape[1]), 0)
    extra = jnp.where(place == 0, high.astype(F32), jnp.where(place == 1, low.astype(F32), 0.0))
    out[block:, :] = extra.astype(BF16)


def block_gradient(idx, arrays, places, pooled):
    hidden = arrays[0].shape[1]
    block = pooled.shape[1]
    vmem = pl.BlockSpec(memory_space=pltpu.VMEM)
    return pl.pallas_call(
        functools.partial(block_kernel, places, len(arrays)),
        out_shape=jax.ShapeDtypeStruct((block + 16, hidden), BF16),
        in_specs=[pl.BlockSpec(memory_space=pltpu.SMEM)] + [vmem] * (len(arrays) + 1),
        out_specs=vmem,
        scratch_shapes=[pltpu.VMEM((block, hidden), F32)],
        cost_estimate=pl.CostEstimate(flops=1_000_000_000, bytes_accessed=3_000_000, transcendentals=0),
        name="block_gradient",
    )(idx, *arrays, pooled)


def per_device(
    groups,
    owners,
    pooled,
    grad_hidden,
    w_first,
    bias_first,
    table_owner,
    shard_owner,
    lookups_whole,
    lookups_split,
    table_whole,
    accum_whole,
    table_split,
    accum_split,
):
    position = lax.axis_index("mem")
    order = lax.iota(jnp.int32, owners)
    whole_id = jnp.sum(jnp.where(table_owner[0] == position, order, 0))
    shard_id = jnp.sum(jnp.where(shard_owner[0] == position, order, 0))
    idx = jnp.stack([position, position, whole_id, shard_id // CS, shard_id % CS])
    samples, features = pooled.shape

    def send(values, turn, side_turn=0):
        pairs = [
            (g * owners + m, (g ^ side_turn) * owners + (m ^ turn))
            for g in range(groups)
            for m in range(owners)
        ]
        return lax.ppermute(values, ("grp", "mem"), pairs)

    pre_act = jnp.dot(pooled, w_first, preferred_element_type=F32) + bias_first
    sigmoid_pre = jax.nn.sigmoid(pre_act)
    slope = sigmoid_pre * (1.0 + pre_act * (1.0 - sigmoid_pre))
    delta = (grad_hidden.astype(F32) * slope).astype(BF16)

    tops = [1 << b for b in range(1, owners.bit_length() - 1)]
    direct = [send(delta, top) for top in reversed(tops)][::-1]
    with jax.named_scope("cross0"):
        delta_crossed = send(delta, 1)

    pooled_here, _ = lax.optimization_barrier((pooled, delta))
    pooled_rows = pooled_here.T.reshape(owners, features // owners, samples)
    with jax.named_scope("pooled_exchange"):
        pooled_all = lax.all_to_all(pooled_rows, "mem", split_axis=0, concat_axis=0, tiled=True)

    arrays = [delta, delta_crossed]
    where = {0: (0, 0), 1: (1, 0)}
    joined = jnp.concatenate(direct)
    with jax.named_scope("cross1"):
        joined_crossed = send(joined, 1)
    for core, array in enumerate((joined, joined_crossed)):
        for spot, top in enumerate(tops):
            where[top + core] = (len(arrays), spot * samples)
        arrays.append(array)
    early = len(arrays)
    for rest in range(2, owners // 2, 2):
        highs = [spot for spot, top in enumerate(tops) if top > rest]
        with jax.named_scope("second"):
            got = send(jnp.concatenate([direct[spot] for spot in highs]), rest)
        with jax.named_scope("cross2"):
            got_crossed = send(got, 1)
        for core, array in enumerate((got, got_crossed)):
            for spot, high in enumerate(highs):
                where[tops[high] + rest + core] = (len(arrays), spot * samples)
            arrays.append(array)
    backward = {place: turn for turn, place in where.items()}
    turns = tuple(
        tuple(
            backward[(at, row)]
            for at in spots
            for row in range(0, arrays[at].shape[0], samples)
        )
        for spots in (range(early), range(early, len(arrays)))
    )

    rows_whole = table_whole.shape[-1]
    rows_split = table_split.shape[-1]
    keys_whole = lookups_whole[0, 0].T
    bits = keys_whole.shape[0].bit_length()
    words = hit_words(
        idx,
        keys_whole,
        jnp.transpose(lookups_split[0], (0, 2, 1)),
        rows_whole,
        rows_split,
        samples,
        turns,
    )
    sum_whole, sum_split = slot_call(
        early_kernel,
        "early_gradients",
        idx,
        arrays[:early],
        w_first,
        words[:2],
        owners,
        bits,
        [],
        [jax.ShapeDtypeStruct((E, rows_whole), F32), jax.ShapeDtypeStruct((E, rows_split), F32)],
        lambda low: [],
    )

    places = tuple(where[turn] for turn in range(owners))
    partial = block_gradient(idx, arrays, places, pooled_all)
    with jax.named_scope("groups"):
        total = partial.astype(F32) + send(partial, 0, 1).astype(F32)
    turn = 2
    while turn < groups:
        total = total + send(total, 0, turn)
        turn *= 2
    block = features // owners
    grad_first = total[:block]
    grad_bias = total[block] + total[block + 1]

    new_whole, new_split = slot_call(
        late_kernel,
        "late_gradients",
        idx,
        arrays[early:],
        w_first,
        words[2:],
        owners,
        bits,
        [
            sum_whole,
            sum_split,
            table_whole[0, 0],
            accum_whole[0],
            table_split[0, 0],
            accum_split[0][:, None, :],
        ],
        [
            jax.ShapeDtypeStruct(table_whole.shape[2:], F32),
            jax.ShapeDtypeStruct(table_split.shape[2:], F32),
        ],
        lambda low: [pltpu.VMEM((E, 2 * low), F32)],
    )
    return (grad_first, grad_bias, new_whole[None, None], new_split[None, None])


def solution(mesh):
    return jax.shard_map(
        functools.partial(per_device, mesh.shape["grp"], mesh.shape["mem"]),
        mesh=mesh,
        in_specs=(
            P(("grp", "mem"), None),
            P(("grp", "mem"), None),
            P(),
            P(),
            P("grp", None),
            P("grp", None),
            P("grp", "mem", None, None),
            P("grp", None, None, None),
            P("grp", "mem", None, None),
            P("grp", "mem", None),
            P("grp", "mem", None, None),
            P("grp", None, None),
        ),
        out_specs=(P("mem", None), P(), P("grp", "mem", None, None), P("grp", "mem", None, None)),
        check_vma=False,
    )
```

time: 220 us -> 55.1 us (0.25)
  blocking collectives: 82.6 us -> 0 us
  other arithmetic: 62.1 us -> 1.28 us
  local copies, waits for them, and re-layouts: 26 us -> 6.2 us
  Pallas kernels: 0 us -> 18.7 us
  matrix products: 19.2 us -> 2.54 us
  between operations: 16.8 us -> 3.49 us
  waiting for transfers between devices: 0.02 us -> 6.08 us
  starting transfers between devices: 12.1 us -> 16.4 us
    psum x2 -> x0, blocking collectives: 76.4 us -> none  [the longest x1 41.9 us: per_device(): lax.psum(jnp.sum(delta_rows.astype(jnp.float32), axis=0), ('grp', 'mem'))]
    reduce_sum x10 -> x1, other arithmetic: 51.4 us -> 0.64 us  [per_device(): whole_id = jnp.sum(jnp.where(table_owner[0] == position, order, 0))]
    pallas_call x0 -> x4, Pallas kernels: none -> 18.7 us  [the longest x2 11.1 us: slot_call(): pl.pallas_call(functools.partial(kernel, bits, len(arrays)), out_shape=ou...]
    dot_general x11 -> x1, matrix products: 19.2 us -> 2.54 us  [per_device(): pre_act = jnp.dot(pooled, w_first, preferred_element_type=F32) + bias_first]
    ppermute x0 -> x12, starting transfers between devices: none -> 12.8 us  [send(): return lax.ppermute(values, ('grp', 'mem'), pairs)]
    all_to_all x2 -> x1, starting transfers between devices: 12 us -> 3.59 us  [per_device(): lax.all_to_all(pooled_rows, 'mem', split_axis=0, concat_axis=0, tiled=True)]
    unnamed x14 -> x34, local copies, waits for them, and re-layouts: 10.9 us -> 2.45 us
    eq x16 -> x0, local copies, waits for them, and re-layouts: 6.77 us -> none  [accumulate(): pick_keys[:, :, None] == positions]
  transfers between devices with their start and end apart: 3 -> 13, of which waited for: 0 -> 3; matrix products, arithmetic and copies ran while one was open for 42% -> 7% of each run, Pallas kernels for 0% -> 28%
where the time goes in v2:
time: 55.1 us; the launch traced here: 54.6 us
  Pallas kernels  18.7 us (34%)
  starting transfers between devices  16.4 us (30%)
  local copies, waits for them, and re-layouts  6.2 us (11%)
  waiting for transfers between devices  6.08 us (11%)
  between operations  3.49 us (6%)
  matrix products  2.54 us (5%)
  other arithmetic  1.28 us (2%)
    ppermute x12, starting transfers between devices, send(): return lax.ppermute(values, ('grp', 'mem'), pairs)  12.8 us
    pallas_call x2, Pallas kernels, slot_call(): pl.pallas_call(functools.partial(kernel, bits, len(arrays)), out_shape=ou...  11.1 us
    ppermute x12, waiting for transfers between devices, send(): return lax.ppermute(values, ('grp', 'mem'), pairs)  6.07 us
    pallas_call x1, Pallas kernels, hit_words(): pl.pallas_call(functools.partial(word_kernel, bits, turns), out_shape=sha...  4.3 us
    all_to_all x1, starting transfers between devices, per_device(): lax.all_to_all(pooled_rows, 'mem', split_axis=0, concat_axis=0, tiled=True)  3.59 us
    pallas_call x1, Pallas kernels, block_gradient(): pl.pallas_call(functools.partial(block_kernel, places, len(arrays)), out_...  3.28 us
    dot_general x1, matrix products, per_device(): pre_act = jnp.dot(pooled, w_first, preferred_element_type=F32) + bias_first  2.54 us
    unnamed x34, local copies, waits for them, and re-layouts  2.45 us
  transfers between devices with their start and end apart: 13, of which 3 were waited for; matrix products, arithmetic and copies ran while one was open for 7% of the time, Pallas kernels for 28%

profile of v2, /device:TPU:0, one launch (start us, length us, event | category | flops | bytes accessed | tf_op | source)
XLA Modules:
  0.0 54.6 jit_solution(9426967696426308992)
XLA Ops:
  0.6 0.0 copy-start
  0.6 0.0 copy-start.5
  0.7 0.0 copy-start.6
  0.7 2.5 %multiply_convert_fusion.refs_0_ = bf16[128,512]{1,0:T(8,128)(2,1)S(1)} fusion(bf16[128,2560]{1,0:T(8,128)(2,1)} %param.12, bf16[2560,512]{1,0:T(8,128)(2,1)} %refs_7_.1, bf16[128,512]{1,0:T(8,128)(2,1)} %param.13, f32[512]{0:T(512)} %param.15), kind=kOutput, calls=%fused_computation.3 | convolution fusion | flops 336265216 | bytes 3540992 | tf_op jit(solution)/shard_map/dot_general | solution.py:233
  3.2 0.0 copy-start.10
  3.2 3.0 %collective-permute-start.1 = (bf16[128,512]{1,0:T(8,128)(2,1)S(1)}, bf16[128,512]{1,0:T(8,128)(2,1)S(1)}, u32[]{:S(2)}, u32[]{:S(2)}) collective-permute-start(bf16[128,512]{1,0:T(8,128)(2,1)S(1)} %multiply_convert_fusion.refs_0_), channel_id=1, source_target_pairs={{0,2},{1,3},{2,0},{3,1},{4,6},{5,7},{6,4},{7,5},{8,10},{9,11},{10,... | collective-permute-start | bytes 393224 | tf_op jit(solution)/shard_map/ppermute | solution.py:231
  6.3 1.6 %collective-permute-start.2 = (bf16[128,512]{1,0:T(8,128)(2,1)S(1)}, bf16[128,512]{1,0:T(8,128)(2,1)S(1)}, u32[]{:S(2)}, u32[]{:S(2)}) collective-permute-start(bf16[128,512]{1,0:T(8,128)(2,1)S(1)} %multiply_convert_fusion.refs_0_), channel_id=1, source_target_pairs={{0,4},{1,5},{2,6},{3,7},{4,0},{5,1},{6,2},{7,3},{8,12},{9,13},{10,... | collective-permute-start | bytes 393224 | tf_op jit(solution)/shard_map/ppermute | solution.py:231
  7.8 2.6 %collective-permute-start.3 = (bf16[128,512]{1,0:T(8,128)(2,1)S(1)}, bf16[128,512]{1,0:T(8,128)(2,1)S(1)}, u32[]{:S(2)}, u32[]{:S(2)}) collective-permute-start(bf16[128,512]{1,0:T(8,128)(2,1)S(1)} %multiply_convert_fusion.refs_0_), channel_id=1, source_target_pairs={{0,8},{1,9},{2,10},{3,11},{4,12},{5,13},{6,14},{7,15},{8,0},{9,1},... | collective-permute-start | bytes 393224 | tf_op jit(solution)/shard_map/ppermute | solution.py:231
  10.4 0.0 collective-permute-start
  10.4 0.0 copy-done
  10.4 1.1 %copy.16 = bf16[2560,128]{1,0:T(8,128)(2,1)} copy(bf16[2560,128]{0,1:T(8,128)(2,1)S(1)} %bitcast.28) | data formatting | bytes 1310720 | tf_op jit(solution)/shard_map/transpose | solution.py:244
  11.5 3.6 %all-to-all-start = ((bf16[16,160,128]{2,1,0:T(8,128)(2,1)}), bf16[16,160,128]{2,1,0:T(8,128)(2,1)S(1)}, u32[]{:S(2)}, u32[]{:S(2)}) async-start(bf16[16,160,128]{2,1,0:T(8,128)(2,1)} %bitcast.7), calls=%async_computation | async-start | bytes 1310720 | tf_op jit(solution)/shard_map/pooled_exchange/all_to_all | solution.py:246
  15.1 0.0 copy-done.5
  15.1 0.0 copy-done.6
  15.1 0.6 %fusion = (s32[]{:T(128)}, s32[]{:T(128)}) fusion(s32[1,16]{1,0:T(1,128)S(1)} %copy-done.5, s32[]{:T(128)} %axis_index.12, s32[1,16]{1,0:T(1,128)S(1)} %copy-done.6), kind=kLoop, calls=%fused_computation.10 | loop fusion | flops 94 | bytes 140 | tf_op jit(solution)/shard_map/reduce_sum | solution.py:220
  18.4 1.3 %stack.20.idx_ref = s32[5]{0:T(128)} concatenate(s32[1]{0:T(128)} %bitcast, s32[1]{0:T(128)} %bitcast, s32[1]{0:T(128)} %bitcast.2, s32[1]{0:T(128)} %bitcast.4, s32[1]{0:T(128)} %bitcast.5), dimensions={0} | concatenate | bytes 40 | tf_op jit(solution)/shard_map/stack | solution.py:222
  19.7 0.0 collective-permute-done.1
  19.7 0.0 collective-permute-done.2
  19.7 0.0 collective-permute-done.3
  19.8 0.0 copy-start.3
  19.8 0.5 collective-permute-start.4
  20.3 1.6 %collective-permute-start.5 = (bf16[256,512]{1,0:T(8,128)(2,1)S(1)}, bf16[256,512]{1,0:T(8,128)(2,1)S(1)}, u32[]{:S(2)}, u32[]{:S(2)}) collective-permute-start(bf16[256,512]{1,0:T(8,128)(2,1)S(1)} %pad_maximum_fusion), channel_id=1, source_target_pairs={{0,2},{1,3},{2,0},{3,1},{4,6},{5,7},{6,4},{7,5},{8,10},{9,11},{10,... | collective-permute-start | bytes 786440 | tf_op jit(solution)/shard_map/second/ppermute | solution.py:231
  21.8 1.5 %collective-permute-start.9 = (bf16[128,512]{1,0:T(8,128)(2,1)S(1)}, bf16[128,512]{1,0:T(8,128)(2,1)S(1)}, u32[]{:S(2)}, u32[]{:S(2)}) collective-permute-start(bf16[128,512]{1,0:T(8,128)(2,1)S(1)} %collective-permute-done.3), channel_id=1, source_target_pairs={{0,6},{1,7},{2,4},{3,5},{4,2},{5,3},{6,0},{7,1},{8,14},{9,15},{10,... | collective-permute-start | bytes 393224 | tf_op jit(solution)/shard_map/second/ppermute | solution.py:231
  23.3 0.5 collective-permute-start.7
  23.8 0.0 copy-start.4
  23.8 4.3 %hit_words.1 = (s32[128,1024]{1,0:T(8,128)}, s32[128,1024]{1,0:T(8,128)}, s32[128,1024]{1,0:T(8,128)}, s32[128,1024]{1,0:T(8,128)}) custom-call(s32[5]{0:T(128)} %stack.20.idx_ref, s32[8,2048]{1,0:T(8,128)} %bitcast.33, s32[4,8,2048]{2,1,0:T(8,128)} %bitcast.31), custom_call_target="tpu_custom_call" | custom-call | flops 4000000000 | bytes 2000000 | tf_op jit(solution)/shard_map/hit_words/pallas_call | solution.py:61
  28.1 0.0 copy-done.10
  28.1 0.0 copy-done.3
  28.1 0.0 copy-done.4
  28.1 0.6 %broadcast_in_dim_squeeze.3.refs_15_ = f32[4,1,1024]{2,1,0:T(1,128)} reshape(f32[1,4,1024]{2,1,0:T(4,128)S(1)} %copy-done.4) | data formatting | bytes 32768 | tf_op jit(solution)/shard_map/broadcast_in_dim;squeeze | solution.py:332
  28.7 3.7 %collective-permute-done.9.refs_8_.refs_4_ = bf16[128,512]{1,0:T(8,128)(2,1)S(1)} collective-permute-done((bf16[128,512]{1,0:T(8,128)(2,1)S(1)}, bf16[128,512]{1,0:T(8,128)(2,1)S(1)}, u32[]{:S(2)}, u32[]{:S(2)}) %collective-permute-start.9) | collective-permute-done | bytes 131104 | tf_op jit(solution)/shard_map/second/ppermute | solution.py:231
  32.4 0.0 copy-start.12
  32.4 0.0 collective-permute-start.10
  32.4 1.8 %collective-permute-done.7.refs_6_.refs_2_ = bf16[128,512]{1,0:T(8,128)(2,1)S(1)} collective-permute-done((bf16[128,512]{1,0:T(8,128)(2,1)S(1)}, bf16[128,512]{1,0:T(8,128)(2,1)S(1)}, u32[]{:S(2)}, u32[]{:S(2)}) %collective-permute-start.7) | collective-permute-done | bytes 131104 | tf_op jit(solution)/shard_map/second/ppermute | solution.py:231
  34.3 0.0 collective-permute-start.8
  34.3 0.5 collective-permute-done.5.refs_4_.refs_0_
  34.8 0.0 collective-permute-start.6
  34.8 0.0 collective-permute-done.refs_1_
  34.8 0.0 copy-start.11
  34.8 0.0 collective-permute-done.4.refs_3_
  34.8 0.0 copy-start.7
  34.8 0.7 %copy-done.11 = bf16[128,512]{1,0:T(8,128)(2,1)} copy-done((bf16[128,512]{1,0:T(8,128)(2,1)}, bf16[128,512]{1,0:T(8,128)(2,1)S(1)}, u32[]{:S(2)}) %copy-start.11) | copy-done | bytes 131096
  35.5 0.1 copy-done.7
  35.7 5.2 %early_gradients.1 = (f32[128,1024]{1,0:T(8,128)}, f32[128,1024]{1,0:T(8,128)}) custom-call(s32[5]{0:T(128)} %stack.20.idx_ref, bf16[128,512]{1,0:T(8,128)(2,1)} %copy-done.10, bf16[128,512]{1,0:T(8,128)(2,1)} %copy-done.11, bf16[384,512]{1,0:T(8,128)(2,1)} %copy-done.3, bf16[384,512]{1,0:T(8,128)(2,1)} %copy-done.7, bf16[2560,512]{1,0:T(8,128)(2,1)} %refs_7_.1, ...), custom_call_target="tpu_custom_call" | custom-call | flops 4000000000 | bytes 4000000 | tf_op jit(solution)/shard_map/early_gradients/pallas_call | solution.py:148
  40.9 0.0 collective-permute-done.10.refs_9_.refs_5_
  40.9 0.0 collective-permute-done.8.refs_7_.refs_3_
  40.9 0.0 copy-start.15
  40.9 0.0 collective-permute-done.6.refs_5_.refs_1_
  40.9 0.0 copy-start.9
  40.9 0.0 all-to-all-done.refs_10_
  41.0 0.0 copy-done.12
  41.0 0.0 copy-done.13
  41.0 0.0 copy-done.8
  41.0 0.6 %copy-done.14 = bf16[128,512]{1,0:T(8,128)(2,1)} copy-done((bf16[128,512]{1,0:T(8,128)(2,1)}, bf16[128,512]{1,0:T(8,128)(2,1)S(1)}, u32[]{:S(2)}) %copy-start.14) | copy-done | bytes 131096
  41.6 0.0 copy-done.15
  41.6 0.1 copy-done.9
  41.7 0.8 %copy-done.1 = bf16[16,160,128]{2,1,0:T(8,128)(2,1)} copy-done((bf16[16,160,128]{2,1,0:T(8,128)(2,1)}, bf16[16,160,128]{2,1,0:T(8,128)(2,1)S(1)}, u32[]{:S(2)}) %copy-start.1) | copy-done | bytes 655384
  42.6 3.3 %block_gradient.1 = bf16[176,512]{1,0:T(8,128)(2,1)} custom-call(s32[5]{0:T(128)} %stack.20.idx_ref, bf16[128,512]{1,0:T(8,128)(2,1)} %copy-done.10, bf16[128,512]{1,0:T(8,128)(2,1)} %copy-done.11, bf16[384,512]{1,0:T(8,128)(2,1)} %copy-done.3, bf16[384,512]{1,0:T(8,128)(2,1)} %copy-done.7, bf16[256,512]{1,0:T(8,128)(2,1)} %copy-done.8, ...), custom_call_target="tpu_custom_call" | custom-call | flops 1000000000 | bytes 3000000 | tf_op jit(solution)/shard_map/block_gradient/pallas_call | solution.py:191
  45.8 1.5 %collective-permute-start.11 = (bf16[176,512]{1,0:T(8,128)(2,1)}, bf16[176,512]{1,0:T(8,128)(2,1)S(1)}, u32[]{:S(2)}, u32[]{:S(2)}) collective-permute-start(bf16[176,512]{1,0:T(8,128)(2,1)} %block_gradient.1), channel_id=1, source_target_pairs={{0,16},{1,17},{2,18},{3,19},{4,20},{5,21},{6,22},{7,23},{8,24},{9,... | collective-permute-start | bytes 540680 | tf_op jit(solution)/shard_map/groups/ppermute | solution.py:231
  47.4 5.8 %late_gradients.1 = (f32[128,1024]{1,0:T(8,128)}, f32[32,1024]{1,0:T(8,128)}) custom-call(s32[5]{0:T(128)} %stack.20.idx_ref, bf16[256,512]{1,0:T(8,128)(2,1)} %copy-done.8, bf16[256,512]{1,0:T(8,128)(2,1)} %copy-done.9, bf16[128,512]{1,0:T(8,128)(2,1)} %copy-done.13, bf16[128,512]{1,0:T(8,128)(2,1)} %copy-done.15, bf16[128,512]{1,0:T(8,128)(2,1)} %copy-done.12, ...), custom_call_target="tpu_custom_call" | custom-call | flops 4000000000 | bytes 4000000 | tf_op jit(solution)/shard_map/late_gradients/pallas_call | solution.py:148
  53.2 0.0 collective-permute-done.11
  53.2 0.0 copy-done.2
  53.3 0.7 %slice.12 = f32[160,512]{1,0:T(8,128)} slice(f32[176,512]{1,0:T(8,128)S(1)} %convert_add_fusion), slice={[0:160], [0:512]} | slice | bytes 655360 | tf_op jit(solution)/shard_map/slice | solution.py:314
  54.0 0.6 %slice_add_fusion = f32[1,512]{1,0:T(1,128)} fusion(f32[176,512]{1,0:T(8,128)S(1)} %convert_add_fusion), kind=kLoop, calls=%fused_computation.7 | loop fusion | flops 512 | bytes 6144 | tf_op jit(solution)/shard_map/add | solution.py:315
  (10 shorter events, 0.1 us)
Async XLA Ops:
  0.6 9.8 %copy-start = (bf16[128,2560]{1,0:T(8,128)(2,1)S(1)}, bf16[128,2560]{1,0:T(8,128)(2,1)}, u32[]{:S(2)}) copy-start(bf16[128,2560]{1,0:T(8,128)(2,1)} %param.12) | copy-start | bytes 1966084
  0.6 14.5 %copy-start.5 = (s32[1,16]{1,0:T(1,128)S(1)}, s32[1,16]{1,0:T(1,128)}, u32[]{:S(2)}) copy-start(s32[1,16]{1,0:T(1,128)} %param.16) | copy-start | bytes 196
  0.7 14.5 %copy-start.6 = (s32[1,16]{1,0:T(1,128)S(1)}, s32[1,16]{1,0:T(1,128)}, u32[]{:S(2)}) copy-start(s32[1,16]{1,0:T(1,128)} %param.17) | copy-start | bytes 196
  3.2 24.9 %copy-start.10 = (bf16[128,512]{1,0:T(8,128)(2,1)}, bf16[128,512]{1,0:T(8,128)(2,1)S(1)}, u32[]{:S(2)}) copy-start(bf16[128,512]{1,0:T(8,128)(2,1)S(1)} %multiply_convert_fusion.refs_0_) | copy-start | bytes 393220
  3.2 16.5 %collective-permute-start.1 = (bf16[128,512]{1,0:T(8,128)(2,1)S(1)}, bf16[128,512]{1,0:T(8,128)(2,1)S(1)}, u32[]{:S(2)}, u32[]{:S(2)}) collective-permute-start(bf16[128,512]{1,0:T(8,128)(2,1)S(1)} %multiply_convert_fusion.refs_0_), channel_id=1, source_target_pairs={{0,2},{1,3},{2,0},{3,1},{4,6},{5,7},{6,4},{7,5},{8,10},{9,11},{10,... | collective-permute-start | bytes 393224 | tf_op jit(solution)/shard_map/ppermute | solution.py:231
  6.3 13.4 %collective-permute-start.2 = (bf16[128,512]{1,0:T(8,128)(2,1)S(1)}, bf16[128,512]{1,0:T(8,128)(2,1)S(1)}, u32[]{:S(2)}, u32[]{:S(2)}) collective-permute-start(bf16[128,512]{1,0:T(8,128)(2,1)S(1)} %multiply_convert_fusion.refs_0_), channel_id=1, source_target_pairs={{0,4},{1,5},{2,6},{3,7},{4,0},{5,1},{6,2},{7,3},{8,12},{9,13},{10,... | collective-permute-start | bytes 393224 | tf_op jit(solution)/shard_map/ppermute | solution.py:231
  7.8 11.9 %collective-permute-start.3 = (bf16[128,512]{1,0:T(8,128)(2,1)S(1)}, bf16[128,512]{1,0:T(8,128)(2,1)S(1)}, u32[]{:S(2)}, u32[]{:S(2)}) collective-permute-start(bf16[128,512]{1,0:T(8,128)(2,1)S(1)} %multiply_convert_fusion.refs_0_), channel_id=1, source_target_pairs={{0,8},{1,9},{2,10},{3,11},{4,12},{5,13},{6,14},{7,15},{8,0},{9,1},... | collective-permute-start | bytes 393224 | tf_op jit(solution)/shard_map/ppermute | solution.py:231
  10.4 24.4 %collective-permute-start = (bf16[128,512]{1,0:T(8,128)(2,1)S(1)}, bf16[128,512]{1,0:T(8,128)(2,1)S(1)}, u32[]{:S(2)}, u32[]{:S(2)}) collective-permute-start(bf16[128,512]{1,0:T(8,128)(2,1)S(1)} %multiply_convert_fusion.refs_0_), channel_id=1, source_target_pairs={{0,1},{1,0},{2,3},{3,2},{4,5},{5,4},{6,7},{7,6},{8,9},{9,8},{10,11... | collective-permute-start | bytes 393224 | tf_op jit(solution)/shard_map/cross0/ppermute | solution.py:231
  11.5 29.4 %all-to-all-start = ((bf16[16,160,128]{2,1,0:T(8,128)(2,1)}), bf16[16,160,128]{2,1,0:T(8,128)(2,1)S(1)}, u32[]{:S(2)}, u32[]{:S(2)}) async-start(bf16[16,160,128]{2,1,0:T(8,128)(2,1)} %bitcast.7), calls=%async_computation | async-start | bytes 1310720 | tf_op jit(solution)/shard_map/pooled_exchange/all_to_all | solution.py:246
  19.8 8.4 %copy-start.3 = (bf16[384,512]{1,0:T(8,128)(2,1)}, bf16[384,512]{1,0:T(8,128)(2,1)S(1)}, u32[]{:S(2)}) copy-start(bf16[384,512]{1,0:T(8,128)(2,1)S(1)} %constant_dynamic-update-slice_fusion.refs_2_) | copy-start | bytes 1179652
  19.8 15.1 %collective-permute-start.4 = (bf16[384,512]{1,0:T(8,128)(2,1)S(1)}, bf16[384,512]{1,0:T(8,128)(2,1)S(1)}, u32[]{:S(2)}, u32[]{:S(2)}) collective-permute-start(bf16[384,512]{1,0:T(8,128)(2,1)S(1)} %constant_dynamic-update-slice_fusion.refs_2_), channel_id=1, source_target_pairs={{0,1},{1,0},{2,3},{3,2},{4,5},{5,4},{6,7},{7,6},{8,9},{9,8},{10,11... | collective-permute-start | bytes 1179656 | tf_op jit(solution)/shard_map/cross1/ppermute | solution.py:231
  20.3 14.5 %collective-permute-start.5 = (bf16[256,512]{1,0:T(8,128)(2,1)S(1)}, bf16[256,512]{1,0:T(8,128)(2,1)S(1)}, u32[]{:S(2)}, u32[]{:S(2)}) collective-permute-start(bf16[256,512]{1,0:T(8,128)(2,1)S(1)} %pad_maximum_fusion), channel_id=1, source_target_pairs={{0,2},{1,3},{2,0},{3,1},{4,6},{5,7},{6,4},{7,5},{8,10},{9,11},{10,... | collective-permute-start | bytes 786440 | tf_op jit(solution)/shard_map/second/ppermute | solution.py:231
  21.8 10.6 %collective-permute-start.9 = (bf16[128,512]{1,0:T(8,128)(2,1)S(1)}, bf16[128,512]{1,0:T(8,128)(2,1)S(1)}, u32[]{:S(2)}, u32[]{:S(2)}) collective-permute-start(bf16[128,512]{1,0:T(8,128)(2,1)S(1)} %collective-permute-done.3), channel_id=1, source_target_pairs={{0,6},{1,7},{2,4},{3,5},{4,2},{5,3},{6,0},{7,1},{8,14},{9,15},{10,... | collective-permute-start | bytes 393224 | tf_op jit(solution)/shard_map/second/ppermute | solution.py:231
  23.3 10.9 %collective-permute-start.7 = (bf16[128,512]{1,0:T(8,128)(2,1)S(1)}, bf16[128,512]{1,0:T(8,128)(2,1)S(1)}, u32[]{:S(2)}, u32[]{:S(2)}) collective-permute-start(bf16[128,512]{1,0:T(8,128)(2,1)S(1)} %collective-permute-done.3), channel_id=1, source_target_pairs={{0,4},{1,5},{2,6},{3,7},{4,0},{5,1},{6,2},{7,3},{8,12},{9,13},{10,... | collective-permute-start | bytes 393224 | tf_op jit(solution)/shard_map/second/ppermute | solution.py:231
  23.8 4.3 %copy-start.4 = (f32[1,4,1024]{2,1,0:T(4,128)S(1)}, f32[1,4,1024]{2,1,0:T(4,128)}, u32[]{:S(2)}) copy-start(f32[1,4,1024]{2,1,0:T(4,128)} %param.23) | copy-start | bytes 49156
  32.4 8.5 %copy-start.12 = (bf16[128,512]{1,0:T(8,128)(2,1)}, bf16[128,512]{1,0:T(8,128)(2,1)S(1)}, u32[]{:S(2)}) copy-start(bf16[128,512]{1,0:T(8,128)(2,1)S(1)} %collective-permute-done.9.refs_8_.refs_4_) | copy-start | bytes 393220
  32.4 8.5 %collective-permute-start.10 = (bf16[128,512]{1,0:T(8,128)(2,1)S(1)}, bf16[128,512]{1,0:T(8,128)(2,1)S(1)}, u32[]{:S(2)}, u32[]{:S(2)}) collective-permute-start(bf16[128,512]{1,0:T(8,128)(2,1)S(1)} %collective-permute-done.9.refs_8_.refs_4_), channel_id=1, source_target_pairs={{0,1},{1,0},{2,3},{3,2},{4,5},{5,4},{6,7},{7,6},{8,9},{9,8},{10,11... | collective-permute-start | bytes 393224 | tf_op jit(solution)/shard_map/cross2/ppermute | solution.py:231
  34.3 6.7 %copy-start.13 = (bf16[128,512]{1,0:T(8,128)(2,1)}, bf16[128,512]{1,0:T(8,128)(2,1)S(1)}, u32[]{:S(2)}) copy-start(bf16[128,512]{1,0:T(8,128)(2,1)S(1)} %collective-permute-done.7.refs_6_.refs_2_) | copy-start | bytes 393220
  34.3 6.6 %collective-permute-start.8 = (bf16[128,512]{1,0:T(8,128)(2,1)S(1)}, bf16[128,512]{1,0:T(8,128)(2,1)S(1)}, u32[]{:S(2)}, u32[]{:S(2)}) collective-permute-start(bf16[128,512]{1,0:T(8,128)(2,1)S(1)} %collective-permute-done.7.refs_6_.refs_2_), channel_id=1, source_target_pairs={{0,1},{1,0},{2,3},{3,2},{4,5},{5,4},{6,7},{7,6},{8,9},{9,8},{10,11... | collective-permute-start | bytes 393224 | tf_op jit(solution)/shard_map/cross2/ppermute | solution.py:231
  34.8 6.2 %copy-start.8 = (bf16[256,512]{1,0:T(8,128)(2,1)}, bf16[256,512]{1,0:T(8,128)(2,1)S(1)}, u32[]{:S(2)}) copy-start(bf16[256,512]{1,0:T(8,128)(2,1)S(1)} %collective-permute-done.5.refs_4_.refs_0_) | copy-start | bytes 786436
  34.8 6.1 %collective-permute-start.6 = (bf16[256,512]{1,0:T(8,128)(2,1)S(1)}, bf16[256,512]{1,0:T(8,128)(2,1)S(1)}, u32[]{:S(2)}, u32[]{:S(2)}) collective-permute-start(bf16[256,512]{1,0:T(8,128)(2,1)S(1)} %collective-permute-done.5.refs_4_.refs_0_), channel_id=1, source_target_pairs={{0,1},{1,0},{2,3},{3,2},{4,5},{5,4},{6,7},{7,6},{8,9},{9,8},{10,11... | collective-permute-start | bytes 786440 | tf_op jit(solution)/shard_map/cross2/ppermute | solution.py:231
  34.8 0.7 %copy-start.11 = (bf16[128,512]{1,0:T(8,128)(2,1)}, bf16[128,512]{1,0:T(8,128)(2,1)S(1)}, u32[]{:S(2)}) copy-start(bf16[128,512]{1,0:T(8,128)(2,1)S(1)} %collective-permute-done.refs_1_) | copy-start | bytes 393220
  34.8 0.8 %copy-start.7 = (bf16[384,512]{1,0:T(8,128)(2,1)}, bf16[384,512]{1,0:T(8,128)(2,1)S(1)}, u32[]{:S(2)}) copy-start(bf16[384,512]{1,0:T(8,128)(2,1)S(1)} %collective-permute-done.4.refs_3_) | copy-start | bytes 1179652
  40.9 0.7 %copy-start.14 = (bf16[128,512]{1,0:T(8,128)(2,1)}, bf16[128,512]{1,0:T(8,128)(2,1)S(1)}, u32[]{:S(2)}) copy-start(bf16[128,512]{1,0:T(8,128)(2,1)S(1)} %collective-permute-done.10.refs_9_.refs_5_) | copy-start | bytes 393220
  40.9 0.7 %copy-start.15 = (bf16[128,512]{1,0:T(8,128)(2,1)}, bf16[128,512]{1,0:T(8,128)(2,1)S(1)}, u32[]{:S(2)}) copy-start(bf16[128,512]{1,0:T(8,128)(2,1)S(1)} %collective-permute-done.8.refs_7_.refs_3_) | copy-start | bytes 393220
  40.9 0.8 %copy-start.9 = (bf16[256,512]{1,0:T(8,128)(2,1)}, bf16[256,512]{1,0:T(8,128)(2,1)S(1)}, u32[]{:S(2)}) copy-start(bf16[256,512]{1,0:T(8,128)(2,1)S(1)} %collective-permute-done.6.refs_5_.refs_1_) | copy-start | bytes 786436
  41.7 0.8 %copy-start.1 = (bf16[16,160,128]{2,1,0:T(8,128)(2,1)}, bf16[16,160,128]{2,1,0:T(8,128)(2,1)S(1)}, u32[]{:S(2)}) copy-start(bf16[16,160,128]{2,1,0:T(8,128)(2,1)S(1)} %all-to-all-done.refs_10_) | copy-start | bytes 1966084
  45.8 7.4 %collective-permute-start.11 = (bf16[176,512]{1,0:T(8,128)(2,1)}, bf16[176,512]{1,0:T(8,128)(2,1)S(1)}, u32[]{:S(2)}, u32[]{:S(2)}) collective-permute-start(bf16[176,512]{1,0:T(8,128)(2,1)} %block_gradient.1), channel_id=1, source_target_pairs={{0,16},{1,17},{2,18},{3,19},{4,20},{5,21},{6,22},{7,23},{8,24},{9,... | collective-permute-start | bytes 540680 | tf_op jit(solution)/shard_map/groups/ppermute | solution.py:231
  47.4 5.8 %copy-start.2 = (bf16[176,512]{1,0:T(8,128)(2,1)S(1)}, bf16[176,512]{1,0:T(8,128)(2,1)}, u32[]{:S(2)}) copy-start(bf16[176,512]{1,0:T(8,128)(2,1)} %block_gradient.1) | copy-start | bytes 540676

commit v3 on v2

v3 whole, which is shorter than its diff:
```python
import functools

import jax
import jax.numpy as jnp
from jax import lax
from jax.experimental import pallas as pl
from jax.experimental.pallas import tpu as pltpu
from jax.sharding import PartitionSpec as P


E = 128
CS = 4
LEARN_RATE = 0.5
EPSILON = 1e-08
VMEM_BYTES = 16 * 1024 * 1024
LATE_VMEM_BYTES = 61 * 1024 * 1024
BF16 = jnp.bfloat16
F32 = jnp.float32

NT_DIMS = (((1,), (1,)), ((), ()))
NN_DIMS = (((1,), (0,)), ((), ()))


def dot_nt(lhs, rhs):
    return lax.dot_general(lhs, rhs, NT_DIMS, preferred_element_type=F32)


def owned(owner_ref):
    place = lax.axis_index("mem")
    found = jnp.int32(0)
    for item in range(owner_ref.shape[1]):
        found = jnp.where(owner_ref[0, item] == place, item, found)
    return found


def owned_split(owner_ref):
    return lax.div(owned(owner_ref), CS)


def dot_nn(lhs, rhs):
    return lax.dot_general(lhs, rhs, NN_DIMS, preferred_element_type=F32)


def word_kernel(bits, turns, owner_ref, shard_ref, whole_ref, split_ref, *outs):
    position = lax.axis_index("mem")
    samples = outs[0].shape[1] // len(turns[0])
    for keys_ref, table in ((whole_ref, 0), (split_ref, 1)):
        pool = keys_ref.shape[0]
        for stage, order in enumerate(turns):
            out = outs[2 * stage + table]
            low_rows = out.shape[0]
            shift = low_rows.bit_length() - 1
            spots = lax.broadcasted_iota(jnp.int32, (low_rows, samples), 0)
            for spot, turn in enumerate(order):
                lane = pl.multiple_of(jnp.bitwise_xor(position, turn) * samples, samples)
                keys = keys_ref[:, pl.ds(lane, samples)]
                low = jnp.bitwise_and(keys, low_rows - 1)
                field = lax.shift_right_logical(keys, jnp.full_like(keys, shift))
                unit = lax.shift_left(jnp.ones_like(keys), field * bits)
                words = jnp.zeros((low_rows, samples), jnp.int32)
                for place in range(pool):
                    row = slice(place, place + 1)
                    words = words + jnp.where(spots == low[row, :], unit[row, :], 0)
                out[:, spot * samples : (spot + 1) * samples] = words


def hit_words(owners_of, keys_whole, keys_split, rows_whole, rows_split, samples, turns):
    pool, total = keys_whole.shape
    bits = pool.bit_length()
    fields = 32 // bits
    whole = lambda i, tables, shards: (0, 0)
    shapes = [
        jax.ShapeDtypeStruct((rows // fields, len(order) * samples), jnp.int32)
        for order in turns
        for rows in (rows_whole, rows_split)
    ]
    return pl.pallas_call(
        functools.partial(word_kernel, bits, turns),
        out_shape=shapes,
        grid_spec=pltpu.PrefetchScalarGridSpec(
            num_scalar_prefetch=2,
            grid=(1,),
            in_specs=[
                pl.BlockSpec((pool, total), whole),
                pl.BlockSpec(
                    (None, pool, total), lambda i, tables, shards: (owned_split(shards), 0, 0)
                ),
            ],
            out_specs=[pl.BlockSpec(shape.shape, whole) for shape in shapes],
        ),
        compiler_params=pltpu.CompilerParams(vmem_limit_bytes=VMEM_BYTES),
        cost_estimate=pl.CostEstimate(flops=4_000_000_000, bytes_accessed=2_000_000, transcendentals=0),
        name="hit_words",
    )(*owners_of, keys_whole, keys_split)


def slot_gradients(bits, refs, w_whole, w_split, words_whole, words_split, back, hits, take, ready=None):
    spot = 0
    for ref in refs:
        rows = ref.shape[0]
        lanes = slice(spot, spot + rows)
        back[:E, lanes] = dot_nt(w_whole[...], ref[...]).astype(BF16)
        back[E:, lanes] = dot_nt(w_split[...], ref[...]).astype(BF16)
        spot += rows
    fields = 32 // bits
    for table, words in enumerate((words_whole, words_split)):
        if ready is not None:
            ready(table)
        low = words.shape[0]
        for field in range(fields):
            packed = words[...]
            count = lax.shift_right_logical(packed, jnp.full_like(packed, field * bits))
            count = jnp.bitwise_and(count, (1 << bits) - 1)
            hits[field * low : (field + 1) * low, :] = count.astype(F32).astype(BF16)
        for first in range(0, fields * low, 2 * low):
            rows = slice(first, first + 2 * low)
            take(table, rows, dot_nt(back[table * E : (table + 1) * E, :], hits[rows, :]))


def early_kernel(bits, count, owner_ref, shard_ref, *refs):
    arrays, rest = refs[:count], refs[count:]
    w_whole, w_split, words_whole, words_split, out_whole, out_split, back, hits = rest
    outs = (out_whole, out_split)

    def take(table, rows, grad):
        outs[table][:, rows] = grad

    slot_gradients(bits, arrays, w_whole, w_split, words_whole, words_split, back, hits, take)


def late_kernel(bits, tables, count, owner_ref, shard_ref, *refs):
    (w_first, words_whole, words_split, sum_whole, sum_split, table_whole, accum_whole,
     table_split, accum_split, new_whole, new_split) = refs[count : count + 11]
    local = list(refs[count + 11 :])
    deltas, local = local[:count], local[count:]
    (back, hits, grads, weights, words, words2, sums, sums2, table, table2, accum, accum2,
     out, out2, sems) = local
    columns = table2.shape[0]
    shard = owned(shard_ref)
    first = pl.multiple_of(lax.rem(shard, CS) * columns, columns)
    split = lax.div(shard, CS)
    spots = (slice(0, 1), pl.ds(split, 1))
    blocks = (owned(owner_ref), tables + split)
    moves = [
        (w_first.at[pl.ds(pl.multiple_of(block * E, E), E), :], weights.at[pl.ds(i * E, E), :])
        for i, block in enumerate(blocks)
    ]
    moves += list(zip(refs[:count], deltas))
    heads = len(moves)
    moves += [(words_whole, words), (sum_whole, sums), (accum_whole, accum), (table_whole, table)]
    moves += [(words_split, words2), (sum_split, sums2), (accum_split, accum2), (table_split, table2)]
    loads = [pltpu.make_async_copy(a, b, sems.at[i]) for i, (a, b) in enumerate(moves)]
    stores = [
        pltpu.make_async_copy(out, new_whole, sems.at[len(moves)]),
        pltpu.make_async_copy(out2, new_split, sems.at[len(moves) + 1]),
    ]
    for load in loads:
        load.start()
    for load in loads[:heads]:
        load.wait()

    def ready(at):
        for load in loads[heads + 4 * at : heads + 4 * at + 4]:
            load.wait()

    def take(at, rows, grad):
        grad = grad + (sums, sums2)[at][:, rows]
        squares = jnp.sum(grad * grad, axis=0, keepdims=True)
        state = (accum, accum2)[at][spots[at], rows] + squares / E
        scale = LEARN_RATE / (jnp.sqrt(state) + EPSILON)
        if at == 0:
            out[:, rows] = table[:, rows] - grad * scale
        else:
            grads[...] = grad
            own = grads[pl.ds(first, columns), :]
            out2[:, rows] = table2[:, rows] - own * scale
        if rows.stop == (out, out2)[at].shape[1]:
            stores[at].start()

    w_parts = (weights.at[pl.ds(0, E), :], weights.at[pl.ds(E, E), :])
    slot_gradients(bits, deltas, *w_parts, words, words2, back, hits, take, ready)
    for store in stores:
        store.wait()


def late_call(owners_of, arrays, w_first, words, sums, tables, bits, extra, out_shape):
    low, total = words[0].shape
    rows = low * (32 // bits)
    hbm = pl.BlockSpec(memory_space=pltpu.HBM)
    operands = [*arrays, w_first, *words, *sums, *extra]
    like = lambda array: pltpu.VMEM(array.shape, array.dtype)
    scratch = [like(array) for array in arrays]
    scratch += [
        pltpu.VMEM((2 * E, total), BF16),
        pltpu.VMEM((rows, total), BF16),
        pltpu.VMEM((E, 2 * low), F32),
        pltpu.VMEM((2 * E, w_first.shape[1]), BF16),
    ]
    scratch += [like(array) for array in (*words, *sums, extra[0], extra[2], extra[1], extra[3])]
    scratch += [pltpu.VMEM(shape.shape, F32) for shape in out_shape]
    scratch += [pltpu.SemaphoreType.DMA((len(arrays) + 12,))]
    return pl.pallas_call(
        functools.partial(late_kernel, bits, tables, len(arrays)),
        out_shape=out_shape,
        grid_spec=pltpu.PrefetchScalarGridSpec(
            num_scalar_prefetch=2,
            grid=(1,),
            in_specs=[hbm] * len(operands),
            out_specs=[hbm] * 2,
            scratch_shapes=scratch,
        ),
        compiler_params=pltpu.CompilerParams(vmem_limit_bytes=LATE_VMEM_BYTES),
        cost_estimate=pl.CostEstimate(flops=4_000_000_000, bytes_accessed=4_000_000, transcendentals=0),
        name="late_gradients",
    )(*owners_of, *operands)


def slot_call(kernel, owners_of, arrays, w_first, words, whole_tables, bits, extra, out_shape, more):
    hidden = w_first.shape[1]
    fixed = lambda i, tables, shards: (0, 0)
    specs = [pl.BlockSpec(array.shape, fixed) for array in arrays]
    specs += [
        pl.BlockSpec((E, hidden), lambda i, tables, shards: (owned(tables), 0)),
        pl.BlockSpec(
            (E, hidden), lambda i, tables, shards: (whole_tables + owned_split(shards), 0)
        ),
    ]
    specs += [pl.BlockSpec(word.shape, fixed) for word in words]
    specs += [pl.BlockSpec(array.shape, fixed) for array in extra]
    low, total = words[0].shape
    rows = low * (32 // bits)
    return pl.pallas_call(
        functools.partial(kernel, bits, len(arrays)),
        out_shape=out_shape,
        grid_spec=pltpu.PrefetchScalarGridSpec(
            num_scalar_prefetch=2,
            grid=(1,),
            in_specs=specs,
            out_specs=[pl.BlockSpec(shape.shape, fixed) for shape in out_shape],
            scratch_shapes=[pltpu.VMEM((2 * E, total), BF16), pltpu.VMEM((rows, total), BF16)]
            + more(low),
        ),
        compiler_params=pltpu.CompilerParams(vmem_limit_bytes=VMEM_BYTES),
        cost_estimate=pl.CostEstimate(flops=4_000_000_000, bytes_accessed=4_000_000, transcendentals=0),
    )(*owners_of, *arrays, w_first, w_first, *words, *extra)


def block_kernel(places, count, *refs):
    position = lax.axis_index("mem")
    arrays, pooled, out, acc = refs[:count], refs[count], refs[count + 1], refs[count + 2]
    samples = pooled.shape[2]
    sums = []
    for turn, (array, row) in enumerate(places):
        rows = arrays[array][row : row + samples, :]
        piece = dot_nn(pooled[jnp.bitwise_xor(position, turn)], rows)
        if turn == 0:
            acc[...] = piece
        else:
            acc[...] += piece
        sums.append(jnp.sum(rows.astype(F32), axis=0, keepdims=True))
    while len(sums) > 1:
        sums = [a + b for a, b in zip(sums[0::2], sums[1::2])]
    high = sums[0].astype(BF16)
    low = (sums[0] - high.astype(F32)).astype(BF16)
    block = acc.shape[0]
    out[:block, :] = acc[...].astype(BF16)
    place = lax.broadcasted_iota(jnp.int32, (16, acc.shape[1]), 0)
    extra = jnp.where(place == 0, high.astype(F32), jnp.where(place == 1, low.astype(F32), 0.0))
    out[block:, :] = extra.astype(BF16)


def block_gradient(arrays, places, pooled):
    hidden = arrays[0].shape[1]
    block = pooled.shape[1]
    vmem = pl.BlockSpec(memory_space=pltpu.VMEM)
    return pl.pallas_call(
        functools.partial(block_kernel, places, len(arrays)),
        out_shape=jax.ShapeDtypeStruct((block + 16, hidden), BF16),
        in_specs=[vmem] * (len(arrays) + 1),
        out_specs=vmem,
        scratch_shapes=[pltpu.VMEM((block, hidden), F32)],
        compiler_params=pltpu.CompilerParams(vmem_limit_bytes=VMEM_BYTES),
        cost_estimate=pl.CostEstimate(flops=1_000_000_000, bytes_accessed=3_000_000, transcendentals=0),
        name="block_gradient",
    )(*arrays, pooled)


def per_device(
    groups,
    owners,
    pooled,
    grad_hidden,
    w_first,
    bias_first,
    table_owner,
    shard_owner,
    lookups_whole,
    lookups_split,
    table_whole,
    accum_whole,
    table_split,
    accum_split,
):
    owners_of = (table_owner, shard_owner)
    samples, features = pooled.shape

    def send(values, turn, side_turn=0):
        pairs = [
            (g * owners + m, (g ^ side_turn) * owners + (m ^ turn))
            for g in range(groups)
            for m in range(owners)
        ]
        return lax.ppermute(values, ("grp", "mem"), pairs)

    pre_act = jnp.dot(pooled, w_first, preferred_element_type=F32) + bias_first
    sigmoid_pre = jax.nn.sigmoid(pre_act)
    slope = sigmoid_pre * (1.0 + pre_act * (1.0 - sigmoid_pre))
    delta = (grad_hidden.astype(F32) * slope).astype(BF16)

    tops = [1 << b for b in range(1, owners.bit_length() - 1)]
    direct = [send(delta, top) for top in reversed(tops)][::-1]
    delta_crossed = send(delta, 1)

    pooled_here, _ = lax.optimization_barrier((pooled, delta))
    pooled_rows = pooled_here.T.reshape(owners, features // owners, samples)
    pooled_all = lax.all_to_all(pooled_rows, "mem", split_axis=0, concat_axis=0, tiled=True)

    arrays = [delta, delta_crossed]
    where = {0: (0, 0), 1: (1, 0)}
    joined = jnp.concatenate(direct)
    joined_crossed = send(joined, 1)
    for core, array in enumerate((joined, joined_crossed)):
        for spot, top in enumerate(tops):
            where[top + core] = (len(arrays), spot * samples)
        arrays.append(array)
    early = len(arrays)
    second = []
    for rest in range(2, owners // 2, 2):
        highs = [spot for spot, top in enumerate(tops) if top > rest]
        second.append(send(jnp.concatenate([direct[spot] for spot in highs]), rest))
        for core in range(2):
            for spot, high in enumerate(highs):
                where[tops[high] + rest + core] = (early + 2 * len(second) - 2 + core, spot * samples)
    backward = {place: turn for turn, place in where.items()}
    lengths = [array.shape[0] for array in arrays]
    for array in second:
        lengths += [array.shape[0]] * 2
    turns = tuple(
        tuple(backward[(at, row)] for at in spots for row in range(0, lengths[at], samples))
        for spots in (range(early), range(early, len(lengths)))
    )

    rows_whole = table_whole.shape[-1]
    rows_split = table_split.shape[-1]
    keys_whole = lookups_whole[0, 0].T
    bits = keys_whole.shape[0].bit_length()
    words = hit_words(
        owners_of,
        keys_whole,
        jnp.transpose(lookups_split[0], (0, 2, 1)),
        rows_whole,
        rows_split,
        samples,
        turns,
    )
    sum_whole, sum_split = slot_call(
        early_kernel,
        owners_of,
        arrays[:early],
        w_first,
        words[:2],
        owners,
        bits,
        [],
        [jax.ShapeDtypeStruct((E, rows_whole), F32), jax.ShapeDtypeStruct((E, rows_split), F32)],
        lambda low: [],
    )

    sum_whole, sum_split, *second = lax.optimization_barrier((sum_whole, sum_split, *second))
    for array in second:
        arrays += [array, send(array, 1)]

    places = tuple(where[turn] for turn in range(owners))
    partial = block_gradient(arrays, places, pooled_all)
    other = send(partial, 0, 1)
    total = partial.astype(F32) + other.astype(F32)
    turn = 2
    while turn < groups:
        total = total + send(total, 0, turn)
        turn *= 2
    block = features // owners
    grad_first = total[:block]
    grad_bias = total[block] + total[block + 1]

    new_whole, new_split = late_call(
        owners_of,
        arrays[early:],
        w_first,
        words[2:],
        (sum_whole, sum_split),
        owners,
        bits,
        [table_whole[0, 0], accum_whole[0], table_split[0, 0], accum_split[0]],
        [
            jax.ShapeDtypeStruct(table_whole.shape[2:], F32),
            jax.ShapeDtypeStruct(table_split.shape[2:], F32),
        ],
    )
    return (grad_first, grad_bias, new_whole[None, None], new_split[None, None])


def solution(mesh):
    def body(*args):
        return per_device(mesh.shape["grp"], mesh.shape["mem"], *args)

    return jax.shard_map(
        body,
        mesh=mesh,
        in_specs=(
            P(("grp", "mem"), None),
            P(("grp", "mem"), None),
            P(),
            P(),
            P("grp", None),
            P("grp", None),
            P("grp", "mem", None, None),
            P("grp", None, None, None),
            P("grp", "mem", None, None),
            P("grp", "mem", None),
            P("grp", "mem", None, None),
            P("grp", None, None),
        ),
        out_specs=(P("mem", None), P(), P("grp", "mem", None, None), P("grp", "mem", None, None)),
        check_vma=False,
    )
```

time: 55.1 us -> 46.7 us (0.85)
  Pallas kernels: 18.7 us -> 11 us
  waiting for transfers between devices: 6.08 us -> 10.5 us
  between operations: 3.49 us -> 0.9 us
  local copies, waits for them, and re-layouts: 6.2 us -> 4.29 us
  other arithmetic: 1.28 us -> 0.64 us
    pallas_call x2 -> x1, Pallas kernels: 11.1 us -> 2.53 us  [slot_call(): pl.pallas_call(functools.partial(kernel, bits, len(arrays)), out_shape=ou...]
    pallas_call x0 -> x1, Pallas kernels: none -> 5.41 us  [late_call(): pl.pallas_call(functools.partial(late_kernel, bits, tables, len(arrays)),...]
    ppermute x12, waiting for transfers between devices: 6.07 us -> 10.5 us  [send(): return lax.ppermute(values, ('grp', 'mem'), pairs)]
    pallas_call x1, Pallas kernels: 3.28 us -> 0.85 us  [block_gradient(): pl.pallas_call(functools.partial(block_kernel, places, len(arrays)), out_...]
    pallas_call x1, Pallas kernels: 4.3 us -> 2.19 us  [hit_words(): pl.pallas_call(functools.partial(word_kernel, bits, turns), out_shape=sha...]
    another operation x2 -> x0, local copies, waits for them, and re-layouts: 1.91 us -> none  [the longest x1 1.3 us: per_device(): jnp.stack([position, position, whole_id, shard_id // CS, shard_id % CS])]
    reduce_sum x1 -> x0, other arithmetic: 0.64 us -> none  [per_device(): whole_id = jnp.sum(jnp.where(table_owner[0] == position, order, 0))]
  transfers between devices with their start and end apart: 13 -> 13, of which waited for: 3 -> 5; matrix products, arithmetic and copies ran while one was open for 7% -> 2% of each run, Pallas kernels for 28% -> 22%
where the time goes in v3:
time: 46.7 us; the launch traced here: 46.5 us
  starting transfers between devices  16.6 us (36%)
  Pallas kernels  11 us (24%)
  waiting for transfers between devices  10.5 us (22%)
  local copies, waits for them, and re-layouts  4.29 us (9%)
  matrix products  2.54 us (5%)
  between operations  0.9 us (2%)
  other arithmetic  0.64 us (1%)
    ppermute x12, starting transfers between devices, send(): return lax.ppermute(values, ('grp', 'mem'), pairs)  13 us
    ppermute x12, waiting for transfers between devices, send(): return lax.ppermute(values, ('grp', 'mem'), pairs)  10.5 us
    pallas_call x1, Pallas kernels, late_call(): pl.pallas_call(functools.partial(late_kernel, bits, tables, len(arrays)),...  5.41 us
    all_to_all x1, starting transfers between devices, per_device(): lax.all_to_all(pooled_rows, 'mem', split_axis=0, concat_axis=0, tiled=True)  3.59 us
    dot_general x1, matrix products, per_device(): pre_act = jnp.dot(pooled, w_first, preferred_element_type=F32) + bias_first  2.54 us
    pallas_call x1, Pallas kernels, slot_call(): pl.pallas_call(functools.partial(kernel, bits, len(arrays)), out_shape=ou...  2.53 us
    unnamed x34, local copies, waits for them, and re-layouts  2.45 us
    pallas_call x1, Pallas kernels, hit_words(): pl.pallas_call(functools.partial(word_kernel, bits, turns), out_shape=sha...  2.19 us
  transfers between devices with their start and end apart: 13, of which 5 were waited for; matrix products, arithmetic and copies ran while one was open for 2% of the time, Pallas kernels for 22%

profile of v3, /device:TPU:0, one launch (start us, length us, event | category | flops | bytes accessed | tf_op | source)
XLA Modules:
  0.0 46.5 jit_solution(17350755209474510313)
XLA Ops:
  0.6 0.0 copy-start.15
  0.6 2.5 %multiply_convert_fusion.refs_0_ = bf16[128,512]{1,0:T(8,128)(2,1)S(1)} fusion(bf16[128,2560]{1,0:T(8,128)(2,1)} %param.12, bf16[2560,512]{1,0:T(8,128)(2,1)} %refs_6_.1, bf16[128,512]{1,0:T(8,128)(2,1)} %param.13, f32[512]{0:T(512)} %param.15), kind=kOutput, calls=%fused_computation.3 | convolution fusion | flops 336265216 | bytes 3540992 | tf_op jit(solution)/shard_map/dot_general | solution.py:315
  3.2 0.0 copy-start.1
  3.2 0.0 copy-start.8
  3.2 0.0 copy-start.9
  3.2 0.0 copy-start.10
  3.2 3.0 %collective-permute-start.1 = (bf16[128,512]{1,0:T(8,128)(2,1)S(1)}, bf16[128,512]{1,0:T(8,128)(2,1)S(1)}, u32[]{:S(2)}, u32[]{:S(2)}) collective-permute-start(bf16[128,512]{1,0:T(8,128)(2,1)S(1)} %multiply_convert_fusion.refs_0_), channel_id=1, source_target_pairs={{0,2},{1,3},{2,0},{3,1},{4,6},{5,7},{6,4},{7,5},{8,10},{9,11},{10,... | collective-permute-start | bytes 393224 | tf_op jit(solution)/shard_map/ppermute | solution.py:313
  6.3 1.6 %collective-permute-start.2 = (bf16[128,512]{1,0:T(8,128)(2,1)S(1)}, bf16[128,512]{1,0:T(8,128)(2,1)S(1)}, u32[]{:S(2)}, u32[]{:S(2)}) collective-permute-start(bf16[128,512]{1,0:T(8,128)(2,1)S(1)} %multiply_convert_fusion.refs_0_), channel_id=1, source_target_pairs={{0,4},{1,5},{2,6},{3,7},{4,0},{5,1},{6,2},{7,3},{8,12},{9,13},{10,... | collective-permute-start | bytes 393224 | tf_op jit(solution)/shard_map/ppermute | solution.py:313
  7.8 2.6 %collective-permute-start.3 = (bf16[128,512]{1,0:T(8,128)(2,1)S(1)}, bf16[128,512]{1,0:T(8,128)(2,1)S(1)}, u32[]{:S(2)}, u32[]{:S(2)}) collective-permute-start(bf16[128,512]{1,0:T(8,128)(2,1)S(1)} %multiply_convert_fusion.refs_0_), channel_id=1, source_target_pairs={{0,8},{1,9},{2,10},{3,11},{4,12},{5,13},{6,14},{7,15},{8,0},{9,1},... | collective-permute-start | bytes 393224 | tf_op jit(solution)/shard_map/ppermute | solution.py:313
  10.4 0.0 collective-permute-start
  10.4 0.0 copy-done.15
  10.4 1.1 %copy.16 = bf16[2560,128]{1,0:T(8,128)(2,1)} copy(bf16[2560,128]{0,1:T(8,128)(2,1)S(1)} %bitcast.19) | data formatting | bytes 1310720 | tf_op jit(solution)/shard_map/transpose | solution.py:325
  11.5 3.6 %all-to-all-start = ((bf16[16,160,128]{2,1,0:T(8,128)(2,1)}), bf16[16,160,128]{2,1,0:T(8,128)(2,1)S(1)}, u32[]{:S(2)}, u32[]{:S(2)}) async-start(bf16[16,160,128]{2,1,0:T(8,128)(2,1)} %bitcast.5), calls=%async_computation | async-start | bytes 1310720 | tf_op jit(solution)/shard_map/all_to_all | solution.py:326
  15.1 0.0 collective-permute-done.1
  15.2 0.0 collective-permute-done.2
  15.2 1.1 %collective-permute-done.3 = bf16[128,512]{1,0:T(8,128)(2,1)S(1)} collective-permute-done((bf16[128,512]{1,0:T(8,128)(2,1)S(1)}, bf16[128,512]{1,0:T(8,128)(2,1)S(1)}, u32[]{:S(2)}, u32[]{:S(2)}) %collective-permute-start.3) | collective-permute-done | bytes 131104 | tf_op jit(solution)/shard_map/ppermute | solution.py:313
  16.3 0.1 collective-permute-start.4
  16.4 0.0 copy-done.1
  16.4 0.0 copy-done.8
  16.4 0.0 copy-done.9
  16.4 0.0 copy-done.10
  16.4 0.0 copy-start
  16.4 2.2 %hit_words.1 = (s32[128,1024]{1,0:T(8,128)S(1)}, s32[128,1024]{1,0:T(8,128)S(1)}, s32[128,1024]{1,0:T(8,128)S(1)}, s32[128,1024]{1,0:T(8,128)S(1)}) custom-call(s32[1,16]{1,0:T(1,128)S(1)} %copy-done.9, s32[1,16]{1,0:T(1,128)S(1)} %copy-done.10, s32[8,2048]{1,0:T(8,128)S(1)} %bitcast.18, s32[4,8,2048]{2,1,0:T(8,128)S(1)} %bitcast.17), custom_call_target="tpu_custom_call" | custom-call | flops 4000000000 | bytes 2000000 | tf_op jit(solution)/shard_map/hit_words/pallas_call | solution.py:77
  18.6 0.0 copy-start.13
  18.6 0.0 copy-start.14
  18.7 0.8 %copy-done.13 = s32[128,1024]{1,0:T(8,128)} copy-done((s32[128,1024]{1,0:T(8,128)}, s32[128,1024]{1,0:T(8,128)S(1)}, u32[]{:S(2)}) %copy-start.13) | copy-done | bytes 524312
  19.4 0.8 %collective-permute-start.5 = (bf16[256,512]{1,0:T(8,128)(2,1)S(1)}, bf16[256,512]{1,0:T(8,128)(2,1)S(1)}, u32[]{:S(2)}, u32[]{:S(2)}) collective-permute-start(bf16[256,512]{1,0:T(8,128)(2,1)S(1)} %pad_maximum_fusion), channel_id=1, source_target_pairs={{0,2},{1,3},{2,0},{3,1},{4,6},{5,7},{6,4},{7,5},{8,10},{9,11},{10,... | collective-permute-start | bytes 786440 | tf_op jit(solution)/shard_map/ppermute | solution.py:313
  20.2 1.5 %collective-permute-start.6 = (bf16[128,512]{1,0:T(8,128)(2,1)S(1)}, bf16[128,512]{1,0:T(8,128)(2,1)S(1)}, u32[]{:S(2)}, u32[]{:S(2)}) collective-permute-start(bf16[128,512]{1,0:T(8,128)(2,1)S(1)} %collective-permute-done.3), channel_id=1, source_target_pairs={{0,4},{1,5},{2,6},{3,7},{4,0},{5,1},{6,2},{7,3},{8,12},{9,13},{10,... | collective-permute-start | bytes 393224 | tf_op jit(solution)/shard_map/ppermute | solution.py:313
  21.7 1.2 %collective-permute-start.7 = (bf16[128,512]{1,0:T(8,128)(2,1)S(1)}, bf16[128,512]{1,0:T(8,128)(2,1)S(1)}, u32[]{:S(2)}, u32[]{:S(2)}) collective-permute-start(bf16[128,512]{1,0:T(8,128)(2,1)S(1)} %collective-permute-done.3), channel_id=1, source_target_pairs={{0,6},{1,7},{2,4},{3,5},{4,2},{5,3},{6,0},{7,1},{8,14},{9,15},{10,... | collective-permute-start | bytes 393224 | tf_op jit(solution)/shard_map/ppermute | solution.py:313
  22.9 0.0 collective-permute-done.refs_1_
  22.9 0.0 collective-permute-done.4.refs_3_
  22.9 0.0 copy-done
  22.9 2.5 %shard_map.147 = (f32[128,1024]{1,0:T(8,128)S(1)}, f32[128,1024]{1,0:T(8,128)S(1)}) custom-call(s32[1,16]{1,0:T(1,128)S(1)} %copy-done.9, s32[1,16]{1,0:T(1,128)S(1)} %copy-done.10, bf16[128,512]{1,0:T(8,128)(2,1)S(1)} %multiply_convert_fusion.refs_0_, bf16[128,512]{1,0:T(8,128)(2,1)S(1)} %collective-permute-done.refs_1_, ...), custom_call_target="tpu_custom_call" | custom-call | flops 4000000000 | bytes 4000000 | tf_op jit(solution)/shard_map/pallas_call | solution.py:232
  25.5 0.0 copy-done.14
  25.5 0.0 copy-start.11
  25.5 0.8 %copy-done.11 = f32[128,1024]{1,0:T(8,128)} copy-done((f32[128,1024]{1,0:T(8,128)}, f32[128,1024]{1,0:T(8,128)S(1)}, u32[]{:S(2)}) %copy-start.11) | copy-done | bytes 524312
  26.3 0.0 copy-start.12
  26.3 0.8 %copy-done.12 = f32[128,1024]{1,0:T(8,128)} copy-done((f32[128,1024]{1,0:T(8,128)}, f32[128,1024]{1,0:T(8,128)S(1)}, u32[]{:S(2)}) %copy-start.12) | copy-done | bytes 524312
  27.1 4.9 %collective-permute-done.6.refs_6_.refs_2_ = bf16[128,512]{1,0:T(8,128)(2,1)S(1)} collective-permute-done((bf16[128,512]{1,0:T(8,128)(2,1)S(1)}, bf16[128,512]{1,0:T(8,128)(2,1)S(1)}, u32[]{:S(2)}, u32[]{:S(2)}) %collective-permute-start.6) | collective-permute-done | bytes 131104 | tf_op jit(solution)/shard_map/ppermute | solution.py:313
  32.0 0.0 copy-start.4
  32.0 3.2 %collective-permute-done.7.refs_8_.refs_4_ = bf16[128,512]{1,0:T(8,128)(2,1)S(1)} collective-permute-done((bf16[128,512]{1,0:T(8,128)(2,1)S(1)}, bf16[128,512]{1,0:T(8,128)(2,1)S(1)}, u32[]{:S(2)}, u32[]{:S(2)}) %collective-permute-start.7) | collective-permute-done | bytes 131104 | tf_op jit(solution)/shard_map/ppermute | solution.py:313
  35.2 0.0 copy-start.5
  35.2 0.0 collective-permute-done.5.refs_4_.refs_0_
  35.2 0.0 copy-start.2
  35.2 0.1 collective-permute-start.8
  35.3 0.5 %collective-permute-start.10 = (bf16[128,512]{1,0:T(8,128)(2,1)S(1)}, bf16[128,512]{1,0:T(8,128)(2,1)S(1)}, u32[]{:S(2)}, u32[]{:S(2)}) collective-permute-start(bf16[128,512]{1,0:T(8,128)(2,1)S(1)} %collective-permute-done.7.refs_8_.refs_4_), channel_id=1, source_target_pairs={{0,1},{1,0},{2,3},{3,2},{4,5},{5,4},{6,7},{7,6},{8,9},{9,8},{10,11... | collective-permute-start | bytes 393224 | tf_op jit(solution)/shard_map/ppermute | solution.py:313
  35.8 0.1 collective-permute-start.9
  35.8 1.1 %collective-permute-done.10.refs_9_.refs_5_ = bf16[128,512]{1,0:T(8,128)(2,1)S(1)} collective-permute-done((bf16[128,512]{1,0:T(8,128)(2,1)S(1)}, bf16[128,512]{1,0:T(8,128)(2,1)S(1)}, u32[]{:S(2)}, u32[]{:S(2)}) %collective-permute-start.10) | collective-permute-done | bytes 131104 | tf_op jit(solution)/shard_map/ppermute | solution.py:313
  37.0 0.0 copy-start.6
  37.0 0.2 collective-permute-done.9.refs_7_.refs_3_
  37.2 0.0 collective-permute-done.8.refs_5_.refs_1_
  37.2 0.0 all-to-all-done.refs_10_
  37.2 0.9 %block_gradient.1 = bf16[176,512]{1,0:T(8,128)(2,1)S(1)} custom-call(bf16[128,512]{1,0:T(8,128)(2,1)S(1)} %multiply_convert_fusion.refs_0_, bf16[128,512]{1,0:T(8,128)(2,1)S(1)} %collective-permute-done.refs_1_, bf16[384,512]{1,0:T(8,128)(2,1)S(1)} %constant_dynamic-update-slice_fusion.refs_2_, bf16[384,512]{1,0:T(8,128)(2,1)S(1)} %collective-permute-done.4.refs_3_, ...), custom_call_target="tpu_custom_call" | custom-call | flops 1000000000 | bytes 3000000 | tf_op jit(solution)/shard_map/block_gradient/pallas_call | solution.py:276
  38.0 1.6 %collective-permute-start.11 = (bf16[176,512]{1,0:T(8,128)(2,1)S(1)}, bf16[176,512]{1,0:T(8,128)(2,1)S(1)}, u32[]{:S(2)}, u32[]{:S(2)}) collective-permute-start(bf16[176,512]{1,0:T(8,128)(2,1)S(1)} %block_gradient.1), channel_id=1, source_target_pairs={{0,16},{1,17},{2,18},{3,19},{4,20},{5,21},{6,22},{7,23},{8,24},{9,... | collective-permute-start | bytes 540680 | tf_op jit(solution)/shard_map/ppermute | solution.py:313
  39.6 0.0 copy-done.4
  39.6 0.0 copy-done.5
  39.6 0.0 copy-done.2
  39.6 0.0 copy-done.6
  39.6 0.0 copy-done.7
  39.6 0.0 copy-done.3
  39.7 5.4 %late_gradients.1 = (f32[128,1024]{1,0:T(8,128)}, f32[32,1024]{1,0:T(8,128)}) custom-call(s32[1,16]{1,0:T(1,128)} %owner_ref.5, s32[1,16]{1,0:T(1,128)} %shard_ref.5, bf16[256,512]{1,0:T(8,128)(2,1)} %copy-done.2, bf16[256,512]{1,0:T(8,128)(2,1)} %copy-done.3, bf16[128,512]{1,0:T(8,128)(2,1)} %copy-done.4, bf16[128,512]{1,0:T(8,128)(2,1)} %copy-done.7, ...), custom_call_target="tpu_custom_call" | custom-call | flops 4000000000 | bytes 4000000 | tf_op jit(solution)/shard_map/late_gradients/pallas_call | solution.py:202
  45.1 0.0 collective-permute-done.11
  45.1 0.7 %slice.12 = f32[160,512]{1,0:T(8,128)} slice(f32[176,512]{1,0:T(8,128)S(1)} %convert_add_fusion), slice={[0:160], [0:512]} | slice | bytes 655360 | tf_op jit(solution)/shard_map/slice | solution.py:392
  45.9 0.6 %slice_add_fusion = f32[1,512]{1,0:T(1,128)} fusion(f32[176,512]{1,0:T(8,128)S(1)} %convert_add_fusion), kind=kLoop, calls=%fused_computation.7 | loop fusion | flops 512 | bytes 6144 | tf_op jit(solution)/shard_map/add | solution.py:393
  (7 shorter events, 0.1 us)
Async XLA Ops:
  0.6 9.8 %copy-start.15 = (bf16[128,2560]{1,0:T(8,128)(2,1)S(1)}, bf16[128,2560]{1,0:T(8,128)(2,1)}, u32[]{:S(2)}) copy-start(bf16[128,2560]{1,0:T(8,128)(2,1)} %param.12) | copy-start | bytes 1966084
  3.2 13.2 %copy-start.1 = (s32[1,4,2048,8]{2,3,1,0:T(8,128)S(1)}, s32[1,4,2048,8]{2,3,1,0:T(8,128)}, u32[]{:S(2)}) copy-start(s32[1,4,2048,8]{2,3,1,0:T(8,128)} %param.19) | copy-start | bytes 786436
  3.2 13.2 %copy-start.8 = (s32[1,1,2048,8]{2,3,1,0:T(8,128)S(1)}, s32[1,1,2048,8]{2,3,1,0:T(8,128)}, u32[]{:S(2)}) copy-start(s32[1,1,2048,8]{2,3,1,0:T(8,128)} %param.18) | copy-start | bytes 196612
  3.2 13.2 %copy-start.9 = (s32[1,16]{1,0:T(1,128)S(1)}, s32[1,16]{1,0:T(1,128)}, u32[]{:S(2)}) copy-start(s32[1,16]{1,0:T(1,128)} %owner_ref.5) | copy-start | bytes 196
  3.2 13.2 %copy-start.10 = (s32[1,16]{1,0:T(1,128)S(1)}, s32[1,16]{1,0:T(1,128)}, u32[]{:S(2)}) copy-start(s32[1,16]{1,0:T(1,128)} %shard_ref.5) | copy-start | bytes 196
  3.2 11.9 %collective-permute-start.1 = (bf16[128,512]{1,0:T(8,128)(2,1)S(1)}, bf16[128,512]{1,0:T(8,128)(2,1)S(1)}, u32[]{:S(2)}, u32[]{:S(2)}) collective-permute-start(bf16[128,512]{1,0:T(8,128)(2,1)S(1)} %multiply_convert_fusion.refs_0_), channel_id=1, source_target_pairs={{0,2},{1,3},{2,0},{3,1},{4,6},{5,7},{6,4},{7,5},{8,10},{9,11},{10,... | collective-permute-start | bytes 393224 | tf_op jit(solution)/shard_map/ppermute | solution.py:313
  6.3 8.9 %collective-permute-start.2 = (bf16[128,512]{1,0:T(8,128)(2,1)S(1)}, bf16[128,512]{1,0:T(8,128)(2,1)S(1)}, u32[]{:S(2)}, u32[]{:S(2)}) collective-permute-start(bf16[128,512]{1,0:T(8,128)(2,1)S(1)} %multiply_convert_fusion.refs_0_), channel_id=1, source_target_pairs={{0,4},{1,5},{2,6},{3,7},{4,0},{5,1},{6,2},{7,3},{8,12},{9,13},{10,... | collective-permute-start | bytes 393224 | tf_op jit(solution)/shard_map/ppermute | solution.py:313
  7.8 8.4 %collective-permute-start.3 = (bf16[128,512]{1,0:T(8,128)(2,1)S(1)}, bf16[128,512]{1,0:T(8,128)(2,1)S(1)}, u32[]{:S(2)}, u32[]{:S(2)}) collective-permute-start(bf16[128,512]{1,0:T(8,128)(2,1)S(1)} %multiply_convert_fusion.refs_0_), channel_id=1, source_target_pairs={{0,8},{1,9},{2,10},{3,11},{4,12},{5,13},{6,14},{7,15},{8,0},{9,1},... | collective-permute-start | bytes 393224 | tf_op jit(solution)/shard_map/ppermute | solution.py:313
  10.4 12.5 %collective-permute-start = (bf16[128,512]{1,0:T(8,128)(2,1)S(1)}, bf16[128,512]{1,0:T(8,128)(2,1)S(1)}, u32[]{:S(2)}, u32[]{:S(2)}) collective-permute-start(bf16[128,512]{1,0:T(8,128)(2,1)S(1)} %multiply_convert_fusion.refs_0_), channel_id=1, source_target_pairs={{0,1},{1,0},{2,3},{3,2},{4,5},{5,4},{6,7},{7,6},{8,9},{9,8},{10,11... | collective-permute-start | bytes 393224 | tf_op jit(solution)/shard_map/ppermute | solution.py:313
  11.5 25.7 %all-to-all-start = ((bf16[16,160,128]{2,1,0:T(8,128)(2,1)}), bf16[16,160,128]{2,1,0:T(8,128)(2,1)S(1)}, u32[]{:S(2)}, u32[]{:S(2)}) async-start(bf16[16,160,128]{2,1,0:T(8,128)(2,1)} %bitcast.5), calls=%async_computation | async-start | bytes 1310720 | tf_op jit(solution)/shard_map/all_to_all | solution.py:326
  16.3 6.6 %collective-permute-start.4 = (bf16[384,512]{1,0:T(8,128)(2,1)S(1)}, bf16[384,512]{1,0:T(8,128)(2,1)S(1)}, u32[]{:S(2)}, u32[]{:S(2)}) collective-permute-start(bf16[384,512]{1,0:T(8,128)(2,1)S(1)} %constant_dynamic-update-slice_fusion.refs_2_), channel_id=1, source_target_pairs={{0,1},{1,0},{2,3},{3,2},{4,5},{5,4},{6,7},{7,6},{8,9},{9,8},{10,11... | collective-permute-start | bytes 1179656 | tf_op jit(solution)/shard_map/ppermute | solution.py:313
  16.4 6.5 %copy-start = (bf16[2560,512]{1,0:T(8,128)(2,1)S(1)}, bf16[2560,512]{1,0:T(8,128)(2,1)}, u32[]{:S(2)}) copy-start(bf16[2560,512]{1,0:T(8,128)(2,1)} %refs_6_.1) | copy-start | bytes 7864324
  18.6 0.8 %copy-start.13 = (s32[128,1024]{1,0:T(8,128)}, s32[128,1024]{1,0:T(8,128)S(1)}, u32[]{:S(2)}) copy-start(s32[128,1024]{1,0:T(8,128)S(1)} %get-tuple-element.26.refs_7_) | copy-start | bytes 1572868
  18.6 6.8 %copy-start.14 = (s32[128,1024]{1,0:T(8,128)}, s32[128,1024]{1,0:T(8,128)S(1)}, u32[]{:S(2)}) copy-start(s32[128,1024]{1,0:T(8,128)S(1)} %get-tuple-element.27.refs_8_) | copy-start | bytes 1572868
  19.4 15.8 %collective-permute-start.5 = (bf16[256,512]{1,0:T(8,128)(2,1)S(1)}, bf16[256,512]{1,0:T(8,128)(2,1)S(1)}, u32[]{:S(2)}, u32[]{:S(2)}) collective-permute-start(bf16[256,512]{1,0:T(8,128)(2,1)S(1)} %pad_maximum_fusion), channel_id=1, source_target_pairs={{0,2},{1,3},{2,0},{3,1},{4,6},{5,7},{6,4},{7,5},{8,10},{9,11},{10,... | collective-permute-start | bytes 786440 | tf_op jit(solution)/shard_map/ppermute | solution.py:313
  20.2 11.8 %collective-permute-start.6 = (bf16[128,512]{1,0:T(8,128)(2,1)S(1)}, bf16[128,512]{1,0:T(8,128)(2,1)S(1)}, u32[]{:S(2)}, u32[]{:S(2)}) collective-permute-start(bf16[128,512]{1,0:T(8,128)(2,1)S(1)} %collective-permute-done.3), channel_id=1, source_target_pairs={{0,4},{1,5},{2,6},{3,7},{4,0},{5,1},{6,2},{7,3},{8,12},{9,13},{10,... | collective-permute-start | bytes 393224 | tf_op jit(solution)/shard_map/ppermute | solution.py:313
  21.7 13.5 %collective-permute-start.7 = (bf16[128,512]{1,0:T(8,128)(2,1)S(1)}, bf16[128,512]{1,0:T(8,128)(2,1)S(1)}, u32[]{:S(2)}, u32[]{:S(2)}) collective-permute-start(bf16[128,512]{1,0:T(8,128)(2,1)S(1)} %collective-permute-done.3), channel_id=1, source_target_pairs={{0,6},{1,7},{2,4},{3,5},{4,2},{5,3},{6,0},{7,1},{8,14},{9,15},{10,... | collective-permute-start | bytes 393224 | tf_op jit(solution)/shard_map/ppermute | solution.py:313
  25.5 0.8 %copy-start.11 = (f32[128,1024]{1,0:T(8,128)}, f32[128,1024]{1,0:T(8,128)S(1)}, u32[]{:S(2)}) copy-start(f32[128,1024]{1,0:T(8,128)S(1)} %get-tuple-element.28.refs_9_) | copy-start | bytes 1572868
  26.3 0.8 %copy-start.12 = (f32[128,1024]{1,0:T(8,128)}, f32[128,1024]{1,0:T(8,128)S(1)}, u32[]{:S(2)}) copy-start(f32[128,1024]{1,0:T(8,128)S(1)} %get-tuple-element.29.refs_10_) | copy-start | bytes 1572868
  32.0 7.6 %copy-start.4 = (bf16[128,512]{1,0:T(8,128)(2,1)}, bf16[128,512]{1,0:T(8,128)(2,1)S(1)}, u32[]{:S(2)}) copy-start(bf16[128,512]{1,0:T(8,128)(2,1)S(1)} %collective-permute-done.6.refs_6_.refs_2_) | copy-start | bytes 393220
  35.2 4.4 %copy-start.5 = (bf16[128,512]{1,0:T(8,128)(2,1)}, bf16[128,512]{1,0:T(8,128)(2,1)S(1)}, u32[]{:S(2)}) copy-start(bf16[128,512]{1,0:T(8,128)(2,1)S(1)} %collective-permute-done.7.refs_8_.refs_4_) | copy-start | bytes 393220
  35.2 4.4 %copy-start.2 = (bf16[256,512]{1,0:T(8,128)(2,1)}, bf16[256,512]{1,0:T(8,128)(2,1)S(1)}, u32[]{:S(2)}) copy-start(bf16[256,512]{1,0:T(8,128)(2,1)S(1)} %collective-permute-done.5.refs_4_.refs_0_) | copy-start | bytes 786436
  35.2 2.0 %collective-permute-start.8 = (bf16[256,512]{1,0:T(8,128)(2,1)S(1)}, bf16[256,512]{1,0:T(8,128)(2,1)S(1)}, u32[]{:S(2)}, u32[]{:S(2)}) collective-permute-start(bf16[256,512]{1,0:T(8,128)(2,1)S(1)} %collective-permute-done.5.refs_4_.refs_0_), channel_id=1, source_target_pairs={{0,1},{1,0},{2,3},{3,2},{4,5},{5,4},{6,7},{7,6},{8,9},{9,8},{10,11... | collective-permute-start | bytes 786440 | tf_op jit(solution)/shard_map/ppermute | solution.py:313
  35.3 1.7 %collective-permute-start.10 = (bf16[128,512]{1,0:T(8,128)(2,1)S(1)}, bf16[128,512]{1,0:T(8,128)(2,1)S(1)}, u32[]{:S(2)}, u32[]{:S(2)}) collective-permute-start(bf16[128,512]{1,0:T(8,128)(2,1)S(1)} %collective-permute-done.7.refs_8_.refs_4_), channel_id=1, source_target_pairs={{0,1},{1,0},{2,3},{3,2},{4,5},{5,4},{6,7},{7,6},{8,9},{9,8},{10,11... | collective-permute-start | bytes 393224 | tf_op jit(solution)/shard_map/ppermute | solution.py:313
  35.8 1.4 %collective-permute-start.9 = (bf16[128,512]{1,0:T(8,128)(2,1)S(1)}, bf16[128,512]{1,0:T(8,128)(2,1)S(1)}, u32[]{:S(2)}, u32[]{:S(2)}) collective-permute-start(bf16[128,512]{1,0:T(8,128)(2,1)S(1)} %collective-permute-done.6.refs_6_.refs_2_), channel_id=1, source_target_pairs={{0,1},{1,0},{2,3},{3,2},{4,5},{5,4},{6,7},{7,6},{8,9},{9,8},{10,11... | collective-permute-start | bytes 393224 | tf_op jit(solution)/shard_map/ppermute | solution.py:313
  37.0 2.7 %copy-start.6 = (bf16[128,512]{1,0:T(8,128)(2,1)}, bf16[128,512]{1,0:T(8,128)(2,1)S(1)}, u32[]{:S(2)}) copy-start(bf16[128,512]{1,0:T(8,128)(2,1)S(1)} %collective-permute-done.10.refs_9_.refs_5_) | copy-start | bytes 393220
  37.2 2.5 %copy-start.7 = (bf16[128,512]{1,0:T(8,128)(2,1)}, bf16[128,512]{1,0:T(8,128)(2,1)S(1)}, u32[]{:S(2)}) copy-start(bf16[128,512]{1,0:T(8,128)(2,1)S(1)} %collective-permute-done.9.refs_7_.refs_3_) | copy-start | bytes 393220
  37.2 2.5 %copy-start.3 = (bf16[256,512]{1,0:T(8,128)(2,1)}, bf16[256,512]{1,0:T(8,128)(2,1)S(1)}, u32[]{:S(2)}) copy-start(bf16[256,512]{1,0:T(8,128)(2,1)S(1)} %collective-permute-done.8.refs_5_.refs_1_) | copy-start | bytes 786436
  38.0 7.0 %collective-permute-start.11 = (bf16[176,512]{1,0:T(8,128)(2,1)S(1)}, bf16[176,512]{1,0:T(8,128)(2,1)S(1)}, u32[]{:S(2)}, u32[]{:S(2)}) collective-permute-start(bf16[176,512]{1,0:T(8,128)(2,1)S(1)} %block_gradient.1), channel_id=1, source_target_pairs={{0,16},{1,17},{2,18},{3,19},{4,20},{5,21},{6,22},{7,23},{8,24},{9,... | collective-permute-start | bytes 540680 | tf_op jit(solution)/shard_map/ppermute | solution.py:313

commit v4 on v3

--- a/solution.py
+++ b/solution.py
@@ -39,6 +39,45 @@
 
 def dot_nn(lhs, rhs):
     return lax.dot_general(lhs, rhs, NN_DIMS, preferred_element_type=F32)
+
+
+def finish_kernel(parts, ours, theirs, grad_first, grad_bias, total, line, sems):
+    block = total.shape[0]
+    rows = block // parts
+    extra = ours[block:, :].astype(F32) + theirs[block:, :].astype(F32)
+    line[...] = extra[0:1, :] + extra[1:2, :]
+    stores = [pltpu.make_async_copy(line, grad_bias, sems.at[parts])]
+    stores[0].start()
+    for i in range(parts):
+        span = pl.ds(i * rows, rows)
+        total[span, :] = ours[span, :].astype(F32) + theirs[span, :].astype(F32)
+        stores.append(pltpu.make_async_copy(total.at[span, :], grad_first.at[span, :], sems.at[i]))
+        stores[-1].start()
+    for store in stores:
+        store.wait()
+
+
+def finish(ours, theirs):
+    rows, hidden = ours.shape
+    block = rows - 16
+    parts = 5
+    vmem = pl.BlockSpec(memory_space=pltpu.VMEM)
+    return pl.pallas_call(
+        functools.partial(finish_kernel, parts),
+        out_shape=[
+            jax.ShapeDtypeStruct((block, hidden), F32),
+            jax.ShapeDtypeStruct((1, hidden), F32),
+        ],
+        in_specs=[vmem, vmem],
+        out_specs=[pl.BlockSpec(memory_space=pltpu.HBM)] * 2,
+        scratch_shapes=[
+            pltpu.VMEM((block, hidden), F32),
+            pltpu.VMEM((1, hidden), F32),
+            pltpu.SemaphoreType.DMA((parts + 1,)),
+        ],
+        compiler_params=pltpu.CompilerParams(vmem_limit_bytes=VMEM_BYTES),
+        name="finish",
+    )(ours, theirs)
 
 
 def word_kernel(bits, turns, owner_ref, shard_ref, whole_ref, split_ref, *outs):
@@ -318,7 +357,8 @@
     delta = (grad_hidden.astype(F32) * slope).astype(BF16)
 
     tops = [1 << b for b in range(1, owners.bit_length() - 1)]
-    direct = [send(delta, top) for top in reversed(tops)][::-1]
+    direct = [send(delta, top) for top in reversed(tops[1:])][::-1]
+    direct = [send(delta, tops[0])] + direct
     delta_crossed = send(delta, 1)
 
     pooled_here, _ = lax.optimization_barrier((pooled, delta))
@@ -383,14 +423,18 @@
     places = tuple(where[turn] for turn in range(owners))
     partial = block_gradient(arrays, places, pooled_all)
     other = send(partial, 0, 1)
-    total = partial.astype(F32) + other.astype(F32)
-    turn = 2
-    while turn < groups:
-        total = total + send(total, 0, turn)
-        turn *= 2
     block = features // owners
-    grad_first = total[:block]
-    grad_bias = total[block] + total[block + 1]
+    if groups == 2:
+        grad_first, grad_bias = finish(partial, other)
+        grad_bias = grad_bias[0]
+    else:
+        total = partial.astype(F32) + other.astype(F32)
+        turn = 2
+        while turn < groups:
+            total = total + send(total, 0, turn)
+            turn *= 2
+        grad_first = total[:block]
+        grad_bias = total[block] + total[block + 1]
 
     new_whole, new_split = late_call(
         owners_of,

time: 46.7 us -> 46.1 us (0.987)
  Pallas kernels: 11 us -> 11.8 us
  local copies, waits for them, and re-layouts: 4.29 us -> 3.54 us
  other arithmetic: 0.64 us -> 0.02 us
    pallas_call x0 -> x1, Pallas kernels: none -> 0.78 us  [finish(): pl.pallas_call(functools.partial(finish_kernel, parts), out_shape=[jax.Sh...]
    slice x1 -> x0, local copies, waits for them, and re-layouts: 0.75 us -> none  [per_device(): grad_first = total[:block]]
    add x2 -> x0, other arithmetic: 0.62 us -> none  [the longest x1 0.58 us: per_device(): grad_bias = total[block] + total[block + 1]]
where the time goes in v4:
time: 46.1 us; the launch traced here: 45.9 us
  starting transfers between devices  16.6 us (36%)
  Pallas kernels  11.8 us (26%)
  waiting for transfers between devices  10.5 us (23%)
  local copies, waits for them, and re-layouts  3.54 us (8%)
  matrix products  2.54 us (6%)
  between operations  0.89 us (2%)
    ppermute x12, starting transfers between devices, send(): return lax.ppermute(values, ('grp', 'mem'), pairs)  13 us
    ppermute x12, waiting for transfers between devices, send(): return lax.ppermute(values, ('grp', 'mem'), pairs)  10.5 us
    pallas_call x1, Pallas kernels, late_call(): pl.pallas_call(functools.partial(late_kernel, bits, tables, len(arrays)),...  5.39 us
    all_to_all x1, starting transfers between devices, per_device(): lax.all_to_all(pooled_rows, 'mem', split_axis=0, concat_axis=0, tiled=True)  3.59 us
    dot_general x1, matrix products, per_device(): pre_act = jnp.dot(pooled, w_first, preferred_element_type=F32) + bias_first  2.54 us
    pallas_call x1, Pallas kernels, slot_call(): pl.pallas_call(functools.partial(kernel, bits, len(arrays)), out_shape=ou...  2.54 us
    unnamed x34, local copies, waits for them, and re-layouts  2.46 us
    pallas_call x1, Pallas kernels, hit_words(): pl.pallas_call(functools.partial(word_kernel, bits, turns), out_shape=sha...  2.19 us
  transfers between devices with their start and end apart: 13, of which 5 were waited for; matrix products, arithmetic and copies ran while one was open for 2% of the time, Pallas kernels for 22%

profile of v4, /device:TPU:0, one launch (start us, length us, event | category | flops | bytes accessed | tf_op | source)
XLA Modules:
  0.0 45.9 jit_solution(6415384580734576403)
XLA Ops:
  0.6 0.0 copy-start.15
  0.6 2.5 %multiply_convert_fusion.refs_0_ = bf16[128,512]{1,0:T(8,128)(2,1)S(1)} fusion(bf16[128,2560]{1,0:T(8,128)(2,1)} %param.12, bf16[2560,512]{1,0:T(8,128)(2,1)} %refs_6_.1, bf16[128,512]{1,0:T(8,128)(2,1)} %param.13, f32[512]{0:T(512)} %param.15), kind=kOutput, calls=%fused_computation.2 | convolution fusion | flops 336265216 | bytes 3540992 | tf_op jit(solution)/shard_map/dot_general | solution.py:354
  3.2 0.0 copy-start.1
  3.2 0.0 copy-start.8
  3.2 0.0 copy-start.9
  3.2 0.0 copy-start.10
  3.2 3.0 %collective-permute-start.1 = (bf16[128,512]{1,0:T(8,128)(2,1)S(1)}, bf16[128,512]{1,0:T(8,128)(2,1)S(1)}, u32[]{:S(2)}, u32[]{:S(2)}) collective-permute-start(bf16[128,512]{1,0:T(8,128)(2,1)S(1)} %multiply_convert_fusion.refs_0_), channel_id=1, source_target_pairs={{0,2},{1,3},{2,0},{3,1},{4,6},{5,7},{6,4},{7,5},{8,10},{9,11},{10,... | collective-permute-start | bytes 393224 | tf_op jit(solution)/shard_map/ppermute | solution.py:352
  6.3 1.6 %collective-permute-start.2 = (bf16[128,512]{1,0:T(8,128)(2,1)S(1)}, bf16[128,512]{1,0:T(8,128)(2,1)S(1)}, u32[]{:S(2)}, u32[]{:S(2)}) collective-permute-start(bf16[128,512]{1,0:T(8,128)(2,1)S(1)} %multiply_convert_fusion.refs_0_), channel_id=1, source_target_pairs={{0,4},{1,5},{2,6},{3,7},{4,0},{5,1},{6,2},{7,3},{8,12},{9,13},{10,... | collective-permute-start | bytes 393224 | tf_op jit(solution)/shard_map/ppermute | solution.py:352
  7.8 2.6 %collective-permute-start.3 = (bf16[128,512]{1,0:T(8,128)(2,1)S(1)}, bf16[128,512]{1,0:T(8,128)(2,1)S(1)}, u32[]{:S(2)}, u32[]{:S(2)}) collective-permute-start(bf16[128,512]{1,0:T(8,128)(2,1)S(1)} %multiply_convert_fusion.refs_0_), channel_id=1, source_target_pairs={{0,8},{1,9},{2,10},{3,11},{4,12},{5,13},{6,14},{7,15},{8,0},{9,1},... | collective-permute-start | bytes 393224 | tf_op jit(solution)/shard_map/ppermute | solution.py:352
  10.4 0.0 collective-permute-start
  10.4 0.0 copy-done.15
  10.4 1.1 %copy.16 = bf16[2560,128]{1,0:T(8,128)(2,1)} copy(bf16[2560,128]{0,1:T(8,128)(2,1)S(1)} %bitcast.19) | data formatting | bytes 1310720 | tf_op jit(solution)/shard_map/transpose | solution.py:365
  11.5 3.6 %all-to-all-start = ((bf16[16,160,128]{2,1,0:T(8,128)(2,1)}), bf16[16,160,128]{2,1,0:T(8,128)(2,1)S(1)}, u32[]{:S(2)}, u32[]{:S(2)}) async-start(bf16[16,160,128]{2,1,0:T(8,128)(2,1)} %bitcast.5), calls=%async_computation | async-start | bytes 1310720 | tf_op jit(solution)/shard_map/all_to_all | solution.py:366
  15.1 0.0 collective-permute-done.1
  15.1 0.0 collective-permute-done.2
  15.2 1.1 %collective-permute-done.3 = bf16[128,512]{1,0:T(8,128)(2,1)S(1)} collective-permute-done((bf16[128,512]{1,0:T(8,128)(2,1)S(1)}, bf16[128,512]{1,0:T(8,128)(2,1)S(1)}, u32[]{:S(2)}, u32[]{:S(2)}) %collective-permute-start.3) | collective-permute-done | bytes 131104 | tf_op jit(solution)/shard_map/ppermute | solution.py:352
  16.3 0.1 collective-permute-start.4
  16.4 0.0 copy-done.1
  16.4 0.0 copy-done.8
  16.4 0.0 copy-done.9
  16.4 0.0 copy-done.10
  16.4 0.0 copy-start
  16.4 2.2 %hit_words.1 = (s32[128,1024]{1,0:T(8,128)S(1)}, s32[128,1024]{1,0:T(8,128)S(1)}, s32[128,1024]{1,0:T(8,128)S(1)}, s32[128,1024]{1,0:T(8,128)S(1)}) custom-call(s32[1,16]{1,0:T(1,128)S(1)} %copy-done.9, s32[1,16]{1,0:T(1,128)S(1)} %copy-done.10, s32[8,2048]{1,0:T(8,128)S(1)} %bitcast.18, s32[4,8,2048]{2,1,0:T(8,128)S(1)} %bitcast.17), custom_call_target="tpu_custom_call" | custom-call | flops 4000000000 | bytes 2000000 | tf_op jit(solution)/shard_map/hit_words/pallas_call | solution.py:116
  18.6 0.0 copy-start.13
  18.6 0.0 copy-start.14
  18.7 0.8 %copy-done.13 = s32[128,1024]{1,0:T(8,128)} copy-done((s32[128,1024]{1,0:T(8,128)}, s32[128,1024]{1,0:T(8,128)S(1)}, u32[]{:S(2)}) %copy-start.13) | copy-done | bytes 524312
  19.5 0.8 %collective-permute-start.5 = (bf16[256,512]{1,0:T(8,128)(2,1)S(1)}, bf16[256,512]{1,0:T(8,128)(2,1)S(1)}, u32[]{:S(2)}, u32[]{:S(2)}) collective-permute-start(bf16[256,512]{1,0:T(8,128)(2,1)S(1)} %pad_maximum_fusion), channel_id=1, source_target_pairs={{0,2},{1,3},{2,0},{3,1},{4,6},{5,7},{6,4},{7,5},{8,10},{9,11},{10,... | collective-permute-start | bytes 786440 | tf_op jit(solution)/shard_map/ppermute | solution.py:352
  20.2 1.5 %collective-permute-start.6 = (bf16[128,512]{1,0:T(8,128)(2,1)S(1)}, bf16[128,512]{1,0:T(8,128)(2,1)S(1)}, u32[]{:S(2)}, u32[]{:S(2)}) collective-permute-start(bf16[128,512]{1,0:T(8,128)(2,1)S(1)} %collective-permute-done.3), channel_id=1, source_target_pairs={{0,4},{1,5},{2,6},{3,7},{4,0},{5,1},{6,2},{7,3},{8,12},{9,13},{10,... | collective-permute-start | bytes 393224 | tf_op jit(solution)/shard_map/ppermute | solution.py:352
  21.7 1.2 %collective-permute-start.7 = (bf16[128,512]{1,0:T(8,128)(2,1)S(1)}, bf16[128,512]{1,0:T(8,128)(2,1)S(1)}, u32[]{:S(2)}, u32[]{:S(2)}) collective-permute-start(bf16[128,512]{1,0:T(8,128)(2,1)S(1)} %collective-permute-done.3), channel_id=1, source_target_pairs={{0,6},{1,7},{2,4},{3,5},{4,2},{5,3},{6,0},{7,1},{8,14},{9,15},{10,... | collective-permute-start | bytes 393224 | tf_op jit(solution)/shard_map/ppermute | solution.py:352
  22.9 0.0 collective-permute-done.refs_1_
  22.9 0.0 collective-permute-done.4.refs_3_
  22.9 0.0 copy-done
  23.0 2.5 %shard_map.147 = (f32[128,1024]{1,0:T(8,128)S(1)}, f32[128,1024]{1,0:T(8,128)S(1)}) custom-call(s32[1,16]{1,0:T(1,128)S(1)} %copy-done.9, s32[1,16]{1,0:T(1,128)S(1)} %copy-done.10, bf16[128,512]{1,0:T(8,128)(2,1)S(1)} %multiply_convert_fusion.refs_0_, bf16[128,512]{1,0:T(8,128)(2,1)S(1)} %collective-permute-done.refs_1_, ...), custom_call_target="tpu_custom_call" | custom-call | flops 4000000000 | bytes 4000000 | tf_op jit(solution)/shard_map/pallas_call | solution.py:271
  25.5 0.0 copy-done.14
  25.5 0.0 copy-start.11
  25.5 0.8 %copy-done.11 = f32[128,1024]{1,0:T(8,128)} copy-done((f32[128,1024]{1,0:T(8,128)}, f32[128,1024]{1,0:T(8,128)S(1)}, u32[]{:S(2)}) %copy-start.11) | copy-done | bytes 524312
  26.3 0.0 copy-start.12
  26.3 0.8 %copy-done.12 = f32[128,1024]{1,0:T(8,128)} copy-done((f32[128,1024]{1,0:T(8,128)}, f32[128,1024]{1,0:T(8,128)S(1)}, u32[]{:S(2)}) %copy-start.12) | copy-done | bytes 524312
  27.1 4.9 %collective-permute-done.6.refs_6_.refs_2_ = bf16[128,512]{1,0:T(8,128)(2,1)S(1)} collective-permute-done((bf16[128,512]{1,0:T(8,128)(2,1)S(1)}, bf16[128,512]{1,0:T(8,128)(2,1)S(1)}, u32[]{:S(2)}, u32[]{:S(2)}) %collective-permute-start.6) | collective-permute-done | bytes 131104 | tf_op jit(solution)/shard_map/ppermute | solution.py:352
  32.0 0.0 copy-start.4
  32.0 3.2 %collective-permute-done.7.refs_8_.refs_4_ = bf16[128,512]{1,0:T(8,128)(2,1)S(1)} collective-permute-done((bf16[128,512]{1,0:T(8,128)(2,1)S(1)}, bf16[128,512]{1,0:T(8,128)(2,1)S(1)}, u32[]{:S(2)}, u32[]{:S(2)}) %collective-permute-start.7) | collective-permute-done | bytes 131104 | tf_op jit(solution)/shard_map/ppermute | solution.py:352
  35.2 0.0 copy-start.5
  35.2 0.0 collective-permute-done.5.refs_4_.refs_0_
  35.2 0.0 copy-start.2
  35.2 0.1 collective-permute-start.8
  35.3 0.5 %collective-permute-start.10 = (bf16[128,512]{1,0:T(8,128)(2,1)S(1)}, bf16[128,512]{1,0:T(8,128)(2,1)S(1)}, u32[]{:S(2)}, u32[]{:S(2)}) collective-permute-start(bf16[128,512]{1,0:T(8,128)(2,1)S(1)} %collective-permute-done.7.refs_8_.refs_4_), channel_id=1, source_target_pairs={{0,1},{1,0},{2,3},{3,2},{4,5},{5,4},{6,7},{7,6},{8,9},{9,8},{10,11... | collective-permute-start | bytes 393224 | tf_op jit(solution)/shard_map/ppermute | solution.py:352
  35.8 0.1 collective-permute-start.9
  35.8 1.1 %collective-permute-done.10.refs_9_.refs_5_ = bf16[128,512]{1,0:T(8,128)(2,1)S(1)} collective-permute-done((bf16[128,512]{1,0:T(8,128)(2,1)S(1)}, bf16[128,512]{1,0:T(8,128)(2,1)S(1)}, u32[]{:S(2)}, u32[]{:S(2)}) %collective-permute-start.10) | collective-permute-done | bytes 131104 | tf_op jit(solution)/shard_map/ppermute | solution.py:352
  37.0 0.0 copy-start.6
  37.0 0.2 collective-permute-done.9.refs_7_.refs_3_
  37.2 0.0 copy-start.7
  37.2 0.0 collective-permute-done.8.refs_5_.refs_1_
  37.2 0.0 all-to-all-done.refs_10_
  37.2 0.8 %block_gradient.1.ours = bf16[176,512]{1,0:T(8,128)(2,1)S(1)} custom-call(bf16[128,512]{1,0:T(8,128)(2,1)S(1)} %multiply_convert_fusion.refs_0_, bf16[128,512]{1,0:T(8,128)(2,1)S(1)} %collective-permute-done.refs_1_, bf16[384,512]{1,0:T(8,128)(2,1)S(1)} %constant_dynamic-update-slice_fusion.refs_2_, bf16[384,512]{1,0:T(8,128)(2,1)S(1)} %collective-permute-done.4.refs_3_, ...), custom_call_target="tpu_custom_call" | custom-call | flops 1000000000 | bytes 3000000 | tf_op jit(solution)/shard_map/block_gradient/pallas_call | solution.py:315
  38.0 1.6 %collective-permute-start.11 = (bf16[176,512]{1,0:T(8,128)(2,1)S(1)}, bf16[176,512]{1,0:T(8,128)(2,1)S(1)}, u32[]{:S(2)}, u32[]{:S(2)}) collective-permute-start(bf16[176,512]{1,0:T(8,128)(2,1)S(1)} %block_gradient.1.ours), channel_id=1, source_target_pairs={{0,16},{1,17},{2,18},{3,19},{4,20},{5,21},{6,22},{7,23},{8,24},{9,... | collective-permute-start | bytes 540680 | tf_op jit(solution)/shard_map/ppermute | solution.py:352
  39.6 0.0 copy-done.4
  39.6 0.0 copy-done.5
  39.6 0.0 copy-done.2
  39.6 0.0 copy-done.6
  39.6 0.0 copy-done.7
  39.6 0.0 copy-done.3
  39.7 5.4 %late_gradients.1 = (f32[128,1024]{1,0:T(8,128)}, f32[32,1024]{1,0:T(8,128)}) custom-call(s32[1,16]{1,0:T(1,128)} %owner_ref.5, s32[1,16]{1,0:T(1,128)} %shard_ref.5, bf16[256,512]{1,0:T(8,128)(2,1)} %copy-done.2, bf16[256,512]{1,0:T(8,128)(2,1)} %copy-done.3, bf16[128,512]{1,0:T(8,128)(2,1)} %copy-done.4, bf16[128,512]{1,0:T(8,128)(2,1)} %copy-done.7, ...), custom_call_target="tpu_custom_call" | custom-call | flops 4000000000 | bytes 4000000 | tf_op jit(solution)/shard_map/late_gradients/pallas_call | solution.py:241
  45.1 0.0 collective-permute-done.11.theirs
  45.1 0.8 %finish.1 = (f32[160,512]{1,0:T(8,128)}, f32[1,512]{1,0:T(1,128)}) custom-call(bf16[176,512]{1,0:T(8,128)(2,1)S(1)} %block_gradient.1.ours, bf16[176,512]{1,0:T(8,128)(2,1)S(1)} %collective-permute-done.11.theirs), custom_call_target="tpu_custom_call" | custom-call | tf_op jit(solution)/shard_map/finish/pallas_call | solution.py:65
  (5 shorter events, 0.1 us)
Async XLA Ops:
  0.6 9.8 %copy-start.15 = (bf16[128,2560]{1,0:T(8,128)(2,1)S(1)}, bf16[128,2560]{1,0:T(8,128)(2,1)}, u32[]{:S(2)}) copy-start(bf16[128,2560]{1,0:T(8,128)(2,1)} %param.12) | copy-start | bytes 1966084
  3.2 13.2 %copy-start.1 = (s32[1,4,2048,8]{2,3,1,0:T(8,128)S(1)}, s32[1,4,2048,8]{2,3,1,0:T(8,128)}, u32[]{:S(2)}) copy-start(s32[1,4,2048,8]{2,3,1,0:T(8,128)} %param.19) | copy-start | bytes 786436
  3.2 13.2 %copy-start.8 = (s32[1,1,2048,8]{2,3,1,0:T(8,128)S(1)}, s32[1,1,2048,8]{2,3,1,0:T(8,128)}, u32[]{:S(2)}) copy-start(s32[1,1,2048,8]{2,3,1,0:T(8,128)} %param.18) | copy-start | bytes 196612
  3.2 13.2 %copy-start.9 = (s32[1,16]{1,0:T(1,128)S(1)}, s32[1,16]{1,0:T(1,128)}, u32[]{:S(2)}) copy-start(s32[1,16]{1,0:T(1,128)} %owner_ref.5) | copy-start | bytes 196
  3.2 13.2 %copy-start.10 = (s32[1,16]{1,0:T(1,128)S(1)}, s32[1,16]{1,0:T(1,128)}, u32[]{:S(2)}) copy-start(s32[1,16]{1,0:T(1,128)} %shard_ref.5) | copy-start | bytes 196
  3.2 11.9 %collective-permute-start.1 = (bf16[128,512]{1,0:T(8,128)(2,1)S(1)}, bf16[128,512]{1,0:T(8,128)(2,1)S(1)}, u32[]{:S(2)}, u32[]{:S(2)}) collective-permute-start(bf16[128,512]{1,0:T(8,128)(2,1)S(1)} %multiply_convert_fusion.refs_0_), channel_id=1, source_target_pairs={{0,2},{1,3},{2,0},{3,1},{4,6},{5,7},{6,4},{7,5},{8,10},{9,11},{10,... | collective-permute-start | bytes 393224 | tf_op jit(solution)/shard_map/ppermute | solution.py:352
  6.3 8.9 %collective-permute-start.2 = (bf16[128,512]{1,0:T(8,128)(2,1)S(1)}, bf16[128,512]{1,0:T(8,128)(2,1)S(1)}, u32[]{:S(2)}, u32[]{:S(2)}) collective-permute-start(bf16[128,512]{1,0:T(8,128)(2,1)S(1)} %multiply_convert_fusion.refs_0_), channel_id=1, source_target_pairs={{0,4},{1,5},{2,6},{3,7},{4,0},{5,1},{6,2},{7,3},{8,12},{9,13},{10,... | collective-permute-start | bytes 393224 | tf_op jit(solution)/shard_map/ppermute | solution.py:352
  7.8 8.4 %collective-permute-start.3 = (bf16[128,512]{1,0:T(8,128)(2,1)S(1)}, bf16[128,512]{1,0:T(8,128)(2,1)S(1)}, u32[]{:S(2)}, u32[]{:S(2)}) collective-permute-start(bf16[128,512]{1,0:T(8,128)(2,1)S(1)} %multiply_convert_fusion.refs_0_), channel_id=1, source_target_pairs={{0,8},{1,9},{2,10},{3,11},{4,12},{5,13},{6,14},{7,15},{8,0},{9,1},... | collective-permute-start | bytes 393224 | tf_op jit(solution)/shard_map/ppermute | solution.py:352
  10.4 12.5 %collective-permute-start = (bf16[128,512]{1,0:T(8,128)(2,1)S(1)}, bf16[128,512]{1,0:T(8,128)(2,1)S(1)}, u32[]{:S(2)}, u32[]{:S(2)}) collective-permute-start(bf16[128,512]{1,0:T(8,128)(2,1)S(1)} %multiply_convert_fusion.refs_0_), channel_id=1, source_target_pairs={{0,1},{1,0},{2,3},{3,2},{4,5},{5,4},{6,7},{7,6},{8,9},{9,8},{10,11... | collective-permute-start | bytes 393224 | tf_op jit(solution)/shard_map/ppermute | solution.py:352
  11.5 25.7 %all-to-all-start = ((bf16[16,160,128]{2,1,0:T(8,128)(2,1)}), bf16[16,160,128]{2,1,0:T(8,128)(2,1)S(1)}, u32[]{:S(2)}, u32[]{:S(2)}) async-start(bf16[16,160,128]{2,1,0:T(8,128)(2,1)} %bitcast.5), calls=%async_computation | async-start | bytes 1310720 | tf_op jit(solution)/shard_map/all_to_all | solution.py:366
  16.3 6.6 %collective-permute-start.4 = (bf16[384,512]{1,0:T(8,128)(2,1)S(1)}, bf16[384,512]{1,0:T(8,128)(2,1)S(1)}, u32[]{:S(2)}, u32[]{:S(2)}) collective-permute-start(bf16[384,512]{1,0:T(8,128)(2,1)S(1)} %constant_dynamic-update-slice_fusion.refs_2_), channel_id=1, source_target_pairs={{0,1},{1,0},{2,3},{3,2},{4,5},{5,4},{6,7},{7,6},{8,9},{9,8},{10,11... | collective-permute-start | bytes 1179656 | tf_op jit(solution)/shard_map/ppermute | solution.py:352
  16.4 6.5 %copy-start = (bf16[2560,512]{1,0:T(8,128)(2,1)S(1)}, bf16[2560,512]{1,0:T(8,128)(2,1)}, u32[]{:S(2)}) copy-start(bf16[2560,512]{1,0:T(8,128)(2,1)} %refs_6_.1) | copy-start | bytes 7864324
  18.6 0.8 %copy-start.13 = (s32[128,1024]{1,0:T(8,128)}, s32[128,1024]{1,0:T(8,128)S(1)}, u32[]{:S(2)}) copy-start(s32[128,1024]{1,0:T(8,128)S(1)} %get-tuple-element.30.refs_7_) | copy-start | bytes 1572868
  18.6 6.9 %copy-start.14 = (s32[128,1024]{1,0:T(8,128)}, s32[128,1024]{1,0:T(8,128)S(1)}, u32[]{:S(2)}) copy-start(s32[128,1024]{1,0:T(8,128)S(1)} %get-tuple-element.31.refs_8_) | copy-start | bytes 1572868
  19.5 15.7 %collective-permute-start.5 = (bf16[256,512]{1,0:T(8,128)(2,1)S(1)}, bf16[256,512]{1,0:T(8,128)(2,1)S(1)}, u32[]{:S(2)}, u32[]{:S(2)}) collective-permute-start(bf16[256,512]{1,0:T(8,128)(2,1)S(1)} %pad_maximum_fusion), channel_id=1, source_target_pairs={{0,2},{1,3},{2,0},{3,1},{4,6},{5,7},{6,4},{7,5},{8,10},{9,11},{10,... | collective-permute-start | bytes 786440 | tf_op jit(solution)/shard_map/ppermute | solution.py:352
  20.2 11.8 %collective-permute-start.6 = (bf16[128,512]{1,0:T(8,128)(2,1)S(1)}, bf16[128,512]{1,0:T(8,128)(2,1)S(1)}, u32[]{:S(2)}, u32[]{:S(2)}) collective-permute-start(bf16[128,512]{1,0:T(8,128)(2,1)S(1)} %collective-permute-done.3), channel_id=1, source_target_pairs={{0,4},{1,5},{2,6},{3,7},{4,0},{5,1},{6,2},{7,3},{8,12},{9,13},{10,... | collective-permute-start | bytes 393224 | tf_op jit(solution)/shard_map/ppermute | solution.py:352
  21.7 13.4 %collective-permute-start.7 = (bf16[128,512]{1,0:T(8,128)(2,1)S(1)}, bf16[128,512]{1,0:T(8,128)(2,1)S(1)}, u32[]{:S(2)}, u32[]{:S(2)}) collective-permute-start(bf16[128,512]{1,0:T(8,128)(2,1)S(1)} %collective-permute-done.3), channel_id=1, source_target_pairs={{0,6},{1,7},{2,4},{3,5},{4,2},{5,3},{6,0},{7,1},{8,14},{9,15},{10,... | collective-permute-start | bytes 393224 | tf_op jit(solution)/shard_map/ppermute | solution.py:352
  25.5 0.8 %copy-start.11 = (f32[128,1024]{1,0:T(8,128)}, f32[128,1024]{1,0:T(8,128)S(1)}, u32[]{:S(2)}) copy-start(f32[128,1024]{1,0:T(8,128)S(1)} %get-tuple-element.32.refs_9_) | copy-start | bytes 1572868
  26.3 0.8 %copy-start.12 = (f32[128,1024]{1,0:T(8,128)}, f32[128,1024]{1,0:T(8,128)S(1)}, u32[]{:S(2)}) copy-start(f32[128,1024]{1,0:T(8,128)S(1)} %get-tuple-element.33.refs_10_) | copy-start | bytes 1572868
  32.0 7.6 %copy-start.4 = (bf16[128,512]{1,0:T(8,128)(2,1)}, bf16[128,512]{1,0:T(8,128)(2,1)S(1)}, u32[]{:S(2)}) copy-start(bf16[128,512]{1,0:T(8,128)(2,1)S(1)} %collective-permute-done.6.refs_6_.refs_2_) | copy-start | bytes 393220
  35.2 4.4 %copy-start.5 = (bf16[128,512]{1,0:T(8,128)(2,1)}, bf16[128,512]{1,0:T(8,128)(2,1)S(1)}, u32[]{:S(2)}) copy-start(bf16[128,512]{1,0:T(8,128)(2,1)S(1)} %collective-permute-done.7.refs_8_.refs_4_) | copy-start | bytes 393220
  35.2 4.4 %copy-start.2 = (bf16[256,512]{1,0:T(8,128)(2,1)}, bf16[256,512]{1,0:T(8,128)(2,1)S(1)}, u32[]{:S(2)}) copy-start(bf16[256,512]{1,0:T(8,128)(2,1)S(1)} %collective-permute-done.5.refs_4_.refs_0_) | copy-start | bytes 786436
  35.2 2.0 %collective-permute-start.8 = (bf16[256,512]{1,0:T(8,128)(2,1)S(1)}, bf16[256,512]{1,0:T(8,128)(2,1)S(1)}, u32[]{:S(2)}, u32[]{:S(2)}) collective-permute-start(bf16[256,512]{1,0:T(8,128)(2,1)S(1)} %collective-permute-done.5.refs_4_.refs_0_), channel_id=1, source_target_pairs={{0,1},{1,0},{2,3},{3,2},{4,5},{5,4},{6,7},{7,6},{8,9},{9,8},{10,11... | collective-permute-start | bytes 786440 | tf_op jit(solution)/shard_map/ppermute | solution.py:352
  35.3 1.7 %collective-permute-start.10 = (bf16[128,512]{1,0:T(8,128)(2,1)S(1)}, bf16[128,512]{1,0:T(8,128)(2,1)S(1)}, u32[]{:S(2)}, u32[]{:S(2)}) collective-permute-start(bf16[128,512]{1,0:T(8,128)(2,1)S(1)} %collective-permute-done.7.refs_8_.refs_4_), channel_id=1, source_target_pairs={{0,1},{1,0},{2,3},{3,2},{4,5},{5,4},{6,7},{7,6},{8,9},{9,8},{10,11... | collective-permute-start | bytes 393224 | tf_op jit(solution)/shard_map/ppermute | solution.py:352
  35.8 1.4 %collective-permute-start.9 = (bf16[128,512]{1,0:T(8,128)(2,1)S(1)}, bf16[128,512]{1,0:T(8,128)(2,1)S(1)}, u32[]{:S(2)}, u32[]{:S(2)}) collective-permute-start(bf16[128,512]{1,0:T(8,128)(2,1)S(1)} %collective-permute-done.6.refs_6_.refs_2_), channel_id=1, source_target_pairs={{0,1},{1,0},{2,3},{3,2},{4,5},{5,4},{6,7},{7,6},{8,9},{9,8},{10,11... | collective-permute-start | bytes 393224 | tf_op jit(solution)/shard_map/ppermute | solution.py:352
  37.0 2.7 %copy-start.6 = (bf16[128,512]{1,0:T(8,128)(2,1)}, bf16[128,512]{1,0:T(8,128)(2,1)S(1)}, u32[]{:S(2)}) copy-start(bf16[128,512]{1,0:T(8,128)(2,1)S(1)} %collective-permute-done.10.refs_9_.refs_5_) | copy-start | bytes 393220
  37.2 2.5 %copy-start.7 = (bf16[128,512]{1,0:T(8,128)(2,1)}, bf16[128,512]{1,0:T(8,128)(2,1)S(1)}, u32[]{:S(2)}) copy-start(bf16[128,512]{1,0:T(8,128)(2,1)S(1)} %collective-permute-done.9.refs_7_.refs_3_) | copy-start | bytes 393220
  37.2 2.5 %copy-start.3 = (bf16[256,512]{1,0:T(8,128)(2,1)}, bf16[256,512]{1,0:T(8,128)(2,1)S(1)}, u32[]{:S(2)}) copy-start(bf16[256,512]{1,0:T(8,128)(2,1)S(1)} %collective-permute-done.8.refs_5_.refs_1_) | copy-start | bytes 786436
  38.0 7.0 %collective-permute-start.11 = (bf16[176,512]{1,0:T(8,128)(2,1)S(1)}, bf16[176,512]{1,0:T(8,128)(2,1)S(1)}, u32[]{:S(2)}, u32[]{:S(2)}) collective-permute-start(bf16[176,512]{1,0:T(8,128)(2,1)S(1)} %block_gradient.1.ours), channel_id=1, source_target_pairs={{0,16},{1,17},{2,18},{3,19},{4,20},{5,21},{6,22},{7,23},{8,24},{9,... | collective-permute-start | bytes 540680 | tf_op jit(solution)/shard_map/ppermute | solution.py:352

commit v5 on v4

--- a/solution.py
+++ b/solution.py
@@ -59,7 +59,7 @@
 
 def finish(ours, theirs):
     rows, hidden = ours.shape
-    block = rows - 16
+    block = rows - 8
     parts = 5
     vmem = pl.BlockSpec(memory_space=pltpu.VMEM)
     return pl.pallas_call(
@@ -133,9 +133,11 @@
     )(*owners_of, keys_whole, keys_split)
 
 
-def slot_gradients(bits, refs, w_whole, w_split, words_whole, words_split, back, hits, take, ready=None):
+def slot_gradients(bits, refs, w_whole, w_split, words_whole, words_split, back, hits, take, ready=None, arrive=None):
     spot = 0
-    for ref in refs:
+    for at, ref in enumerate(refs):
+        if arrive is not None:
+            arrive(at)
         rows = ref.shape[0]
         lanes = slice(spot, spot + rows)
         back[:E, lanes] = dot_nt(w_whole[...], ref[...]).astype(BF16)
@@ -195,8 +197,11 @@
     ]
     for load in loads:
         load.start()
-    for load in loads[:heads]:
+    for load in loads[: len(blocks)]:
         load.wait()
+
+    def arrive(at):
+        loads[len(blocks) + at].wait()
 
     def ready(at):
         for load in loads[heads + 4 * at : heads + 4 * at + 4]:
@@ -217,7 +222,7 @@
             stores[at].start()
 
     w_parts = (weights.at[pl.ds(0, E), :], weights.at[pl.ds(E, E), :])
-    slot_gradients(bits, deltas, *w_parts, words, words2, back, hits, take, ready)
+    slot_gradients(bits, deltas, *w_parts, words, words2, back, hits, take, ready, arrive)
     for store in stores:
         store.wait()
 
@@ -303,7 +308,7 @@
     low = (sums[0] - high.astype(F32)).astype(BF16)
     block = acc.shape[0]
     out[:block, :] = acc[...].astype(BF16)
-    place = lax.broadcasted_iota(jnp.int32, (16, acc.shape[1]), 0)
+    place = lax.broadcasted_iota(jnp.int32, (8, acc.shape[1]), 0)
     extra = jnp.where(place == 0, high.astype(F32), jnp.where(place == 1, low.astype(F32), 0.0))
     out[block:, :] = extra.astype(BF16)
 
@@ -314,7 +319,7 @@
     vmem = pl.BlockSpec(memory_space=pltpu.VMEM)
     return pl.pallas_call(
         functools.partial(block_kernel, places, len(arrays)),
-        out_shape=jax.ShapeDtypeStruct((block + 16, hidden), BF16),
+        out_shape=jax.ShapeDtypeStruct((block + 8, hidden), BF16),
         in_specs=[vmem] * (len(arrays) + 1),
         out_specs=vmem,
         scratch_shapes=[pltpu.VMEM((block, hidden), F32)],

time: 46.1 us -> 46.7 us (1.013)
  Pallas kernels: 11.8 us -> 12.3 us
    pallas_call x1, Pallas kernels: 5.39 us -> 5.97 us  [late_call(): pl.pallas_call(functools.partial(late_kernel, bits, tables, len(arrays)),...]
  transfers between devices with their start and end apart: 13 -> 13, of which waited for: 5 -> 5; matrix products, arithmetic and copies ran while one was open for 2% -> 2% of each run, Pallas kernels for 22% -> 23%
where the time goes in v5:
time: 46.7 us; the launch traced here: 46.4 us
  starting transfers between devices  16.6 us (36%)
  Pallas kernels  12.3 us (26%)
  waiting for transfers between devices  10.5 us (22%)
  local copies, waits for them, and re-layouts  3.54 us (8%)
  matrix products  2.54 us (5%)
  between operations  0.89 us (2%)
    ppermute x12, starting transfers between devices, send(): return lax.ppermute(values, ('grp', 'mem'), pairs)  13 us
    ppermute x12, waiting for transfers between devices, send(): return lax.ppermute(values, ('grp', 'mem'), pairs)  10.5 us
    pallas_call x1, Pallas kernels, late_call(): pl.pallas_call(functools.partial(late_kernel, bits, tables, len(arrays)),...  5.97 us
    all_to_all x1, starting transfers between devices, per_device(): lax.all_to_all(pooled_rows, 'mem', split_axis=0, concat_axis=0, tiled=True)  3.59 us
    dot_general x1, matrix products, per_device(): pre_act = jnp.dot(pooled, w_first, preferred_element_type=F32) + bias_first  2.54 us
    pallas_call x1, Pallas kernels, slot_call(): pl.pallas_call(functools.partial(kernel, bits, len(arrays)), out_shape=ou...  2.54 us
    unnamed x34, local copies, waits for them, and re-layouts  2.46 us
    pallas_call x1, Pallas kernels, hit_words(): pl.pallas_call(functools.partial(word_kernel, bits, turns), out_shape=sha...  2.19 us
  transfers between devices with their start and end apart: 13, of which 5 were waited for; matrix products, arithmetic and copies ran while one was open for 2% of the time, Pallas kernels for 23%

profile of v5, /device:TPU:0, one launch (start us, length us, event | category | flops | bytes accessed | tf_op | source)
XLA Modules:
  0.0 46.4 jit_solution(16006445540687383570)
XLA Ops:
  0.6 0.0 copy-start.15
  0.6 2.5 %multiply_convert_fusion.refs_0_ = bf16[128,512]{1,0:T(8,128)(2,1)S(1)} fusion(bf16[128,2560]{1,0:T(8,128)(2,1)} %param.12, bf16[2560,512]{1,0:T(8,128)(2,1)} %refs_6_.1, bf16[128,512]{1,0:T(8,128)(2,1)} %param.13, f32[512]{0:T(512)} %param.15), kind=kOutput, calls=%fused_computation.2 | convolution fusion | flops 336265216 | bytes 3540992 | tf_op jit(solution)/shard_map/dot_general | solution.py:359
  3.2 0.0 copy-start.1
  3.2 0.0 copy-start.8
  3.2 0.0 copy-start.9
  3.2 0.0 copy-start.10
  3.2 3.0 %collective-permute-start.1 = (bf16[128,512]{1,0:T(8,128)(2,1)S(1)}, bf16[128,512]{1,0:T(8,128)(2,1)S(1)}, u32[]{:S(2)}, u32[]{:S(2)}) collective-permute-start(bf16[128,512]{1,0:T(8,128)(2,1)S(1)} %multiply_convert_fusion.refs_0_), channel_id=1, source_target_pairs={{0,2},{1,3},{2,0},{3,1},{4,6},{5,7},{6,4},{7,5},{8,10},{9,11},{10,... | collective-permute-start | bytes 393224 | tf_op jit(solution)/shard_map/ppermute | solution.py:357
  6.3 1.6 %collective-permute-start.2 = (bf16[128,512]{1,0:T(8,128)(2,1)S(1)}, bf16[128,512]{1,0:T(8,128)(2,1)S(1)}, u32[]{:S(2)}, u32[]{:S(2)}) collective-permute-start(bf16[128,512]{1,0:T(8,128)(2,1)S(1)} %multiply_convert_fusion.refs_0_), channel_id=1, source_target_pairs={{0,4},{1,5},{2,6},{3,7},{4,0},{5,1},{6,2},{7,3},{8,12},{9,13},{10,... | collective-permute-start | bytes 393224 | tf_op jit(solution)/shard_map/ppermute | solution.py:357
  7.8 2.6 %collective-permute-start.3 = (bf16[128,512]{1,0:T(8,128)(2,1)S(1)}, bf16[128,512]{1,0:T(8,128)(2,1)S(1)}, u32[]{:S(2)}, u32[]{:S(2)}) collective-permute-start(bf16[128,512]{1,0:T(8,128)(2,1)S(1)} %multiply_convert_fusion.refs_0_), channel_id=1, source_target_pairs={{0,8},{1,9},{2,10},{3,11},{4,12},{5,13},{6,14},{7,15},{8,0},{9,1},... | collective-permute-start | bytes 393224 | tf_op jit(solution)/shard_map/ppermute | solution.py:357
  10.4 0.0 collective-permute-start
  10.4 0.0 copy-done.15
  10.4 1.1 %copy.16 = bf16[2560,128]{1,0:T(8,128)(2,1)} copy(bf16[2560,128]{0,1:T(8,128)(2,1)S(1)} %bitcast.19) | data formatting | bytes 1310720 | tf_op jit(solution)/shard_map/transpose | solution.py:370
  11.5 3.6 %all-to-all-start = ((bf16[16,160,128]{2,1,0:T(8,128)(2,1)}), bf16[16,160,128]{2,1,0:T(8,128)(2,1)S(1)}, u32[]{:S(2)}, u32[]{:S(2)}) async-start(bf16[16,160,128]{2,1,0:T(8,128)(2,1)} %bitcast.5), calls=%async_computation | async-start | bytes 1310720 | tf_op jit(solution)/shard_map/all_to_all | solution.py:371
  15.1 0.0 collective-permute-done.1
  15.1 0.0 collective-permute-done.2
  15.2 1.1 %collective-permute-done.3 = bf16[128,512]{1,0:T(8,128)(2,1)S(1)} collective-permute-done((bf16[128,512]{1,0:T(8,128)(2,1)S(1)}, bf16[128,512]{1,0:T(8,128)(2,1)S(1)}, u32[]{:S(2)}, u32[]{:S(2)}) %collective-permute-start.3) | collective-permute-done | bytes 131104 | tf_op jit(solution)/shard_map/ppermute | solution.py:357
  16.3 0.1 collective-permute-start.4
  16.4 0.0 copy-done.1
  16.4 0.0 copy-done.8
  16.4 0.0 copy-done.9
  16.4 0.0 copy-done.10
  16.4 0.0 copy-start
  16.4 2.2 %hit_words.1 = (s32[128,1024]{1,0:T(8,128)S(1)}, s32[128,1024]{1,0:T(8,128)S(1)}, s32[128,1024]{1,0:T(8,128)S(1)}, s32[128,1024]{1,0:T(8,128)S(1)}) custom-call(s32[1,16]{1,0:T(1,128)S(1)} %copy-done.9, s32[1,16]{1,0:T(1,128)S(1)} %copy-done.10, s32[8,2048]{1,0:T(8,128)S(1)} %bitcast.18, s32[4,8,2048]{2,1,0:T(8,128)S(1)} %bitcast.17), custom_call_target="tpu_custom_call" | custom-call | flops 4000000000 | bytes 2000000 | tf_op jit(solution)/shard_map/hit_words/pallas_call | solution.py:116
  18.6 0.0 copy-start.13
  18.6 0.0 copy-start.14
  18.7 0.8 %copy-done.13 = s32[128,1024]{1,0:T(8,128)} copy-done((s32[128,1024]{1,0:T(8,128)}, s32[128,1024]{1,0:T(8,128)S(1)}, u32[]{:S(2)}) %copy-start.13) | copy-done | bytes 524312
  19.5 0.8 %collective-permute-start.5 = (bf16[256,512]{1,0:T(8,128)(2,1)S(1)}, bf16[256,512]{1,0:T(8,128)(2,1)S(1)}, u32[]{:S(2)}, u32[]{:S(2)}) collective-permute-start(bf16[256,512]{1,0:T(8,128)(2,1)S(1)} %pad_maximum_fusion), channel_id=1, source_target_pairs={{0,2},{1,3},{2,0},{3,1},{4,6},{5,7},{6,4},{7,5},{8,10},{9,11},{10,... | collective-permute-start | bytes 786440 | tf_op jit(solution)/shard_map/ppermute | solution.py:357
  20.2 1.5 %collective-permute-start.6 = (bf16[128,512]{1,0:T(8,128)(2,1)S(1)}, bf16[128,512]{1,0:T(8,128)(2,1)S(1)}, u32[]{:S(2)}, u32[]{:S(2)}) collective-permute-start(bf16[128,512]{1,0:T(8,128)(2,1)S(1)} %collective-permute-done.3), channel_id=1, source_target_pairs={{0,4},{1,5},{2,6},{3,7},{4,0},{5,1},{6,2},{7,3},{8,12},{9,13},{10,... | collective-permute-start | bytes 393224 | tf_op jit(solution)/shard_map/ppermute | solution.py:357
  21.7 1.2 %collective-permute-start.7 = (bf16[128,512]{1,0:T(8,128)(2,1)S(1)}, bf16[128,512]{1,0:T(8,128)(2,1)S(1)}, u32[]{:S(2)}, u32[]{:S(2)}) collective-permute-start(bf16[128,512]{1,0:T(8,128)(2,1)S(1)} %collective-permute-done.3), channel_id=1, source_target_pairs={{0,6},{1,7},{2,4},{3,5},{4,2},{5,3},{6,0},{7,1},{8,14},{9,15},{10,... | collective-permute-start | bytes 393224 | tf_op jit(solution)/shard_map/ppermute | solution.py:357
  22.9 0.0 collective-permute-done.refs_1_
  22.9 0.0 collective-permute-done.4.refs_3_
  22.9 0.0 copy-done
  23.0 2.5 %shard_map.147 = (f32[128,1024]{1,0:T(8,128)S(1)}, f32[128,1024]{1,0:T(8,128)S(1)}) custom-call(s32[1,16]{1,0:T(1,128)S(1)} %copy-done.9, s32[1,16]{1,0:T(1,128)S(1)} %copy-done.10, bf16[128,512]{1,0:T(8,128)(2,1)S(1)} %multiply_convert_fusion.refs_0_, bf16[128,512]{1,0:T(8,128)(2,1)S(1)} %collective-permute-done.refs_1_, ...), custom_call_target="tpu_custom_call" | custom-call | flops 4000000000 | bytes 4000000 | tf_op jit(solution)/shard_map/pallas_call | solution.py:276
  25.5 0.0 copy-done.14
  25.5 0.0 copy-start.11
  25.5 0.8 %copy-done.11 = f32[128,1024]{1,0:T(8,128)} copy-done((f32[128,1024]{1,0:T(8,128)}, f32[128,1024]{1,0:T(8,128)S(1)}, u32[]{:S(2)}) %copy-start.11) | copy-done | bytes 524312
  26.3 0.0 copy-start.12
  26.3 0.8 %copy-done.12 = f32[128,1024]{1,0:T(8,128)} copy-done((f32[128,1024]{1,0:T(8,128)}, f32[128,1024]{1,0:T(8,128)S(1)}, u32[]{:S(2)}) %copy-start.12) | copy-done | bytes 524312
  27.1 4.9 %collective-permute-done.6.refs_6_.refs_2_ = bf16[128,512]{1,0:T(8,128)(2,1)S(1)} collective-permute-done((bf16[128,512]{1,0:T(8,128)(2,1)S(1)}, bf16[128,512]{1,0:T(8,128)(2,1)S(1)}, u32[]{:S(2)}, u32[]{:S(2)}) %collective-permute-start.6) | collective-permute-done | bytes 131104 | tf_op jit(solution)/shard_map/ppermute | solution.py:357
  32.0 0.0 copy-start.4
  32.0 3.2 %collective-permute-done.7.refs_8_.refs_4_ = bf16[128,512]{1,0:T(8,128)(2,1)S(1)} collective-permute-done((bf16[128,512]{1,0:T(8,128)(2,1)S(1)}, bf16[128,512]{1,0:T(8,128)(2,1)S(1)}, u32[]{:S(2)}, u32[]{:S(2)}) %collective-permute-start.7) | collective-permute-done | bytes 131104 | tf_op jit(solution)/shard_map/ppermute | solution.py:357
  35.2 0.0 copy-start.5
  35.2 0.0 collective-permute-done.5.refs_4_.refs_0_
  35.2 0.0 copy-start.2
  35.2 0.1 collective-permute-start.8
  35.3 0.5 %collective-permute-start.10 = (bf16[128,512]{1,0:T(8,128)(2,1)S(1)}, bf16[128,512]{1,0:T(8,128)(2,1)S(1)}, u32[]{:S(2)}, u32[]{:S(2)}) collective-permute-start(bf16[128,512]{1,0:T(8,128)(2,1)S(1)} %collective-permute-done.7.refs_8_.refs_4_), channel_id=1, source_target_pairs={{0,1},{1,0},{2,3},{3,2},{4,5},{5,4},{6,7},{7,6},{8,9},{9,8},{10,11... | collective-permute-start | bytes 393224 | tf_op jit(solution)/shard_map/ppermute | solution.py:357
  35.8 0.1 collective-permute-start.9
  35.8 1.1 %collective-permute-done.10.refs_9_.refs_5_ = bf16[128,512]{1,0:T(8,128)(2,1)S(1)} collective-permute-done((bf16[128,512]{1,0:T(8,128)(2,1)S(1)}, bf16[128,512]{1,0:T(8,128)(2,1)S(1)}, u32[]{:S(2)}, u32[]{:S(2)}) %collective-permute-start.10) | collective-permute-done | bytes 131104 | tf_op jit(solution)/shard_map/ppermute | solution.py:357
  37.0 0.0 copy-start.6
  37.0 0.2 collective-permute-done.9.refs_7_.refs_3_
  37.2 0.0 copy-start.7
  37.2 0.0 collective-permute-done.8.refs_5_.refs_1_
  37.2 0.0 all-to-all-done.refs_10_
  37.2 0.9 %block_gradient.1.ours = bf16[168,512]{1,0:T(8,128)(2,1)S(1)} custom-call(bf16[128,512]{1,0:T(8,128)(2,1)S(1)} %multiply_convert_fusion.refs_0_, bf16[128,512]{1,0:T(8,128)(2,1)S(1)} %collective-permute-done.refs_1_, bf16[384,512]{1,0:T(8,128)(2,1)S(1)} %constant_dynamic-update-slice_fusion.refs_2_, bf16[384,512]{1,0:T(8,128)(2,1)S(1)} %collective-permute-done.4.refs_3_, ...), custom_call_target="tpu_custom_call" | custom-call | flops 1000000000 | bytes 3000000 | tf_op jit(solution)/shard_map/block_gradient/pallas_call | solution.py:320
  38.0 1.6 %collective-permute-start.11 = (bf16[168,512]{1,0:T(8,128)(2,1)S(1)}, bf16[168,512]{1,0:T(8,128)(2,1)S(1)}, u32[]{:S(2)}, u32[]{:S(2)}) collective-permute-start(bf16[168,512]{1,0:T(8,128)(2,1)S(1)} %block_gradient.1.ours), channel_id=1, source_target_pairs={{0,16},{1,17},{2,18},{3,19},{4,20},{5,21},{6,22},{7,23},{8,24},{9,... | collective-permute-start | bytes 516104 | tf_op jit(solution)/shard_map/ppermute | solution.py:357
  39.6 0.0 copy-done.4
  39.6 0.0 copy-done.5
  39.6 0.0 copy-done.2
  39.6 0.0 copy-done.6
  39.6 0.0 copy-done.7
  39.6 0.0 copy-done.3
  39.7 6.0 %late_gradients.1 = (f32[128,1024]{1,0:T(8,128)}, f32[32,1024]{1,0:T(8,128)}) custom-call(s32[1,16]{1,0:T(1,128)} %owner_ref.5, s32[1,16]{1,0:T(1,128)} %shard_ref.5, bf16[256,512]{1,0:T(8,128)(2,1)} %copy-done.2, bf16[256,512]{1,0:T(8,128)(2,1)} %copy-done.3, bf16[128,512]{1,0:T(8,128)(2,1)} %copy-done.4, bf16[128,512]{1,0:T(8,128)(2,1)} %copy-done.7, ...), custom_call_target="tpu_custom_call" | custom-call | flops 4000000000 | bytes 4000000 | tf_op jit(solution)/shard_map/late_gradients/pallas_call | solution.py:246
  45.6 0.0 collective-permute-done.11.theirs
  45.7 0.8 %finish.1 = (f32[160,512]{1,0:T(8,128)}, f32[1,512]{1,0:T(1,128)}) custom-call(bf16[168,512]{1,0:T(8,128)(2,1)S(1)} %block_gradient.1.ours, bf16[168,512]{1,0:T(8,128)(2,1)S(1)} %collective-permute-done.11.theirs), custom_call_target="tpu_custom_call" | custom-call | tf_op jit(solution)/shard_map/finish/pallas_call | solution.py:65
  (5 shorter events, 0.1 us)
Async XLA Ops:
  0.6 9.8 %copy-start.15 = (bf16[128,2560]{1,0:T(8,128)(2,1)S(1)}, bf16[128,2560]{1,0:T(8,128)(2,1)}, u32[]{:S(2)}) copy-start(bf16[128,2560]{1,0:T(8,128)(2,1)} %param.12) | copy-start | bytes 1966084
  3.2 13.2 %copy-start.1 = (s32[1,4,2048,8]{2,3,1,0:T(8,128)S(1)}, s32[1,4,2048,8]{2,3,1,0:T(8,128)}, u32[]{:S(2)}) copy-start(s32[1,4,2048,8]{2,3,1,0:T(8,128)} %param.19) | copy-start | bytes 786436
  3.2 13.2 %copy-start.8 = (s32[1,1,2048,8]{2,3,1,0:T(8,128)S(1)}, s32[1,1,2048,8]{2,3,1,0:T(8,128)}, u32[]{:S(2)}) copy-start(s32[1,1,2048,8]{2,3,1,0:T(8,128)} %param.18) | copy-start | bytes 196612
  3.2 13.2 %copy-start.9 = (s32[1,16]{1,0:T(1,128)S(1)}, s32[1,16]{1,0:T(1,128)}, u32[]{:S(2)}) copy-start(s32[1,16]{1,0:T(1,128)} %owner_ref.5) | copy-start | bytes 196
  3.2 13.2 %copy-start.10 = (s32[1,16]{1,0:T(1,128)S(1)}, s32[1,16]{1,0:T(1,128)}, u32[]{:S(2)}) copy-start(s32[1,16]{1,0:T(1,128)} %shard_ref.5) | copy-start | bytes 196
  3.2 11.9 %collective-permute-start.1 = (bf16[128,512]{1,0:T(8,128)(2,1)S(1)}, bf16[128,512]{1,0:T(8,128)(2,1)S(1)}, u32[]{:S(2)}, u32[]{:S(2)}) collective-permute-start(bf16[128,512]{1,0:T(8,128)(2,1)S(1)} %multiply_convert_fusion.refs_0_), channel_id=1, source_target_pairs={{0,2},{1,3},{2,0},{3,1},{4,6},{5,7},{6,4},{7,5},{8,10},{9,11},{10,... | collective-permute-start | bytes 393224 | tf_op jit(solution)/shard_map/ppermute | solution.py:357
  6.3 8.9 %collective-permute-start.2 = (bf16[128,512]{1,0:T(8,128)(2,1)S(1)}, bf16[128,512]{1,0:T(8,128)(2,1)S(1)}, u32[]{:S(2)}, u32[]{:S(2)}) collective-permute-start(bf16[128,512]{1,0:T(8,128)(2,1)S(1)} %multiply_convert_fusion.refs_0_), channel_id=1, source_target_pairs={{0,4},{1,5},{2,6},{3,7},{4,0},{5,1},{6,2},{7,3},{8,12},{9,13},{10,... | collective-permute-start | bytes 393224 | tf_op jit(solution)/shard_map/ppermute | solution.py:357
  7.8 8.4 %collective-permute-start.3 = (bf16[128,512]{1,0:T(8,128)(2,1)S(1)}, bf16[128,512]{1,0:T(8,128)(2,1)S(1)}, u32[]{:S(2)}, u32[]{:S(2)}) collective-permute-start(bf16[128,512]{1,0:T(8,128)(2,1)S(1)} %multiply_convert_fusion.refs_0_), channel_id=1, source_target_pairs={{0,8},{1,9},{2,10},{3,11},{4,12},{5,13},{6,14},{7,15},{8,0},{9,1},... | collective-permute-start | bytes 393224 | tf_op jit(solution)/shard_map/ppermute | solution.py:357
  10.4 12.5 %collective-permute-start = (bf16[128,512]{1,0:T(8,128)(2,1)S(1)}, bf16[128,512]{1,0:T(8,128)(2,1)S(1)}, u32[]{:S(2)}, u32[]{:S(2)}) collective-permute-start(bf16[128,512]{1,0:T(8,128)(2,1)S(1)} %multiply_convert_fusion.refs_0_), channel_id=1, source_target_pairs={{0,1},{1,0},{2,3},{3,2},{4,5},{5,4},{6,7},{7,6},{8,9},{9,8},{10,11... | collective-permute-start | bytes 393224 | tf_op jit(solution)/shard_map/ppermute | solution.py:357
  11.5 25.7 %all-to-all-start = ((bf16[16,160,128]{2,1,0:T(8,128)(2,1)}), bf16[16,160,128]{2,1,0:T(8,128)(2,1)S(1)}, u32[]{:S(2)}, u32[]{:S(2)}) async-start(bf16[16,160,128]{2,1,0:T(8,128)(2,1)} %bitcast.5), calls=%async_computation | async-start | bytes 1310720 | tf_op jit(solution)/shard_map/all_to_all | solution.py:371
  16.3 6.6 %collective-permute-start.4 = (bf16[384,512]{1,0:T(8,128)(2,1)S(1)}, bf16[384,512]{1,0:T(8,128)(2,1)S(1)}, u32[]{:S(2)}, u32[]{:S(2)}) collective-permute-start(bf16[384,512]{1,0:T(8,128)(2,1)S(1)} %constant_dynamic-update-slice_fusion.refs_2_), channel_id=1, source_target_pairs={{0,1},{1,0},{2,3},{3,2},{4,5},{5,4},{6,7},{7,6},{8,9},{9,8},{10,11... | collective-permute-start | bytes 1179656 | tf_op jit(solution)/shard_map/ppermute | solution.py:357
  16.4 6.5 %copy-start = (bf16[2560,512]{1,0:T(8,128)(2,1)S(1)}, bf16[2560,512]{1,0:T(8,128)(2,1)}, u32[]{:S(2)}) copy-start(bf16[2560,512]{1,0:T(8,128)(2,1)} %refs_6_.1) | copy-start | bytes 7864324
  18.6 0.8 %copy-start.13 = (s32[128,1024]{1,0:T(8,128)}, s32[128,1024]{1,0:T(8,128)S(1)}, u32[]{:S(2)}) copy-start(s32[128,1024]{1,0:T(8,128)S(1)} %get-tuple-element.30.refs_7_) | copy-start | bytes 1572868
  18.6 6.9 %copy-start.14 = (s32[128,1024]{1,0:T(8,128)}, s32[128,1024]{1,0:T(8,128)S(1)}, u32[]{:S(2)}) copy-start(s32[128,1024]{1,0:T(8,128)S(1)} %get-tuple-element.31.refs_8_) | copy-start | bytes 1572868
  19.5 15.7 %collective-permute-start.5 = (bf16[256,512]{1,0:T(8,128)(2,1)S(1)}, bf16[256,512]{1,0:T(8,128)(2,1)S(1)}, u32[]{:S(2)}, u32[]{:S(2)}) collective-permute-start(bf16[256,512]{1,0:T(8,128)(2,1)S(1)} %pad_maximum_fusion), channel_id=1, source_target_pairs={{0,2},{1,3},{2,0},{3,1},{4,6},{5,7},{6,4},{7,5},{8,10},{9,11},{10,... | collective-permute-start | bytes 786440 | tf_op jit(solution)/shard_map/ppermute | solution.py:357
  20.2 11.8 %collective-permute-start.6 = (bf16[128,512]{1,0:T(8,128)(2,1)S(1)}, bf16[128,512]{1,0:T(8,128)(2,1)S(1)}, u32[]{:S(2)}, u32[]{:S(2)}) collective-permute-start(bf16[128,512]{1,0:T(8,128)(2,1)S(1)} %collective-permute-done.3), channel_id=1, source_target_pairs={{0,4},{1,5},{2,6},{3,7},{4,0},{5,1},{6,2},{7,3},{8,12},{9,13},{10,... | collective-permute-start | bytes 393224 | tf_op jit(solution)/shard_map/ppermute | solution.py:357
  21.7 13.4 %collective-permute-start.7 = (bf16[128,512]{1,0:T(8,128)(2,1)S(1)}, bf16[128,512]{1,0:T(8,128)(2,1)S(1)}, u32[]{:S(2)}, u32[]{:S(2)}) collective-permute-start(bf16[128,512]{1,0:T(8,128)(2,1)S(1)} %collective-permute-done.3), channel_id=1, source_target_pairs={{0,6},{1,7},{2,4},{3,5},{4,2},{5,3},{6,0},{7,1},{8,14},{9,15},{10,... | collective-permute-start | bytes 393224 | tf_op jit(solution)/shard_map/ppermute | solution.py:357
  25.5 0.8 %copy-start.11 = (f32[128,1024]{1,0:T(8,128)}, f32[128,1024]{1,0:T(8,128)S(1)}, u32[]{:S(2)}) copy-start(f32[128,1024]{1,0:T(8,128)S(1)} %get-tuple-element.32.refs_9_) | copy-start | bytes 1572868
  26.3 0.8 %copy-start.12 = (f32[128,1024]{1,0:T(8,128)}, f32[128,1024]{1,0:T(8,128)S(1)}, u32[]{:S(2)}) copy-start(f32[128,1024]{1,0:T(8,128)S(1)} %get-tuple-element.33.refs_10_) | copy-start | bytes 1572868
  32.0 7.6 %copy-start.4 = (bf16[128,512]{1,0:T(8,128)(2,1)}, bf16[128,512]{1,0:T(8,128)(2,1)S(1)}, u32[]{:S(2)}) copy-start(bf16[128,512]{1,0:T(8,128)(2,1)S(1)} %collective-permute-done.6.refs_6_.refs_2_) | copy-start | bytes 393220
  35.2 4.4 %copy-start.5 = (bf16[128,512]{1,0:T(8,128)(2,1)}, bf16[128,512]{1,0:T(8,128)(2,1)S(1)}, u32[]{:S(2)}) copy-start(bf16[128,512]{1,0:T(8,128)(2,1)S(1)} %collective-permute-done.7.refs_8_.refs_4_) | copy-start | bytes 393220
  35.2 4.4 %copy-start.2 = (bf16[256,512]{1,0:T(8,128)(2,1)}, bf16[256,512]{1,0:T(8,128)(2,1)S(1)}, u32[]{:S(2)}) copy-start(bf16[256,512]{1,0:T(8,128)(2,1)S(1)} %collective-permute-done.5.refs_4_.refs_0_) | copy-start | bytes 786436
  35.2 2.0 %collective-permute-start.8 = (bf16[256,512]{1,0:T(8,128)(2,1)S(1)}, bf16[256,512]{1,0:T(8,128)(2,1)S(1)}, u32[]{:S(2)}, u32[]{:S(2)}) collective-permute-start(bf16[256,512]{1,0:T(8,128)(2,1)S(1)} %collective-permute-done.5.refs_4_.refs_0_), channel_id=1, source_target_pairs={{0,1},{1,0},{2,3},{3,2},{4,5},{5,4},{6,7},{7,6},{8,9},{9,8},{10,11... | collective-permute-start | bytes 786440 | tf_op jit(solution)/shard_map/ppermute | solution.py:357
  35.3 1.7 %collective-permute-start.10 = (bf16[128,512]{1,0:T(8,128)(2,1)S(1)}, bf16[128,512]{1,0:T(8,128)(2,1)S(1)}, u32[]{:S(2)}, u32[]{:S(2)}) collective-permute-start(bf16[128,512]{1,0:T(8,128)(2,1)S(1)} %collective-permute-done.7.refs_8_.refs_4_), channel_id=1, source_target_pairs={{0,1},{1,0},{2,3},{3,2},{4,5},{5,4},{6,7},{7,6},{8,9},{9,8},{10,11... | collective-permute-start | bytes 393224 | tf_op jit(solution)/shard_map/ppermute | solution.py:357
  35.8 1.4 %collective-permute-start.9 = (bf16[128,512]{1,0:T(8,128)(2,1)S(1)}, bf16[128,512]{1,0:T(8,128)(2,1)S(1)}, u32[]{:S(2)}, u32[]{:S(2)}) collective-permute-start(bf16[128,512]{1,0:T(8,128)(2,1)S(1)} %collective-permute-done.6.refs_6_.refs_2_), channel_id=1, source_target_pairs={{0,1},{1,0},{2,3},{3,2},{4,5},{5,4},{6,7},{7,6},{8,9},{9,8},{10,11... | collective-permute-start | bytes 393224 | tf_op jit(solution)/shard_map/ppermute | solution.py:357
  37.0 2.7 %copy-start.6 = (bf16[128,512]{1,0:T(8,128)(2,1)}, bf16[128,512]{1,0:T(8,128)(2,1)S(1)}, u32[]{:S(2)}) copy-start(bf16[128,512]{1,0:T(8,128)(2,1)S(1)} %collective-permute-done.10.refs_9_.refs_5_) | copy-start | bytes 393220
  37.2 2.5 %copy-start.7 = (bf16[128,512]{1,0:T(8,128)(2,1)}, bf16[128,512]{1,0:T(8,128)(2,1)S(1)}, u32[]{:S(2)}) copy-start(bf16[128,512]{1,0:T(8,128)(2,1)S(1)} %collective-permute-done.9.refs_7_.refs_3_) | copy-start | bytes 393220
  37.2 2.5 %copy-start.3 = (bf16[256,512]{1,0:T(8,128)(2,1)}, bf16[256,512]{1,0:T(8,128)(2,1)S(1)}, u32[]{:S(2)}) copy-start(bf16[256,512]{1,0:T(8,128)(2,1)S(1)} %collective-permute-done.8.refs_5_.refs_1_) | copy-start | bytes 786436
  38.0 7.6 %collective-permute-start.11 = (bf16[168,512]{1,0:T(8,128)(2,1)S(1)}, bf16[168,512]{1,0:T(8,128)(2,1)S(1)}, u32[]{:S(2)}, u32[]{:S(2)}) collective-permute-start(bf16[168,512]{1,0:T(8,128)(2,1)S(1)} %block_gradient.1.ours), channel_id=1, source_target_pairs={{0,16},{1,17},{2,18},{3,19},{4,20},{5,21},{6,22},{7,23},{8,24},{9,... | collective-permute-start | bytes 516104 | tf_op jit(solution)/shard_map/ppermute | solution.py:357
